TPU v7x, 256 devices: a whole 4x4x8 slice. The times are simulated.
256 devices in a mesh: seq: 64 (over x, z, core), head: 4 (over y).
Axes of the slice: x: 4, y: 4, z: 8, core: 2. Of those that a mesh axis runs over, the one named last changes fastest.
Arguments:
- stream: bfloat16 [32768, 5120], P('seq', 'head'), may hold values from -6 to 6
- gate_input: bfloat16 [32768, 5120], P('seq', 'head'), may hold values from -6 to 6
- in_coeff: bfloat16 [32768, 128], P('seq'), may hold values from -0.5 to 0.5
- out_coeff: bfloat16 [32768, 128], P('seq'), may hold values from -0.5 to 0.5
- step_raw: float32 [80, 32768], P('head', 'seq'), may hold values from -4 to 4
- step_bias: float32 [80], P('head'), may hold values from -1 to 1
- decay_rate: float32 [80], P('head'), may hold values from 3.0517578e-05 to 0.05
- skip_scale: float32 [80], P('head'), may hold values from 0.5 to 5
- norm_gain: float32 [5120], P('head'), may hold values from 0.1 to 1.9
- out_proj: bfloat16 [5120, 2560], P('head'), may hold values from -0.078125 to 0.078125
- doc_starts: int32 [128], replicated, may hold values from 0 to 32767, as said below
Outputs:
- layer_out: bfloat16 [32768, 2560], P(('seq', 'head'))
Inputs may be any that keep to these rules, and one draw needn't show every extreme that they name: `doc_starts`: the first entry is 0, the last is 32767, and the entries strictly increase; entry i is the position where document i begins.
All inputs are finite; a program needn't handle non-finite values.
Results may differ from a plain program's by a relative error of at most 0.01.
Values may be sent and summed in bfloat16 or wider, within the bound.
No kernel may reach another device: no remote copies, remote signals or barrier semaphores. Data moves between devices by JAX's collectives and lax.ppermute only.
A program may use at most 128 MiB of HBM per device.

v0:
```python
import jax
import jax.numpy as jnp
from jax import lax
from jax.sharding import Mesh
from jax.sharding import PartitionSpec as P

DI = 5120
BLOCK = 256
SEQ = ("seq_0", "seq_1", "seq_2")
SEQ_HEAD = ("seq_0", "seq_1", "seq_2", "head")


EPSILON = 1e-05


def neutral_like(value, identity):
    return jax.tree.map(
        lambda a, e: jnp.broadcast_to(jnp.asarray(e, a.dtype), a.shape), value, identity
    )


def prefix_by_axis(value, axes, combine, identity):
    before = start = neutral_like(value, identity)
    total = value
    for axis in reversed(axes):
        devices, place = (lax.axis_size(axis), lax.axis_index(axis))
        pieces = jax.tree.map(lambda part: lax.all_gather(part, axis), total)
        inside, total = (start, start)
        for k in range(devices):
            passed = k < place
            total = combine(total, jax.tree.map(lambda part: part[k], pieces))
            inside = jax.tree.map(lambda new, old: jnp.where(passed, new, old), total, inside)
        before = combine(inside, before)
    return before


def from_everyone(value, axis):
    devices = lax.axis_size(axis)
    return lax.all_to_all(
        jnp.broadcast_to(value[None], (devices, *value.shape)), axis, 0, 0, tiled=True
    )


def taken_together(value, axis):
    return from_everyone(value, axis).sum(axis=0)


def split_up(value, dim, devices):
    shape = value.shape
    pieces = value.reshape(*shape[:dim], devices, shape[dim] // devices, *shape[dim + 1 :])
    return jnp.moveaxis(pieces, dim, 0)


def sent_and_summed(value, axis, dim):
    devices = lax.axis_size(axis)
    pieces = lax.all_to_all(split_up(value, dim, devices), axis, 0, 0, tiled=True)
    return jnp.sum(pieces.astype(jnp.float32), axis=0)


def block_pass(carry_state, block_piece, want_output):
    stream_blk, in_blk, out_blk, step_blk, log_blk, doc_blk, before = block_piece
    head_count = step_blk.shape[0]
    span = step_blk.shape[1]
    head_size = stream_blk.shape[1] // head_count
    index_row = lax.iota(jnp.int32, span)
    upper_ones = (index_row[:, None] <= index_row[None, :]).astype(jnp.float32)
    cumulative = jnp.dot(log_blk, upper_ones)
    last_cum = cumulative[:, -1]
    same_end = (doc_blk == doc_blk[-1]).astype(jnp.float32)
    end_weight = (
        jnp.exp(jnp.minimum(last_cum[:, None] - cumulative, 0.0)) * step_blk * same_end[None, :]
    )
    scaled_in = (end_weight[:, :, None] * in_blk.astype(jnp.float32)[None, :, :]).astype(
        jnp.bfloat16
    )
    values = stream_blk.reshape(span, head_count, head_size)
    fresh_state = jnp.einsum("hsn,shp->hnp", scaled_in, values, preferred_element_type=jnp.float32)
    joined = doc_blk == before
    carry_gate = jnp.where(joined[-1], jnp.exp(last_cum), 0.0)
    new_state = carry_gate[:, None, None] * carry_state + fresh_state
    if not want_output:
        return (new_state, None)
    scores = jnp.dot(out_blk, in_blk.T, preferred_element_type=jnp.float32)
    live_pairs = (doc_blk[:, None] == doc_blk[None, :]) & (index_row[:, None] >= index_row[None, :])
    decay_pairs = jnp.where(
        live_pairs[None],
        jnp.exp(jnp.minimum(cumulative[:, :, None] - cumulative[:, None, :], 0.0)),
        0.0,
    )
    weights = (scores[None] * decay_pairs * step_blk[:, None, :]).astype(jnp.bfloat16)
    within = jnp.einsum("hts,shp->thp", weights, values, preferred_element_type=jnp.float32)
    carried = jnp.einsum("tn,hnp->thp", out_blk.astype(jnp.float32), carry_state)
    factor = jnp.where(joined[None, :], jnp.exp(cumulative), 0.0)
    output = within + factor.T[:, :, None] * carried
    return (new_state, output)


def state_step(carry_state, block_piece):
    return block_pass(carry_state, block_piece, False)


def full_step(carry_state, block_piece):
    return block_pass(carry_state, block_piece, True)


def combine_pair(earlier, later):
    return (earlier[0] * later[0], later[0][:, None, None] * earlier[1] + later[1])


def chain(shard_link, summary):
    identity = (jnp.ones_like(shard_link), jnp.zeros_like(summary))
    prior = prefix_by_axis((shard_link, summary), SEQ, combine_pair, identity)
    return prior[1]


def correction(log_decay, joined, out_coeff, incoming):
    shard_cum = jnp.cumsum(log_decay, axis=1)
    factor = jnp.where(joined[None, :], jnp.exp(shard_cum), 0.0)
    carried = jnp.einsum("tn,hnp->thp", out_coeff.astype(jnp.float32), incoming)
    return factor.T[:, :, None] * carried


def local(
    stream,
    gate_input,
    in_coeff,
    out_coeff,
    step_raw,
    step_bias,
    decay_rate,
    skip_scale,
    norm_gain,
    out_proj,
    doc_starts,
):
    row_count = stream.shape[0]
    channels = stream.shape[1]
    head_count = step_raw.shape[0]
    head_size = channels // head_count
    state_size = in_coeff.shape[1]
    block_count = row_count // BLOCK
    shard_index = lax.axis_index(SEQ)
    offset = shard_index * row_count
    position = offset + lax.iota(jnp.int32, row_count)
    doc_ids = jnp.sum((doc_starts[None, :] <= position[:, None]).astype(jnp.int32), axis=1) - 1
    before = jnp.sum((doc_starts <= offset - 1).astype(jnp.int32)) - 1
    step_size = jax.nn.softplus(step_raw + step_bias[:, None])
    log_decay = -step_size * decay_rate[:, None]
    block_docs = doc_ids.reshape(block_count, BLOCK)
    block_before = jnp.concatenate([before[None], block_docs[:-1, -1]])
    pieces = (
        stream.reshape(block_count, BLOCK, channels),
        in_coeff.reshape(block_count, BLOCK, state_size),
        out_coeff.reshape(block_count, BLOCK, state_size),
        step_size.reshape(head_count, block_count, BLOCK).transpose(1, 0, 2),
        log_decay.reshape(head_count, block_count, BLOCK).transpose(1, 0, 2),
        block_docs,
        block_before,
    )
    zero_state = jnp.zeros((head_count, state_size, head_size), jnp.float32)
    joined = doc_ids == before
    shard_link = jnp.where(joined[-1], jnp.exp(jnp.sum(log_decay, axis=1)), 0.0)
    summary, unused = lax.scan(state_step, zero_state, pieces)
    incoming = chain(shard_link, summary)
    last_state, outputs = lax.scan(full_step, zero_state, pieces)
    ssm_out = outputs.reshape(row_count, head_count, head_size) + correction(
        log_decay, joined, out_coeff, incoming
    )
    ssm_out = ssm_out + skip_scale[None, :, None] * stream.reshape(
        row_count, head_count, head_size
    ).astype(jnp.float32)
    gated = ssm_out.reshape(row_count, channels) * jax.nn.silu(gate_input.astype(jnp.float32))
    square_sum = taken_together(jnp.sum(gated * gated, axis=1), "head")
    scale_row = lax.rsqrt(square_sum / DI + EPSILON)
    hidden = (gated * scale_row[:, None] * norm_gain[None, :]).astype(jnp.bfloat16)
    summed = sent_and_summed(
        jnp.dot(hidden, out_proj, preferred_element_type=jnp.float32).astype(jnp.bfloat16),
        "head",
        0,
    )
    return summed.astype(jnp.bfloat16)


def solution(mesh):
    split = Mesh(
        mesh.devices.reshape(4, 8, 2, mesh.shape["head"]), ("seq_0", "seq_1", "seq_2", "head")
    )
    in_specs = (
        P(SEQ, "head"),
        P(SEQ, "head"),
        P(SEQ, None),
        P(SEQ, None),
        P("head", SEQ),
        P("head"),
        P("head"),
        P("head"),
        P("head"),
        P("head", None),
        P(),
    )
    out_specs = P(SEQ_HEAD, None)
    return jax.shard_map(local, mesh=split, in_specs=in_specs, out_specs=out_specs, check_vma=False)
```

profile of v0, /device:TPU:8, one launch (start us, length us, event | category | flops | bytes accessed | tf_op | source)
XLA Modules:
  0.0 283.6 jit_solution(16058988615829512872)
XLA Ops:
  8.2 1.3 fusion.132
  12.4 1.6 copy.51
  14.0 1.3 pad_add_fusion
  15.4 13.8 %while.25 = (s32[]{:T(128)}, f32[20,128,64]{1,2,0:T(8,128)S(1)}, s32[2,256]{1,0:T(2,128)S(1)}, s32[2]{0:T(128)}, bf16[2,20,256]{2,1,0:T(8,128)(2,1)}, /*index=5*...) while((s32[]{:T(128)}, f32[20,128,64]{1,2,0:T(8,128)S(1)}, ...), condition=%wide.region_8.9_spmd.clone, body=%wide.region_7.8_spmd.clone.sunk | while | flops 88429080 | bytes 3722917 | solution.py:163
  18.7 1.3 dynamic_slice.114
  25.6 1.3 dynamic_slice.114
  34.1 2.4 all-reduce
  36.7 11.1 %all-gather.12.cloned.1.call-done = f32[40,128,64]{1,2,0:T(8,128)} async-done(((f32[20,128,64]{1,2,0:T(8,128)}), f32[40,128,64]{1,2,0:T(8,128)}) %all-gather.12.cloned.1.call-update) | async-done | bytes 1310736 | tf_op jit(solution)/shard_map/all_gather | solution.py:27
  47.8 2.3 bitcast_add_fusion.8
  50.2 17.5 %all-reduce.1 = f32[160]{0:T(256)S(1)} all-reduce(f32[160]{0:T(256)S(1)} %get-tuple-element.291), channel_id=4, replica_groups=mesh['seq_0'=4,'seq_1'=8,'seq_2'=2,'head'=4] {'seq_1'}, use_global_device_ids=true, to_apply=%add.1 | all-reduce | flops 160 | bytes 1280
  67.8 48.4 %all-gather.8.cloned.1.call-done = f32[8,20,128,64]{2,3,1,0:T(8,128)} async-done(((f32[1,20,128,64]{2,3,1,0:T(8,128)}), f32[8,20,128,64]{2,3,1,0:T(8,128)}) %all-gather.8.cloned.1.call-update) | async-done | bytes 5242896 | tf_op jit(solution)/shard_map/all_gather | solution.py:27
  116.2 3.8 %multiply_add_fusion = f32[1,20,128,64]{2,3,1,0:T(8,128)} fusion(f32[8,20,128,64]{2,3,1,0:T(8,128)} %all-gather.8.cloned.1.call-done, f32[20]{0:T(128)S(1)} %get-tuple-element.284, f32[20]{0:T(128)S(1)} %get-tuple-element.289, f32[20]{0:T(128)S(1)} %get-tuple-element.288, f32[20]{0:T(128)S(1)} %get-tuple-element.287, f32[20]{0:T(128)S(1)} %get-tuple-element.286, ...), kind=kLoop, calls=%fused_computation.129 | loop fusion | flops 2457600 | bytes 5898880 | tf_op jit(solution)/shard_map/add | solution.py:107
  120.1 78.2 %while.24 = (s32[]{:T(128)}, f32[20,128,64]{1,2,0:T(8,128)S(1)}, f32[2,256,20,64]{1,0,3,2:T(2,128)}, s32[2,256]{1,0:T(2,128)S(1)}, s32[2]{0:T(128)}, /*index=5*/...) while((s32[]{:T(128)}, f32[20,128,64]{1,2,0:T(8,128)S(1)}, ...), condition=%wide.region_3.4_spmd.clone, body=%wide.region_2.3_spmd.clone.sunk | while | flops 365586464 | bytes 16479678 | solution.py:165
  121.0 1.3 dynamic_slice.108
  129.0 1.7 fusion.175
  130.7 1.3 copy.71
  132.1 27.1 %dynamic_update_slice.6 = f32[2,256,20,64]{1,0,3,2:T(2,128)} dynamic-update-slice(f32[2,256,20,64]{1,0,3,2:T(2,128)} %get-tuple-element.429, f32[1,256,20,64]{1,0,3,2:T(1,128)S(1)} %copy.71, s32[]{:T(128)S(6)} %copy.76, s32[]{:T(128)} %constant.49.clone.1..sunk, s32[]{:T(128)} %constant.49.clone.1..sunk, s32[]{:T(128)} %constant.49.clone.1..sunk) | dynamic-update-slice | bytes 2621444 | tf_op jit(solution)/shard_map/while/body/jit(dynamic_update_index_in_dim)/dynamic_update_slice | solution.py:165
  160.1 1.3 dynamic_slice.108
  168.1 1.7 fusion.175
  169.8 1.3 copy.71
  171.2 27.0 %dynamic_update_slice.6 = f32[2,256,20,64]{1,0,3,2:T(2,128)} dynamic-update-slice(f32[2,256,20,64]{1,0,3,2:T(2,128)} %get-tuple-element.429, f32[1,256,20,64]{1,0,3,2:T(1,128)S(1)} %copy.71, s32[]{:T(128)S(6)} %copy.76, s32[]{:T(128)} %constant.49.clone.1..sunk, s32[]{:T(128)} %constant.49.clone.1..sunk, s32[]{:T(128)} %constant.49.clone.1..sunk) | dynamic-update-slice | bytes 2621444 | tf_op jit(solution)/shard_map/while/body/jit(dynamic_update_index_in_dim)/dynamic_update_slice | solution.py:165
  198.2 2.9 %copy.58 = f32[512,1280]{0,1:T(8,128)} copy(bf16[512,1280]{1,0:T(8,128)(2,1)} %param.15) | data formatting | bytes 3932160 | tf_op jit(solution)/shard_map/convert_element_type | solution.py:171
  201.3 3.6 %reshape.255 = f32[512,20,64]{0,2,1:T(8,128)S(1)} reshape(f32[2,256,20,64]{1,0,3,2:T(2,128)} %get-tuple-element.99) | data formatting | bytes 5242880 | tf_op jit(solution)/shard_map/reshape | solution.py:166
  204.9 1.2 reduce-window.6
  206.5 9.8 %all-gather.3 = f32[4,1,20]{2,1,0:T(1,128)S(1)} all-gather(f32[1,1,20]{2,1,0:T(1,128)S(1)} %fusion.134), channel_id=1, replica_groups=mesh['seq_0'=4,'seq_1'=8,'seq_2'=2,'head'=4] {'seq_0'}, dimensions={0}, use_global_device_ids=true | all-gather | bytes 400 | tf_op jit(solution)/shard_map/all_gather | solution.py:27
  216.5 7.7 %fusion.44 = f32[512,20,64]{0,2,1:T(8,128)} fusion(f32[512,20,64]{0,2,1:T(8,128)S(1)} %reshape.255, f32[512,20,64]{0,2,1:T(8,128)} %bitcast.257, f32[20]{0:T(128)S(1)} %copy-done.26, f32[512,20]{0,1:T(8,128)S(1)} %select_bitcast_fusion.1, f32[4,20,128,64]{2,3,1,0:T(8,128)} %all-gather.10.cloned.1.call-done, ...), kind=kOutput, calls=%fused_computation.74 | convolution fusion | flops 177438720 | bytes 17212766 | tf_op jit(solution)/shard_map/tn,hnp->thp/dot_general | solution.py:119
  224.2 2.1 copy.59
  226.4 2.2 multiply_reduce_fusion
  228.6 8.5 %all_to_all.11 = f32[4,1,512]{2,1,0:T(1,128)S(1)} all-to-all(f32[4,1,512]{2,1,0:T(1,128)S(1)} %broadcast_in_dim.75), channel_id=1, replica_groups=mesh['seq_0'=4,'seq_1'=8,'seq_2'=2,'head'=4] {'head'}, dimensions={0} | all-to-all | bytes 16384 | tf_op jit(solution)/shard_map/all_to_all | solution.py:39
  237.1 7.4 %convolution_convert_fusion = bf16[512,2560]{1,0:T(8,128)(2,1)S(1)} fusion(bf16[1280,2560]{1,0:T(8,128)(2,1)} %param.24, f32[1280]{0:T(1024)S(1)} %copy-done.25, f32[512]{0:T(512)S(1)} %add_rsqrt_fusion, f32[512,1280]{1,0:T(8,128)S(1)} %copy.59, bf16[512,1280]{1,0:T(8,128)(2,1)} %param.16), kind=kOutput, calls=%fused_computation.65 | convolution fusion | flops 3362652160 | bytes 13114368 | tf_op jit(solution)/shard_map/dot_general | solution.py:177
  244.5 31.1 %all_to_all.12 = bf16[4,128,2560]{2,1,0:T(8,128)(2,1)S(1)} all-to-all(bf16[4,128,2560]{2,1,0:T(8,128)(2,1)S(1)} %bitcast.256), channel_id=1, replica_groups=mesh['seq_0'=4,'seq_1'=8,'seq_2'=2,'head'=4] {'head'}, dimensions={0} | all-to-all | bytes 5242880 | tf_op jit(solution)/shard_map/all_to_all | solution.py:56
  275.6 1.4 reduce_sum.62
  (153 shorter events, 32.1 us)
Async XLA Ops:
  6.5 8.8 %copy-start = (bf16[512,128]{1,0:T(8,128)(2,1)S(1)}, bf16[512,128]{1,0:T(8,128)(2,1)}, u32[]{:S(2)}) copy-start(bf16[512,128]{1,0:T(8,128)(2,1)} %param.17) | copy-start | bytes 393220
  6.5 41.3 %all-gather.12.cloned.1.call-start = ((), (), s32[]{:S(2)}) async-start(), calls=%async_computation.4 | async-start | bytes 1966080 | tf_op jit(solution)/shard_map/all_gather | solution.py:27
  11.1 4.2 %copy-start.3 = (f32[20,512]{1,0:T(8,128)}, f32[20,512]{1,0:T(8,128)S(1)}, u32[]{:S(2)}) copy-start(f32[20,512]{1,0:T(8,128)S(1)} %get-tuple-element.276) | copy-start | bytes 122884
  15.4 14.7 %copy-start.28 = (u32[256]{0:T(256)S(1)}, u32[256]{0:T(256)}, u32[]{:S(2)}) copy-start(u32[256]{0:T(256)} %constant.101) | copy-start | bytes 3076
  15.4 15.4 %copy-start.27 = (u32[256]{0:T(256)S(1)}, u32[256]{0:T(256)}, u32[]{:S(2)}) copy-start(u32[256]{0:T(256)} %constant.96) | copy-start | bytes 3076
  29.2 0.8 copy-start.2
  30.0 86.2 %all-gather.8.cloned.1.call-start = ((), (), s32[]{:S(2)}) async-start(), calls=%async_computation.2 | async-start | bytes 5898240 | tf_op jit(solution)/shard_map/all_gather | solution.py:27
  32.7 83.5 %copy-start.19 = (pred[512]{0:T(512)(128)(4,1)}, pred[512]{0:T(512)(128)(4,1)S(1)}, u32[]{:S(2)}) copy-start(pred[512]{0:T(512)(128)(4,1)S(1)} %broadcast_compare_fusion.1) | copy-start | bytes 1540
  36.7 79.5 %copy-start.21 = (f32[20]{0:T(128)}, f32[20]{0:T(128)S(1)}, u32[]{:S(2)}) copy-start(f32[20]{0:T(128)S(1)} %get-tuple-element.292) | copy-start | bytes 244
  36.7 79.5 %copy-start.23 = (f32[20]{0:T(128)}, f32[20]{0:T(128)S(1)}, u32[]{:S(2)}) copy-start(f32[20]{0:T(128)S(1)} %get-tuple-element.293) | copy-start | bytes 244
  50.1 166.3 %all-gather.10.cloned.1.call-start = ((), (), s32[]{:S(2)}) async-start(), calls=%async_computation.3 | async-start | bytes 3276800 | tf_op jit(solution)/shard_map/all_gather | solution.py:27
  67.7 52.2 %copy-start.5 = (f32[20]{0:T(128)}, f32[20]{0:T(128)S(1)}, u32[]{:S(2)}) copy-start(f32[20]{0:T(128)S(1)} %get-tuple-element.284) | copy-start | bytes 244
  67.7 52.2 %copy-start.7 = (f32[20]{0:T(128)}, f32[20]{0:T(128)S(1)}, u32[]{:S(2)}) copy-start(f32[20]{0:T(128)S(1)} %get-tuple-element.285) | copy-start | bytes 244
  67.7 52.2 %copy-start.9 = (f32[20]{0:T(128)}, f32[20]{0:T(128)S(1)}, u32[]{:S(2)}) copy-start(f32[20]{0:T(128)S(1)} %get-tuple-element.286) | copy-start | bytes 244
  67.8 52.2 %copy-start.11 = (f32[20]{0:T(128)}, f32[20]{0:T(128)S(1)}, u32[]{:S(2)}) copy-start(f32[20]{0:T(128)S(1)} %get-tuple-element.287) | copy-start | bytes 244
  67.8 52.2 %copy-start.13 = (f32[20]{0:T(128)}, f32[20]{0:T(128)S(1)}, u32[]{:S(2)}) copy-start(f32[20]{0:T(128)S(1)} %get-tuple-element.288) | copy-start | bytes 244
  67.8 52.2 %copy-start.15 = (f32[20]{0:T(128)}, f32[20]{0:T(128)S(1)}, u32[]{:S(2)}) copy-start(f32[20]{0:T(128)S(1)} %get-tuple-element.289) | copy-start | bytes 244
  67.8 52.2 %copy-start.17 = (f32[20]{0:T(128)}, f32[20]{0:T(128)S(1)}, u32[]{:S(2)}) copy-start(f32[20]{0:T(128)S(1)} %get-tuple-element.290) | copy-start | bytes 244
  116.2 3.8 %copy-start.1 = (bf16[512,128]{1,0:T(8,128)(2,1)S(1)}, bf16[512,128]{1,0:T(8,128)(2,1)}, u32[]{:S(2)}) copy-start(bf16[512,128]{1,0:T(8,128)(2,1)} %param.18) | copy-start | bytes 393220
  198.2 2.9 %copy-start.4 = (f32[20,512]{1,0:T(8,128)S(1)}, f32[20,512]{1,0:T(8,128)}, u32[]{:S(2)}) copy-start(f32[20,512]{1,0:T(8,128)} %copy-done.3) | copy-start | bytes 122884
  201.2 15.2 %copy-start.20 = (pred[512]{0:T(512)(128)(4,1)S(1)}, pred[512]{0:T(512)(128)(4,1)}, u32[]{:S(2)}) copy-start(pred[512]{0:T(512)(128)(4,1)} %copy-done.19) | copy-start | bytes 1540
  201.2 15.3 %copy-start.6 = (f32[20]{0:T(128)S(1)}, f32[20]{0:T(128)}, u32[]{:S(2)}) copy-start(f32[20]{0:T(128)} %copy-done.5) | copy-start | bytes 244
  201.2 15.3 %copy-start.8 = (f32[20]{0:T(128)S(1)}, f32[20]{0:T(128)}, u32[]{:S(2)}) copy-start(f32[20]{0:T(128)} %copy-done.7) | copy-start | bytes 244
  201.2 15.3 %copy-start.10 = (f32[20]{0:T(128)S(1)}, f32[20]{0:T(128)}, u32[]{:S(2)}) copy-start(f32[20]{0:T(128)} %copy-done.9) | copy-start | bytes 244
  201.2 15.3 %copy-start.12 = (f32[20]{0:T(128)S(1)}, f32[20]{0:T(128)}, u32[]{:S(2)}) copy-start(f32[20]{0:T(128)} %copy-done.11) | copy-start | bytes 244
  201.2 15.3 %copy-start.14 = (f32[20]{0:T(128)S(1)}, f32[20]{0:T(128)}, u32[]{:S(2)}) copy-start(f32[20]{0:T(128)} %copy-done.13) | copy-start | bytes 244
  201.2 15.3 %copy-start.16 = (f32[20]{0:T(128)S(1)}, f32[20]{0:T(128)}, u32[]{:S(2)}) copy-start(f32[20]{0:T(128)} %copy-done.15) | copy-start | bytes 244
  201.2 15.3 %copy-start.18 = (f32[20]{0:T(128)S(1)}, f32[20]{0:T(128)}, u32[]{:S(2)}) copy-start(f32[20]{0:T(128)} %copy-done.17) | copy-start | bytes 244
  201.2 15.3 %copy-start.22 = (f32[20]{0:T(128)S(1)}, f32[20]{0:T(128)}, u32[]{:S(2)}) copy-start(f32[20]{0:T(128)} %copy-done.21) | copy-start | bytes 244
  201.3 15.3 %copy-start.24 = (f32[20]{0:T(128)S(1)}, f32[20]{0:T(128)}, u32[]{:S(2)}) copy-start(f32[20]{0:T(128)} %copy-done.23) | copy-start | bytes 244
  201.3 15.3 %copy-start.26 = (f32[20]{0:T(128)S(1)}, f32[20]{0:T(128)}, u32[]{:S(2)}) copy-start(f32[20]{0:T(128)} %param.22) | copy-start | bytes 244
  226.3 10.7 %copy-start.25 = (f32[1280]{0:T(1024)S(1)}, f32[1280]{0:T(1024)}, u32[]{:S(2)}) copy-start(f32[1280]{0:T(1024)} %param.23) | copy-start | bytes 15364
Sparse Core Ops, SparseCore 0:
  30.2 17.6 all-gather.11
  50.3 65.9 all-gather.7
  120.2 36.1 all-gather.9
where the time goes:
time: 288 us; the launch traced here: 284 us
  local copies, waits for them, and re-layouts  82 us (28%)
  blocking collectives  69.3 us (24%)
  waiting for transfers between devices  59.6 us (21%)
  other arithmetic  27.1 us (9%)
  matrix products  27 us (9%)
  between operations  15.6 us (5%)
    all_gather x3, waiting for transfers between devices, prefix_by_axis(): pieces = jax.tree.map(lambda part: lax.all_gather(part, axis), total)  59.5 us
    dynamic_update_slice x4, local copies, waits for them, and re-layouts, local(): last_state, outputs = lax.scan(full_step, zero_state, pieces)  56.8 us
    all_to_all x1, blocking collectives, sent_and_summed(): lax.all_to_all(split_up(value, dim, devices), axis, 0, 0, tiled=True)  31.1 us
    unnamed x2, blocking collectives  19.9 us
    all_gather x1, blocking collectives, prefix_by_axis(): pieces = jax.tree.map(lambda part: lax.all_gather(part, axis), total)  9.81 us
    all_to_all x1, blocking collectives, from_everyone(): lax.all_to_all(jnp.broadcast_to(value[None], (devices, *value.shape)), ax...  8.47 us
    dot_general x1, matrix products, correction(): carried = jnp.einsum('tn,hnp->thp', out_coeff.astype(jnp.float32), incoming)  7.67 us
    dot_general x1, matrix products, local(): jnp.dot(hidden, out_proj, preferred_element_type=jnp.float32)  7.4 us
  transfers between devices with their start and end apart: 3, of which 2 were waited for; matrix products, arithmetic and copies ran while one was open for 31% of the time, Pallas kernels for 0%

commit v1 on v0

v1 whole, which is shorter than its diff:
```python
import functools

import jax
import jax.numpy as jnp
from jax import lax
from jax.experimental import pallas as pl
from jax.experimental.pallas import tpu as pltpu
from jax.sharding import Mesh
from jax.sharding import PartitionSpec as P

BLOCK = 256
SEQ = ("seq_0", "seq_1", "seq_2")
SEQ_HEAD = ("seq_0", "seq_1", "seq_2", "head")
EPSILON = 1e-05
F32 = jnp.float32
BF16 = jnp.bfloat16
PAD = 32
LANES = 128

VMEM_SPEC = pl.BlockSpec(memory_space=pltpu.VMEM)
SMEM_SPEC = pl.BlockSpec(memory_space=pltpu.SMEM)


def dot(a, b):
    return jnp.dot(a, b, preferred_element_type=F32)


def dot_first(a, b):
    return lax.dot_general(a, b, (((0,), (0,)), ((), ())), preferred_element_type=F32)


def dot_last(a, b):
    return lax.dot_general(a, b, (((1,), (1,)), ((), ())), preferred_element_type=F32)


def two_parts(value):
    high = value.astype(BF16)
    low = (value - high.astype(F32)).astype(BF16)
    return jnp.concatenate([high, low], axis=0)


def head_lanes(width, head_size):
    row = lax.broadcasted_iota(jnp.int32, (2 * PAD, width), 0)
    lane = lax.broadcasted_iota(jnp.int32, (2 * PAD, width), 1)
    head = jnp.where(row >= PAD, row - PAD, row)
    first = head * head_size
    return jnp.where((lane >= first) & (lane < first + head_size), 1.0, 0.0).astype(BF16)


def as_column(row, count):
    wide = jnp.broadcast_to(row, (count, row.shape[1]))
    i = lax.broadcasted_iota(jnp.int32, wide.shape, 0)
    j = lax.broadcasted_iota(jnp.int32, wide.shape, 1)
    return jnp.sum(jnp.where(i == j, wide, 0.0), axis=1, keepdims=True)


def as_row(column, width):
    wide = jnp.broadcast_to(column, (column.shape[0], width))
    i = lax.broadcasted_iota(jnp.int32, wide.shape, 0)
    j = lax.broadcasted_iota(jnp.int32, wide.shape, 1)
    return jnp.sum(jnp.where(i == j, wide, 0.0), axis=0, keepdims=True)


def docs_column(starts_row, first, count):
    position = first + lax.broadcasted_iota(jnp.int32, (count, starts_row.shape[1]), 0)
    hit = jnp.where(starts_row <= position, 1.0, 0.0)
    return jnp.sum(hit, axis=1, keepdims=True)


def docs_row(starts_row, first, count):
    position = first + lax.broadcasted_iota(jnp.int32, (count, starts_row.shape[1]), 0)
    hit = jnp.where(starts_row <= position, 1.0, 0.0).astype(BF16)
    ones = jnp.ones((8, starts_row.shape[1]), BF16)
    return dot_last(ones, hit)[:1, :]


def state_kernel(
    head_size,
    offset_ref,
    stream_ref,
    in_ref,
    step_ref,
    bias_ref,
    rate_ref,
    starts_ref,
    summary_ref,
    scaled_ref,
    first_ref,
    factor_ref,
):
    heads, rows = step_ref.shape
    width = stream_ref.shape[1]
    offset = offset_ref[0]
    starts = starts_ref[...]
    docs = docs_column(starts, offset, rows)
    before = jnp.max(docs_column(starts, offset - 1, 8)[:1, :], axis=0, keepdims=True)
    raw = step_ref[...] + as_column(bias_ref[...], heads)
    step = jnp.maximum(raw, 0.0) + jnp.log1p(jnp.exp(-jnp.abs(raw)))
    log_decay = -step * as_column(rate_ref[...], heads)
    i = lax.broadcasted_iota(jnp.int32, (BLOCK, BLOCK), 0)
    j = lax.broadcasted_iota(jnp.int32, (BLOCK, BLOCK), 1)
    upper = jnp.where(i <= j, 1.0, 0.0)
    into, out_of, half, last = [], [], [], []
    for block in range(rows // BLOCK):
        cut = slice(block * BLOCK, (block + 1) * BLOCK)
        cumulative = jnp.dot(
            log_decay[:, cut], upper, precision=lax.Precision.HIGHEST, preferred_element_type=F32
        )
        end = cumulative[:, BLOCK - 1 :]
        middle = 0.5 * end
        into.append(step[:, cut] * jnp.exp(middle - cumulative))
        out_of.append(jnp.exp(cumulative - middle))
        half.append(jnp.exp(middle))
        last.append(end)
    ends = [docs[(b + 1) * BLOCK - 1 : (b + 1) * BLOCK, :] for b in range(rows // BLOCK)]
    joined_0 = jnp.where(ends[0] == before, 1.0, 0.0)
    joined_1 = jnp.where(ends[1] == ends[0], 1.0, 0.0)
    gate_0 = joined_0 * jnp.exp(last[0])
    gate_1 = joined_1 * jnp.exp(last[1])
    link = joined_0 * joined_1 * jnp.exp(last[0] + last[1])
    lane = lax.broadcasted_iota(jnp.int32, (heads, LANES), 1)
    constants = jnp.where(lane == 0, half[0], 0.0)
    constants = jnp.where(lane == 1, half[1], constants)
    constants = jnp.where(lane == 2, gate_0, constants)
    constants = jnp.where(lane == 3, gate_1, constants)
    nothing = jnp.zeros((PAD - heads, rows + LANES), F32)
    spread = head_lanes(width, head_size)
    wide_in = jnp.concatenate([jnp.concatenate(into + [constants], axis=1), nothing], axis=0)
    wide_out = jnp.concatenate([jnp.concatenate(out_of + [constants], axis=1), nothing], axis=0)
    factor_ref[...] = two_parts(wide_out)
    per_lane = dot_first(two_parts(wide_in), spread)
    constant_rows = per_lane[rows : rows + 8, :]
    states = []
    for block in range(rows // BLOCK):
        cut = slice(block * BLOCK, (block + 1) * BLOCK)
        scaled = (stream_ref[cut, :].astype(F32) * per_lane[cut, :]).astype(BF16)
        scaled_ref[cut, :] = scaled
        to_end = jnp.where(docs[cut, :] == ends[block], in_ref[cut, :].astype(F32), 0.0)
        states.append(constant_rows[block : block + 1, :] * dot_first(to_end.astype(BF16), scaled))
    first_ref[...] = states[0]
    summary = constant_rows[3:4, :] * states[0] + states[1]
    high = link.astype(BF16).astype(F32)
    link_row = as_row(high, LANES) + pltpu.roll(as_row(link - high, LANES), PAD, 1)
    summary_ref[:, :width] = summary.astype(BF16)
    summary_ref[:, width:] = jnp.broadcast_to(link_row, (summary.shape[0], LANES)).astype(BF16)


def within_kernel(
    head_size,
    offset_ref,
    stream_ref,
    gate_ref,
    in_ref,
    out_ref,
    scaled_ref,
    factor_ref,
    skip_ref,
    starts_ref,
    base_ref,
    slope_ref,
):
    rows, width = stream_ref.shape
    heads = skip_ref.shape[1]
    offset = offset_ref[0]
    starts = starts_ref[...]
    docs = docs_column(starts, offset, rows)
    docs_across = docs_row(starts, offset, rows)
    spread = head_lanes(width, head_size)
    skip = jnp.concatenate(
        [as_column(skip_ref[...], heads), jnp.zeros((PAD - heads, 1), F32)], axis=0
    )
    skip_row = dot_first(two_parts(jnp.broadcast_to(skip, (PAD, LANES))), spread)[:1, :]
    i = lax.broadcasted_iota(jnp.int32, (BLOCK, BLOCK), 0)
    j = lax.broadcasted_iota(jnp.int32, (BLOCK, BLOCK), 1)
    for block in range(rows // BLOCK):
        cut = slice(block * BLOCK, (block + 1) * BLOCK)
        scores = dot_last(out_ref[cut, :], in_ref[cut, :])
        live = (i >= j) & (docs[cut, :] == docs_across[:, cut])
        weights = jnp.where(live, scores, 0.0).astype(BF16)
        per_lane = dot_first(factor_ref[:, cut], spread)
        within = dot(weights, scaled_ref[cut, :])
        value = per_lane * within + skip_row * stream_ref[cut, :].astype(F32)
        gate = gate_ref[cut, :].astype(F32)
        gate = gate / (1.0 + jnp.exp(-gate))
        base_ref[cut, :] = value * gate
        slope_ref[cut, :] = per_lane * gate


def scan_kernel(head_size, pieces_ref, before_ref):
    shards, rows, wide = pieces_ref.shape
    width = wide - LANES
    links = pieces_ref[:, 0, width:]
    lane = lax.broadcasted_iota(jnp.int32, (LANES, width), 0)
    spot = lax.broadcasted_iota(jnp.int32, (LANES, width), 1)
    head = jnp.where(lane >= PAD, lane - PAD, lane)
    first = head * head_size
    spread = jnp.where(
        (lane < 2 * PAD) & (spot >= first) & (spot < first + head_size), 1.0, 0.0
    ).astype(BF16)
    per_lane = dot(links, spread)
    state = jnp.zeros((rows, width), F32)
    for shard in range(shards):
        before_ref[shard] = state.astype(BF16)
        state = per_lane[shard : shard + 1, :] * state + pieces_ref[shard, :, :width].astype(F32)


def finish_kernel(
    head_size,
    offset_ref,
    blocks_ref,
    out_ref,
    before_ref,
    first_ref,
    factor_ref,
    base_ref,
    slope_ref,
    gain_ref,
    starts_ref,
    proj_ref,
    hidden_ref,
    squares_ref,
    send_a_ref,
    send_b_ref,
):
    rows, width = base_ref.shape
    offset = offset_ref[0]
    starts = starts_ref[...]
    docs = docs_column(starts, offset, rows)
    before = jnp.max(docs_column(starts, offset - 1, 8)[:1, :], axis=0, keepdims=True)
    spread = head_lanes(width, head_size)
    constant_rows = dot_first(factor_ref[:, rows:], spread)[:8, :]
    state = before_ref[...].astype(F32)
    gain = gain_ref[...]
    sums = []
    for block in range(rows // BLOCK):
        cut = slice(block * BLOCK, (block + 1) * BLOCK)
        joined = jnp.where(docs[cut, :] == before, out_ref[cut, :].astype(F32), 0.0).astype(BF16)
        carried = dot(joined, (constant_rows[block : block + 1, :] * state).astype(BF16))
        gated = base_ref[cut, :] + slope_ref[cut, :] * carried
        square = gated * gated
        total = square[:, :LANES]
        for lane in range(LANES, width, LANES):
            total = total + square[:, lane : lane + LANES]
        sums.append(total)
        hidden_ref[cut, :] = (gated * gain).astype(BF16)
        state = constant_rows[2:3, :] * state + first_ref[...]
        before = docs[(block + 1) * BLOCK - 1 : (block + 1) * BLOCK, :]
    flat = jnp.concatenate([jnp.sum(jnp.transpose(s), axis=0, keepdims=True) for s in sums], axis=1)
    squares_ref[...] = flat
    step = rows // 4
    half = proj_ref.shape[1] // 2
    for number, (send_ref, low) in enumerate(((send_a_ref, 0), (send_b_ref, half))):
        for part in range(2):
            block = blocks_ref[2 * number + part]
            piece = hidden_ref[pl.ds(block * step, step), :]
            send_ref[part * step : (part + 1) * step, :] = dot(
                piece, proj_ref[:, low : low + half]
            ).astype(BF16)


def keep_kernel(blocks_ref, hidden_ref, proj_ref, keep_a_ref, keep_b_ref):
    step = hidden_ref.shape[0] // 4
    half = proj_ref.shape[1] // 2
    for number, (keep_ref, low) in enumerate(((keep_a_ref, 0), (keep_b_ref, half))):
        for part in range(2):
            block = blocks_ref[4 + 2 * number + part]
            piece = hidden_ref[pl.ds(block * step, step), :]
            keep_ref[part * step : (part + 1) * step, :] = dot(
                piece, proj_ref[:, low : low + half]
            ).astype(BF16)


def middle_kernel(keep_a_ref, keep_b_ref, got_a_ref, got_b_ref, send_a_ref, send_b_ref):
    step = send_a_ref.shape[0]
    for keep_ref, got_ref, send_ref in (
        (keep_a_ref, got_a_ref, send_a_ref),
        (keep_b_ref, got_b_ref, send_b_ref),
    ):
        send_ref[...] = (
            keep_ref[step:, :].astype(F32) + got_ref[step:, :].astype(F32)
        ).astype(BF16)


def last_kernel(
    channels, squares_ref, keep_a_ref, keep_b_ref, got_a_ref, got_b_ref, far_a_ref, far_b_ref, out_ref
):
    step = far_a_ref.shape[0]
    half = far_a_ref.shape[1]
    mean = jnp.sum(squares_ref[...], axis=(0, 1))[None, :] / channels
    scale = as_column(lax.rsqrt(mean + EPSILON), step)
    for keep_ref, got_ref, far_ref, low in (
        (keep_a_ref, got_a_ref, far_a_ref, 0),
        (keep_b_ref, got_b_ref, far_b_ref, half),
    ):
        total = (
            keep_ref[:step, :].astype(F32) + got_ref[:step, :].astype(F32) + far_ref[...].astype(F32)
        )
        out_ref[:, low : low + half] = (total * scale).astype(BF16)


def call(kernel, out_shape, scalars, arrays, flops, name):
    single = not isinstance(out_shape, (tuple, list))
    return pl.pallas_call(
        kernel,
        out_shape=out_shape,
        in_specs=[SMEM_SPEC] * len(scalars) + [VMEM_SPEC] * len(arrays),
        out_specs=VMEM_SPEC if single else [VMEM_SPEC] * len(out_shape),
        cost_estimate=pl.CostEstimate(flops=flops, bytes_accessed=4_000_000, transcendentals=0),
        compiler_params=pltpu.CompilerParams(vmem_limit_bytes=48 * 1024 * 1024),
        name=name,
    )(*scalars, *arrays)


def local(
    total_channels,
    stream,
    gate_input,
    in_coeff,
    out_coeff,
    step_raw,
    step_bias,
    decay_rate,
    skip_scale,
    norm_gain,
    out_proj,
    doc_starts,
):
    rows, width = stream.shape
    heads = step_raw.shape[0]
    head_size = width // heads
    states = in_coeff.shape[1]
    model = out_proj.shape[1]
    shards = lax.axis_size(SEQ)
    y = lax.axis_index("head")
    offset = (lax.axis_index(SEQ) * rows).astype(jnp.int32)[None]
    starts = doc_starts[None, :]
    shape = jax.ShapeDtypeStruct
    summary, scaled, first, factor = call(
        functools.partial(state_kernel, head_size),
        [
            shape((states, width + LANES), BF16),
            shape((rows, width), BF16),
            shape((states, width), F32),
            shape((2 * PAD, rows + LANES), BF16),
        ],
        [offset],
        [stream, in_coeff, step_raw, step_bias[None], decay_rate[None], starts],
        2_000_000_000,
        "state",
    )
    pieces = lax.all_to_all(
        summary.reshape(shards, states // shards, width + LANES), SEQ, 0, 0, tiled=True
    )
    base, slope = call(
        functools.partial(within_kernel, head_size),
        [shape((rows, width), F32), shape((rows, width), F32)],
        [offset],
        [stream, gate_input, in_coeff, out_coeff, scaled, factor, skip_scale[None], starts],
        4_000_000_000,
        "within",
    )
    prior = call(
        functools.partial(scan_kernel, head_size),
        shape((shards, states // shards, width), BF16),
        [],
        [pieces],
        1_000_000_000,
        "scan",
    )
    incoming = lax.all_to_all(prior, SEQ, 0, 0, tiled=True).reshape(states, width)
    one, two, three = y ^ 1, y ^ 2, y ^ 3
    blocks = jnp.stack([one, two, three, two, y, three, y, one]).astype(jnp.int32)
    step = rows // 4
    half = model // 2
    hidden, squares, send_a, send_b = call(
        functools.partial(finish_kernel, head_size),
        [
            shape((rows, width), BF16),
            shape((1, rows), F32),
            shape((2 * step, half), BF16),
            shape((2 * step, half), BF16),
        ],
        [offset, blocks],
        [out_coeff, incoming, first, factor, base, slope, norm_gain[None], starts, out_proj],
        4_000_000_000,
        "finish",
    )
    pair_1 = [(i, i ^ 1) for i in range(4)]
    pair_3 = [(i, i ^ 3) for i in range(4)]
    all_squares = lax.all_to_all(squares.reshape(4, 1, step), "head", 0, 0, tiled=True)
    got_a = lax.ppermute(send_a, "head", pair_1)
    got_b = lax.ppermute(send_b, "head", pair_3)
    keep_a, keep_b = call(
        keep_kernel,
        [shape((2 * step, half), BF16), shape((2 * step, half), BF16)],
        [blocks],
        [hidden, out_proj],
        2_000_000_000,
        "keep",
    )
    more_a, more_b = call(
        middle_kernel,
        [shape((step, half), BF16), shape((step, half), BF16)],
        [],
        [keep_a, keep_b, got_a, got_b],
        1_000_000_000,
        "middle",
    )
    far_a = lax.ppermute(more_a, "head", pair_3)
    far_b = lax.ppermute(more_b, "head", pair_1)
    return call(
        functools.partial(last_kernel, total_channels),
        shape((step, model), BF16),
        [],
        [all_squares, keep_a, keep_b, got_a, got_b, far_a, far_b],
        1_000_000_000,
        "last",
    )


def solution(mesh):
    split = Mesh(
        mesh.devices.reshape(4, 8, 2, mesh.shape["head"]), ("seq_0", "seq_1", "seq_2", "head")
    )
    in_specs = (
        P(SEQ, "head"),
        P(SEQ, "head"),
        P(SEQ, None),
        P(SEQ, None),
        P("head", SEQ),
        P("head"),
        P("head"),
        P("head"),
        P("head"),
        P("head", None),
        P(),
    )
    out_specs = P(SEQ_HEAD, None)

    def whole(*args):
        step = functools.partial(local, float(args[0].shape[1]))
        return jax.shard_map(
            step, mesh=split, in_specs=in_specs, out_specs=out_specs, check_vma=False
        )(*args)

    return whole
```

time: 288 us -> 95.9 us (0.33); the launches traced: 284 us -> 94.4 us
  local copies, waits for them, and re-layouts: 82 us -> 9.66 us
  waiting for transfers between devices: 59.6 us -> 17.7 us
  blocking collectives: 69.3 us -> 33 us
  other arithmetic: 27.1 us -> 0 us
  matrix products: 27 us -> 0 us
  Pallas kernels: 0 us -> 20.3 us
  between operations: 15.6 us -> 0.16 us
  starting transfers between devices: 0.09 us -> 13.6 us
    all_gather x3 -> x0, waiting for transfers between devices: 59.5 us -> none  [prefix_by_axis(): pieces = jax.tree.map(lambda part: lax.all_gather(part, axis), total)]
    dynamic_update_slice x4 -> x0, local copies, waits for them, and re-layouts: 56.8 us -> none  [local(): last_state, outputs = lax.scan(full_step, zero_state, pieces)]
    dot_general x14 -> x0, matrix products: 26.3 us -> none  [the longest x1 7.67 us: correction(): carried = jnp.einsum('tn,hnp->thp', out_coeff.astype(jnp.float32), incoming)]
    pallas_call x0 -> x7, Pallas kernels: none -> 20.3 us  [call(): pl.pallas_call(kernel, out_shape=out_shape, in_specs=[SMEM_SPEC] * len(sc...]
    unnamed x2 -> x0, blocking collectives: 19.9 us -> none
    ppermute x0 -> x4, waiting for transfers between devices: none -> 9.99 us  [the longest x1 9.15 us: local(): got_a = lax.ppermute(send_a, 'head', pair_1)]
    all_gather x1 -> x0, blocking collectives: 9.81 us -> none  [prefix_by_axis(): pieces = jax.tree.map(lambda part: lax.all_gather(part, axis), total)]
    all_to_all x0 -> x1, waiting for transfers between devices: none -> 7.75 us  [local(): lax.all_to_all(prior, SEQ, 0, 0, tiled=True).reshape(states, width)]
  transfers between devices with their start and end apart: 3 -> 5, of which waited for: 2 -> 3; matrix products, arithmetic and copies ran while one was open for 31% -> 0% of each run, Pallas kernels for 0% -> 9%
where the time goes in v1:
time: 95.9 us; the launch traced here: 94.4 us
  blocking collectives  33 us (34%)
  Pallas kernels  20.3 us (21%)
  waiting for transfers between devices  17.7 us (18%)
  starting transfers between devices  13.6 us (14%)
  local copies, waits for them, and re-layouts  9.66 us (10%)
    all_to_all x1, blocking collectives, local(): lax.all_to_all(summary.reshape(shards, states // shards, width + LANES),...  25.6 us
    pallas_call x7, Pallas kernels, call(): pl.pallas_call(kernel, out_shape=out_shape, in_specs=[SMEM_SPEC] * len(sc...  20.3 us
    unnamed x34, local copies, waits for them, and re-layouts  9.31 us
    ppermute x1, waiting for transfers between devices, local(): got_a = lax.ppermute(send_a, 'head', pair_1)  9.15 us
    all_to_all x1, waiting for transfers between devices, local(): lax.all_to_all(prior, SEQ, 0, 0, tiled=True).reshape(states, width)  7.75 us
    all_to_all x1, blocking collectives, local(): lax.all_to_all(squares.reshape(4, 1, step), 'head', 0, 0, tiled=True)  7.4 us
    all_to_all x1, starting transfers between devices, local(): lax.all_to_all(prior, SEQ, 0, 0, tiled=True).reshape(states, width)  6.27 us
    ppermute x1, starting transfers between devices, local(): far_b = lax.ppermute(more_b, 'head', pair_1)  2.56 us
  transfers between devices with their start and end apart: 5, of which 3 were waited for; matrix products, arithmetic and copies ran while one was open for 0% of the time, Pallas kernels for 9%

profile of v1, /device:TPU:8, one launch (start us, length us, event | category | flops | bytes accessed | tf_op | source)
XLA Modules:
  0.0 94.4 jit_solution(11829587252176412253)
XLA Ops:
  0.0 1.3 %copy-done = bf16[512,1280]{1,0:T(8,128)(2,1)S(1)} copy-done((bf16[512,1280]{1,0:T(8,128)(2,1)S(1)}, bf16[512,1280]{1,0:T(8,128)(2,1)}, u32[]{:S(2)}) %copy-start) | copy-done | bytes 1310744
  1.3 0.9 copy-done.3
  2.2 0.8 copy-done.6
  3.0 0.7 copy-done.7
  3.7 0.7 copy-done.8
  4.3 0.7 copy-done.10
  5.0 1.4 %state.1 = (bf16[128,1408]{1,0:T(8,128)(2,1)S(1)}, bf16[512,1280]{1,0:T(8,128)(2,1)S(1)}, f32[128,1280]{1,0:T(8,128)S(1)}, bf16[64,640]{1,0:T(8,128)(2,1)S(1)}) custom-call(s32[1]{0:T(128)} %bitcast.offset_ref, bf16[512,1280]{1,0:T(8,128)(2,1)S(1)} %copy-done, bf16[512,128]{1,0:T(8,128)(2,1)S(1)} %copy-done.3, f32[20,512]{1,0:T(8,128)S(1)} %copy-done.6, ...), custom_call_target="tpu_custom_call" | custom-call | flops 2000000000 | bytes 4000000 | tf_op jit(solution)/shard_map/state/pallas_call | solution.py:303
  6.4 0.8 copy-done.12
  7.2 1.1 %copy-done.14 = bf16[512,1280]{1,0:T(8,128)(2,1)} copy-done((bf16[512,1280]{1,0:T(8,128)(2,1)}, bf16[512,1280]{1,0:T(8,128)(2,1)S(1)}, u32[]{:S(2)}) %copy-start.14) | copy-done | bytes 1310744
  8.3 0.1 reshape.9
  8.4 25.6 %all_to_all.15.pieces_ref = bf16[64,2,1408]{2,1,0:T(2,128)(2,1)S(1)} all-to-all(bf16[64,2,1408]{2,1,0:T(2,128)(2,1)S(1)} %reshape.9), channel_id=1, replica_groups=mesh['seq_0'=4,'seq_1'=8,'seq_2'=2,'head'=4] {'seq_0','seq_1','seq_2'}, dimensions={0} | all-to-all | bytes 720896 | tf_op jit(solution)/shard_map/all_to_all | solution.py:351
  34.0 0.0 copy-start.5
  34.1 1.4 %scan.1 = bf16[64,2,1280]{2,1,0:T(2,128)(2,1)} custom-call(bf16[64,2,1408]{2,1,0:T(2,128)(2,1)S(1)} %all_to_all.15.pieces_ref), custom_call_target="tpu_custom_call" | custom-call | flops 1000000000 | bytes 4000000 | tf_op jit(solution)/shard_map/scan/pallas_call | solution.py:303
  35.5 6.3 %all-to-all-start.1 = ((bf16[64,2,1280]{2,1,0:T(2,128)(2,1)}), bf16[64,2,1280]{2,1,0:T(2,128)(2,1)S(1)}, u32[]{:S(2)}, u32[]{:S(2)}) async-start(bf16[64,2,1280]{2,1,0:T(2,128)(2,1)} %scan.1), calls=%async_computation.1 | async-start | bytes 655360 | tf_op jit(solution)/shard_map/all_to_all | solution.py:370
  41.8 0.1 stack.23.blocks_ref
  41.9 1.3 %copy-done.15 = bf16[512,1280]{1,0:T(8,128)(2,1)S(1)} copy-done((bf16[512,1280]{1,0:T(8,128)(2,1)S(1)}, bf16[512,1280]{1,0:T(8,128)(2,1)}, u32[]{:S(2)}) %copy-start.15) | copy-done | bytes 1310744
  43.2 4.0 %within.1 = (f32[512,1280]{1,0:T(8,128)}, f32[512,1280]{1,0:T(8,128)}) custom-call(s32[1]{0:T(128)} %bitcast.offset_ref, bf16[512,1280]{1,0:T(8,128)(2,1)S(1)} %copy-done.1, bf16[512,1280]{1,0:T(8,128)(2,1)S(1)} %copy-done.2, bf16[512,128]{1,0:T(8,128)(2,1)S(1)} %copy-done.4, bf16[512,128]{1,0:T(8,128)(2,1)S(1)} %copy-done.5, ...), custom_call_target="tpu_custom_call" | custom-call | flops 4000000000 | bytes 4000000 | tf_op jit(solution)/shard_map/within/pallas_call | solution.py:303
  47.2 7.7 %all-to-all-done.1 = bf16[64,2,1280]{2,1,0:T(2,128)(2,1)S(1)} async-done(((bf16[64,2,1280]{2,1,0:T(2,128)(2,1)}), bf16[64,2,1280]{2,1,0:T(2,128)(2,1)S(1)}, u32[]{:S(2)}, u32[]{:S(2)}) %all-to-all-start.1) | async-done | bytes 327712 | tf_op jit(solution)/shard_map/all_to_all | solution.py:370
  54.9 0.1 reshape.10.before_ref
  55.1 0.0 copy-start.13
  55.1 1.1 %copy-done.13 = f32[128,1280]{1,0:T(8,128)S(1)} copy-done((f32[128,1280]{1,0:T(8,128)S(1)}, f32[128,1280]{1,0:T(8,128)}, u32[]{:S(2)}) %copy-start.13) | copy-done | bytes 655384
  56.2 7.3 %finish.1 = (bf16[512,1280]{1,0:T(8,128)(2,1)S(1)}, f32[1,512]{1,0:T(1,128)S(1)}, bf16[256,1280]{1,0:T(8,128)(2,1)S(1)}, bf16[256,1280]{1,0:T(8,128)(2,1)S(1)}) custom-call(s32[1]{0:T(128)} %bitcast.offset_ref, s32[8]{0:T(128)S(1)} %stack.23.blocks_ref, bf16[512,128]{1,0:T(8,128)(2,1)S(1)} %copy-done.5, bf16[128,1280]{1,0:T(8,128)(2,1)S(1)} %reshape.10.before_ref, ...), custom_call_target="tpu_custom_call" | custom-call | flops 4000000000 | bytes 4000000 | tf_op jit(solution)/shard_map/finish/pallas_call | solution.py:303
  63.4 0.5 collective-permute-start
  64.0 2.4 %collective-permute-start.1 = (bf16[256,1280]{1,0:T(8,128)(2,1)S(1)}, bf16[256,1280]{1,0:T(8,128)(2,1)S(1)}, u32[]{:S(2)}, u32[]{:S(2)}) collective-permute-start(bf16[256,1280]{1,0:T(8,128)(2,1)S(1)} %get-tuple-element.30), channel_id=1, source_target_pairs={{0,3},{1,2},{2,1},{3,0},{4,7},{5,6},{6,5},{7,4},{8,11},{9,10},{10,... | collective-permute-start | bytes 1966088 | tf_op jit(solution)/shard_map/ppermute | solution.py:392
  66.4 4.7 %keep.1 = (bf16[256,1280]{1,0:T(8,128)(2,1)S(1)}, bf16[256,1280]{1,0:T(8,128)(2,1)S(1)}) custom-call(s32[8]{0:T(128)S(1)} %stack.23.blocks_ref, bf16[512,1280]{1,0:T(8,128)(2,1)S(1)} %get-tuple-element.26.hidden_ref, bf16[1280,2560]{1,0:T(8,128)(2,1)} %proj_ref.3), custom_call_target="tpu_custom_call" | custom-call | flops 2000000000 | bytes 4000000 | tf_op jit(solution)/shard_map/keep/pallas_call | solution.py:303
  71.1 9.2 %collective-permute-done.got_a_ref = bf16[256,1280]{1,0:T(8,128)(2,1)S(1)} collective-permute-done((bf16[256,1280]{1,0:T(8,128)(2,1)S(1)}, bf16[256,1280]{1,0:T(8,128)(2,1)S(1)}, u32[]{:S(2)}, u32[]{:S(2)}) %collective-permute-start) | collective-permute-done | bytes 655392 | tf_op jit(solution)/shard_map/ppermute | solution.py:391
  80.3 0.8 collective-permute-done.1.got_b_ref
  81.1 0.2 middle.1
  81.3 1.8 %collective-permute-start.2 = (bf16[128,1280]{1,0:T(8,128)(2,1)S(1)}, bf16[128,1280]{1,0:T(8,128)(2,1)S(1)}, u32[]{:S(2)}, u32[]{:S(2)}) collective-permute-start(bf16[128,1280]{1,0:T(8,128)(2,1)S(1)} %get-tuple-element.31), channel_id=1, source_target_pairs={{0,3},{1,2},{2,1},{3,0},{4,7},{5,6},{6,5},{7,4},{8,11},{9,10},{10,... | collective-permute-start | bytes 983048 | tf_op jit(solution)/shard_map/ppermute | solution.py:409
  83.1 2.6 %collective-permute-start.3 = (bf16[128,1280]{1,0:T(8,128)(2,1)S(1)}, bf16[128,1280]{1,0:T(8,128)(2,1)S(1)}, u32[]{:S(2)}, u32[]{:S(2)}) collective-permute-start(bf16[128,1280]{1,0:T(8,128)(2,1)S(1)} %get-tuple-element.32), channel_id=1, source_target_pairs={{0,1},{1,0},{2,3},{3,2},{4,5},{5,4},{6,7},{7,6},{8,9},{9,8},{10,11... | collective-permute-start | bytes 983048 | tf_op jit(solution)/shard_map/ppermute | solution.py:410
  85.6 7.4 %all_to_all.16.squares_ref = f32[4,1,128]{2,1,0:T(1,128)S(1)} all-to-all(f32[4,1,128]{2,1,0:T(1,128)S(1)} %bitcast.10), channel_id=1, replica_groups=mesh['seq_0'=4,'seq_1'=8,'seq_2'=2,'head'=4] {'head'}, dimensions={0} | all-to-all | bytes 4096 | tf_op jit(solution)/shard_map/all_to_all | solution.py:390
  93.0 1.4 %last.1 = bf16[128,2560]{1,0:T(8,128)(2,1)} custom-call(f32[4,1,128]{2,1,0:T(1,128)S(1)} %all_to_all.16.squares_ref, bf16[256,1280]{1,0:T(8,128)(2,1)S(1)} %get-tuple-element.27.keep_a_ref, bf16[256,1280]{1,0:T(8,128)(2,1)S(1)} %get-tuple-element.28.keep_b_ref, bf16[256,1280]{1,0:T(8,128)(2,1)S(1)} %collective-permute-done.got_a_ref, ...), custom_call_target="tpu_custom_call" | custom-call | flops 1000000000 | bytes 4000000 | tf_op jit(solution)/shard_map/last/pallas_call | solution.py:303
  (25 shorter events, 0.1 us)
Async XLA Ops:
  0.0 1.3 %copy-start = (bf16[512,1280]{1,0:T(8,128)(2,1)S(1)}, bf16[512,1280]{1,0:T(8,128)(2,1)}, u32[]{:S(2)}) copy-start(bf16[512,1280]{1,0:T(8,128)(2,1)} %stream_ref.3) | copy-start | bytes 3932164
  1.3 0.9 copy-start.3
  2.2 0.8 copy-start.6
  3.0 0.7 copy-start.7
  3.7 0.7 copy-start.8
  4.3 0.7 copy-start.10
  6.4 0.8 copy-start.12
  7.2 1.1 %copy-start.14 = (bf16[512,1280]{1,0:T(8,128)(2,1)}, bf16[512,1280]{1,0:T(8,128)(2,1)S(1)}, u32[]{:S(2)}) copy-start(bf16[512,1280]{1,0:T(8,128)(2,1)S(1)} %get-tuple-element.22.scaled_ref) | copy-start | bytes 3932164
  34.0 7.7 %copy-start.16 = (f32[1280]{0:T(1024)S(1)}, f32[1280]{0:T(1024)}, u32[]{:S(2)}) copy-start(f32[1280]{0:T(1024)} %param.19) | copy-start | bytes 15364
  34.0 7.8 %copy-start.1 = (bf16[512,1280]{1,0:T(8,128)(2,1)S(1)}, bf16[512,1280]{1,0:T(8,128)(2,1)}, u32[]{:S(2)}) copy-start(bf16[512,1280]{1,0:T(8,128)(2,1)} %stream_ref.3) | copy-start | bytes 3932164
  34.0 7.8 %copy-start.2 = (bf16[512,1280]{1,0:T(8,128)(2,1)S(1)}, bf16[512,1280]{1,0:T(8,128)(2,1)}, u32[]{:S(2)}) copy-start(bf16[512,1280]{1,0:T(8,128)(2,1)} %gate_ref.1) | copy-start | bytes 3932164
  34.0 7.8 %copy-start.4 = (bf16[512,128]{1,0:T(8,128)(2,1)S(1)}, bf16[512,128]{1,0:T(8,128)(2,1)}, u32[]{:S(2)}) copy-start(bf16[512,128]{1,0:T(8,128)(2,1)} %in_ref.3) | copy-start | bytes 393220
  34.0 7.8 %copy-start.5 = (bf16[512,128]{1,0:T(8,128)(2,1)S(1)}, bf16[512,128]{1,0:T(8,128)(2,1)}, u32[]{:S(2)}) copy-start(bf16[512,128]{1,0:T(8,128)(2,1)} %out_ref.3) | copy-start | bytes 393220
  34.0 7.8 %copy-start.9 = (f32[20]{0:T(128)S(1)}, f32[20]{0:T(128)}, u32[]{:S(2)}) copy-start(f32[20]{0:T(128)} %param.18) | copy-start | bytes 244
  34.0 7.8 %copy-start.11 = (s32[128]{0:T(128)S(1)}, s32[128]{0:T(128)}, u32[]{:S(2)}) copy-start(s32[128]{0:T(128)} %param.21) | copy-start | bytes 1540
  35.5 19.5 %all-to-all-start.1 = ((bf16[64,2,1280]{2,1,0:T(2,128)(2,1)}), bf16[64,2,1280]{2,1,0:T(2,128)(2,1)S(1)}, u32[]{:S(2)}, u32[]{:S(2)}) async-start(bf16[64,2,1280]{2,1,0:T(2,128)(2,1)} %scan.1), calls=%async_computation.1 | async-start | bytes 655360 | tf_op jit(solution)/shard_map/all_to_all | solution.py:370
  41.9 1.3 %copy-start.15 = (bf16[512,1280]{1,0:T(8,128)(2,1)S(1)}, bf16[512,1280]{1,0:T(8,128)(2,1)}, u32[]{:S(2)}) copy-start(bf16[512,1280]{1,0:T(8,128)(2,1)} %copy-done.14) | copy-start | bytes 3932164
  55.1 1.1 %copy-start.13 = (f32[128,1280]{1,0:T(8,128)S(1)}, f32[128,1280]{1,0:T(8,128)}, u32[]{:S(2)}) copy-start(f32[128,1280]{1,0:T(8,128)} %copy-done.12) | copy-start | bytes 1966084
  63.4 16.8 %collective-permute-start = (bf16[256,1280]{1,0:T(8,128)(2,1)S(1)}, bf16[256,1280]{1,0:T(8,128)(2,1)S(1)}, u32[]{:S(2)}, u32[]{:S(2)}) collective-permute-start(bf16[256,1280]{1,0:T(8,128)(2,1)S(1)} %get-tuple-element.29), channel_id=1, source_target_pairs={{0,1},{1,0},{2,3},{3,2},{4,5},{5,4},{6,7},{7,6},{8,9},{9,8},{10,11... | collective-permute-start | bytes 1966088 | tf_op jit(solution)/shard_map/ppermute | solution.py:391
  64.0 17.1 %collective-permute-start.1 = (bf16[256,1280]{1,0:T(8,128)(2,1)S(1)}, bf16[256,1280]{1,0:T(8,128)(2,1)S(1)}, u32[]{:S(2)}, u32[]{:S(2)}) collective-permute-start(bf16[256,1280]{1,0:T(8,128)(2,1)S(1)} %get-tuple-element.30), channel_id=1, source_target_pairs={{0,3},{1,2},{2,1},{3,0},{4,7},{5,6},{6,5},{7,4},{8,11},{9,10},{10,... | collective-permute-start | bytes 1966088 | tf_op jit(solution)/shard_map/ppermute | solution.py:392
  81.3 11.8 %collective-permute-start.2 = (bf16[128,1280]{1,0:T(8,128)(2,1)S(1)}, bf16[128,1280]{1,0:T(8,128)(2,1)S(1)}, u32[]{:S(2)}, u32[]{:S(2)}) collective-permute-start(bf16[128,1280]{1,0:T(8,128)(2,1)S(1)} %get-tuple-element.31), channel_id=1, source_target_pairs={{0,3},{1,2},{2,1},{3,0},{4,7},{5,6},{6,5},{7,4},{8,11},{9,10},{10,... | collective-permute-start | bytes 983048 | tf_op jit(solution)/shard_map/ppermute | solution.py:409
  83.1 10.0 %collective-permute-start.3 = (bf16[128,1280]{1,0:T(8,128)(2,1)S(1)}, bf16[128,1280]{1,0:T(8,128)(2,1)S(1)}, u32[]{:S(2)}, u32[]{:S(2)}) collective-permute-start(bf16[128,1280]{1,0:T(8,128)(2,1)S(1)} %get-tuple-element.32), channel_id=1, source_target_pairs={{0,1},{1,0},{2,3},{3,2},{4,5},{5,4},{6,7},{7,6},{8,9},{9,8},{10,11... | collective-permute-start | bytes 983048 | tf_op jit(solution)/shard_map/ppermute | solution.py:410

commit v2 on v1

--- a/solution.py
+++ b/solution.py
@@ -16,9 +16,11 @@
 BF16 = jnp.bfloat16
 PAD = 32
 LANES = 128
+FULL = 67_043_328 / 1024**2
 
 VMEM_SPEC = pl.BlockSpec(memory_space=pltpu.VMEM)
 SMEM_SPEC = pl.BlockSpec(memory_space=pltpu.SMEM)
+HBM_SPEC = pl.BlockSpec(memory_space=pltpu.HBM)
 
 
 def dot(a, b):
@@ -77,17 +79,40 @@
 def state_kernel(
     head_size,
     offset_ref,
+    y_ref,
+    stream_hbm,
+    in_hbm,
+    step_hbm,
+    bias_hbm,
+    rate_hbm,
+    starts_hbm,
+    summary_ref,
+    into_ref,
+    factor_ref,
     stream_ref,
     in_ref,
     step_ref,
     bias_ref,
     rate_ref,
     starts_ref,
-    summary_ref,
-    scaled_ref,
-    first_ref,
-    factor_ref,
+    arrived,
 ):
+    pairs = (
+        (step_hbm, step_ref),
+        (bias_hbm, bias_ref),
+        (rate_hbm, rate_ref),
+        (starts_hbm, starts_ref),
+        (in_hbm, in_ref),
+        (stream_hbm, stream_ref),
+    )
+    copies = [
+        pltpu.make_async_copy(source, target, arrived.at[number])
+        for number, (source, target) in enumerate(pairs)
+    ]
+    for copy in copies:
+        copy.start()
+    for copy in copies[:4]:
+        copy.wait()
     heads, rows = step_ref.shape
     width = stream_ref.shape[1]
     offset = offset_ref[0]
@@ -128,21 +153,25 @@
     wide_in = jnp.concatenate([jnp.concatenate(into + [constants], axis=1), nothing], axis=0)
     wide_out = jnp.concatenate([jnp.concatenate(out_of + [constants], axis=1), nothing], axis=0)
     factor_ref[...] = two_parts(wide_out)
-    per_lane = dot_first(two_parts(wide_in), spread)
+    into_parts = two_parts(wide_in)
+    into_ref[...] = into_parts
+    per_lane = dot_first(into_parts, spread)
     constant_rows = per_lane[rows : rows + 8, :]
+    for copy in copies[4:]:
+        copy.wait()
     states = []
     for block in range(rows // BLOCK):
         cut = slice(block * BLOCK, (block + 1) * BLOCK)
         scaled = (stream_ref[cut, :].astype(F32) * per_lane[cut, :]).astype(BF16)
-        scaled_ref[cut, :] = scaled
         to_end = jnp.where(docs[cut, :] == ends[block], in_ref[cut, :].astype(F32), 0.0)
         states.append(constant_rows[block : block + 1, :] * dot_first(to_end.astype(BF16), scaled))
-    first_ref[...] = states[0]
     summary = constant_rows[3:4, :] * states[0] + states[1]
     high = link.astype(BF16).astype(F32)
     link_row = as_row(high, LANES) + pltpu.roll(as_row(link - high, LANES), PAD, 1)
-    summary_ref[:, :width] = summary.astype(BF16)
-    summary_ref[:, width:] = jnp.broadcast_to(link_row, (summary.shape[0], LANES)).astype(BF16)
+    whole = jnp.concatenate(
+        [summary, jnp.broadcast_to(link_row, (summary.shape[0], LANES))], axis=1
+    ).astype(BF16)
+    summary_ref[...] = whole.reshape(summary_ref.shape)
 
 
 def within_kernel(
@@ -152,12 +181,13 @@
     gate_ref,
     in_ref,
     out_ref,
-    scaled_ref,
+    into_ref,
     factor_ref,
     skip_ref,
     starts_ref,
     base_ref,
     slope_ref,
+    first_ref,
 ):
     rows, width = stream_ref.shape
     heads = skip_ref.shape[1]
@@ -172,13 +202,20 @@
     skip_row = dot_first(two_parts(jnp.broadcast_to(skip, (PAD, LANES))), spread)[:1, :]
     i = lax.broadcasted_iota(jnp.int32, (BLOCK, BLOCK), 0)
     j = lax.broadcasted_iota(jnp.int32, (BLOCK, BLOCK), 1)
+    constant_rows = dot_first(into_ref[:, rows:], spread)[:8, :]
     for block in range(rows // BLOCK):
         cut = slice(block * BLOCK, (block + 1) * BLOCK)
+        scaled = stream_ref[cut, :].astype(F32) * dot_first(into_ref[:, cut], spread)
+        scaled = scaled.astype(BF16)
+        if block == 0:
+            end = docs[BLOCK - 1 : BLOCK, :]
+            to_end = jnp.where(docs[cut, :] == end, in_ref[cut, :].astype(F32), 0.0)
+            first_ref[...] = constant_rows[:1, :] * dot_first(to_end.astype(BF16), scaled)
         scores = dot_last(out_ref[cut, :], in_ref[cut, :])
         live = (i >= j) & (docs[cut, :] == docs_across[:, cut])
         weights = jnp.where(live, scores, 0.0).astype(BF16)
         per_lane = dot_first(factor_ref[:, cut], spread)
-        within = dot(weights, scaled_ref[cut, :])
+        within = dot(weights, scaled)
         value = per_lane * within + skip_row * stream_ref[cut, :].astype(F32)
         gate = gate_ref[cut, :].astype(F32)
         gate = gate / (1.0 + jnp.exp(-gate))
@@ -204,10 +241,25 @@
         state = per_lane[shard : shard + 1, :] * state + pieces_ref[shard, :, :width].astype(F32)
 
 
+def with_squares(piece, squares):
+    width = piece.shape[1]
+    high = squares.astype(BF16).astype(F32)
+    row = jnp.concatenate(
+        [high, squares - high, jnp.zeros((1, width - 2 * squares.shape[1]), F32)], axis=1
+    )
+    return jnp.concatenate(
+        [piece.astype(BF16), jnp.broadcast_to(row, (8, width)).astype(BF16)], axis=0
+    )
+
+
+def squares_of(got_ref, step):
+    row = got_ref[step:, :].astype(F32)[:1, :]
+    return row[:, :step] + row[:, step : 2 * step]
+
+
 def finish_kernel(
     head_size,
     offset_ref,
-    blocks_ref,
     out_ref,
     before_ref,
     first_ref,
@@ -216,11 +268,8 @@
     slope_ref,
     gain_ref,
     starts_ref,
-    proj_ref,
     hidden_ref,
     squares_ref,
-    send_a_ref,
-    send_b_ref,
 ):
     rows, width = base_ref.shape
     offset = offset_ref[0]
@@ -229,9 +278,9 @@
     before = jnp.max(docs_column(starts, offset - 1, 8)[:1, :], axis=0, keepdims=True)
     spread = head_lanes(width, head_size)
     constant_rows = dot_first(factor_ref[:, rows:], spread)[:8, :]
-    state = before_ref[...].astype(F32)
-    gain = gain_ref[...]
-    sums = []
+    state = before_ref[...].reshape(-1, width).astype(F32)
+    gain = gain_ref[...].reshape(1, width)
+    step = rows // 4
     for block in range(rows // BLOCK):
         cut = slice(block * BLOCK, (block + 1) * BLOCK)
         joined = jnp.where(docs[cut, :] == before, out_ref[cut, :].astype(F32), 0.0).astype(BF16)
@@ -241,73 +290,95 @@
         total = square[:, :LANES]
         for lane in range(LANES, width, LANES):
             total = total + square[:, lane : lane + LANES]
-        sums.append(total)
+        for part in range(BLOCK // step):
+            piece = total[part * step : (part + 1) * step, :]
+            number = block * (BLOCK // step) + part
+            squares_ref[number : number + 1, :] = jnp.sum(
+                jnp.transpose(piece), axis=0, keepdims=True
+            )
         hidden_ref[cut, :] = (gated * gain).astype(BF16)
         state = constant_rows[2:3, :] * state + first_ref[...]
         before = docs[(block + 1) * BLOCK - 1 : (block + 1) * BLOCK, :]
-    flat = jnp.concatenate([jnp.sum(jnp.transpose(s), axis=0, keepdims=True) for s in sums], axis=1)
-    squares_ref[...] = flat
-    step = rows // 4
-    half = proj_ref.shape[1] // 2
-    for number, (send_ref, low) in enumerate(((send_a_ref, 0), (send_b_ref, half))):
-        for part in range(2):
-            block = blocks_ref[2 * number + part]
-            piece = hidden_ref[pl.ds(block * step, step), :]
-            send_ref[part * step : (part + 1) * step, :] = dot(
-                piece, proj_ref[:, low : low + half]
-            ).astype(BF16)
-
-
-def keep_kernel(blocks_ref, hidden_ref, proj_ref, keep_a_ref, keep_b_ref):
+
+
+def far_kernel(y_ref, hidden_ref, proj_ref, squares_ref, send_a_ref, send_b_ref):
     step = hidden_ref.shape[0] // 4
     half = proj_ref.shape[1] // 2
-    for number, (keep_ref, low) in enumerate(((keep_a_ref, 0), (keep_b_ref, half))):
-        for part in range(2):
-            block = blocks_ref[4 + 2 * number + part]
-            piece = hidden_ref[pl.ds(block * step, step), :]
-            keep_ref[part * step : (part + 1) * step, :] = dot(
-                piece, proj_ref[:, low : low + half]
-            ).astype(BF16)
-
-
-def middle_kernel(keep_a_ref, keep_b_ref, got_a_ref, got_b_ref, send_a_ref, send_b_ref):
-    step = send_a_ref.shape[0]
-    for keep_ref, got_ref, send_ref in (
-        (keep_a_ref, got_a_ref, send_a_ref),
-        (keep_b_ref, got_b_ref, send_b_ref),
-    ):
-        send_ref[...] = (
-            keep_ref[step:, :].astype(F32) + got_ref[step:, :].astype(F32)
-        ).astype(BF16)
+    far = y_ref[0] ^ 2
+    piece = hidden_ref[pl.ds(far * step, step), :]
+    send_a_ref[...] = with_squares(
+        dot(piece, proj_ref[:, :half]), squares_ref[pl.ds(far, 1), :]
+    )
+    send_b_ref[...] = dot(piece, proj_ref[:, half:]).astype(BF16)
+
+
+def near_kernel(y_ref, hidden_ref, proj_ref, squares_ref, send_a_ref, send_b_ref):
+    step = hidden_ref.shape[0] // 4
+    half = proj_ref.shape[1] // 2
+    one, three = y_ref[0] ^ 1, y_ref[0] ^ 3
+    send_a_ref[...] = with_squares(
+        dot(hidden_ref[pl.ds(one * step, step), :], proj_ref[:, :half]),
+        squares_ref[pl.ds(one, 1), :],
+    )
+    send_b_ref[...] = dot(
+        hidden_ref[pl.ds(three * step, step), :], proj_ref[:, half:]
+    ).astype(BF16)
+
+
+def keep_kernel(y_ref, hidden_ref, proj_ref, own_ref, via_a_ref, via_b_ref):
+    step = hidden_ref.shape[0] // 4
+    half = proj_ref.shape[1] // 2
+    one, three = y_ref[0] ^ 1, y_ref[0] ^ 3
+    via_a_ref[...] = dot(hidden_ref[pl.ds(three * step, step), :], proj_ref[:, :half])
+    via_b_ref[...] = dot(hidden_ref[pl.ds(one * step, step), :], proj_ref[:, half:])
+    own_ref[...] = dot(hidden_ref[pl.ds(y_ref[0] * step, step), :], proj_ref[...])
+
+
+def middle_kernel(
+    y_ref, squares_ref, via_a_ref, via_b_ref, got_a_ref, got_b_ref, send_a_ref, send_b_ref
+):
+    step = via_a_ref.shape[0]
+    squares = squares_ref[pl.ds(y_ref[0] ^ 3, 1), :] + squares_of(got_a_ref, step)
+    send_a_ref[...] = with_squares(via_a_ref[...] + got_a_ref[:step, :].astype(F32), squares)
+    send_b_ref[...] = (via_b_ref[...] + got_b_ref[...].astype(F32)).astype(BF16)
 
 
 def last_kernel(
-    channels, squares_ref, keep_a_ref, keep_b_ref, got_a_ref, got_b_ref, far_a_ref, far_b_ref, out_ref
+    channels,
+    y_ref,
+    squares_ref,
+    own_ref,
+    near_a_ref,
+    near_b_ref,
+    far_a_ref,
+    far_b_ref,
+    out_ref,
 ):
-    step = far_a_ref.shape[0]
-    half = far_a_ref.shape[1]
-    mean = jnp.sum(squares_ref[...], axis=(0, 1))[None, :] / channels
-    scale = as_column(lax.rsqrt(mean + EPSILON), step)
-    for keep_ref, got_ref, far_ref, low in (
-        (keep_a_ref, got_a_ref, far_a_ref, 0),
-        (keep_b_ref, got_b_ref, far_b_ref, half),
-    ):
+    step, model = own_ref.shape
+    half = model // 2
+    squares = squares_ref[pl.ds(y_ref[0], 1), :]
+    squares = squares + squares_of(near_a_ref, step) + squares_of(far_a_ref, step)
+    scale = as_column(lax.rsqrt(squares / channels + EPSILON), step)
+    for near_ref, far_ref, low in ((near_a_ref, far_a_ref, 0), (near_b_ref, far_b_ref, half)):
         total = (
-            keep_ref[:step, :].astype(F32) + got_ref[:step, :].astype(F32) + far_ref[...].astype(F32)
+            own_ref[:, low : low + half]
+            + near_ref[:step, :].astype(F32)
+            + far_ref[:step, :].astype(F32)
         )
         out_ref[:, low : low + half] = (total * scale).astype(BF16)
 
 
-def call(kernel, out_shape, scalars, arrays, flops, name):
+def call(kernel, out_shape, scalars, arrays, flops, limit, scratch=()):
     single = not isinstance(out_shape, (tuple, list))
+    space = HBM_SPEC if scratch else VMEM_SPEC
     return pl.pallas_call(
         kernel,
         out_shape=out_shape,
-        in_specs=[SMEM_SPEC] * len(scalars) + [VMEM_SPEC] * len(arrays),
+        in_specs=[SMEM_SPEC] * len(scalars) + [space] * len(arrays),
         out_specs=VMEM_SPEC if single else [VMEM_SPEC] * len(out_shape),
+        scratch_shapes=scratch,
         cost_estimate=pl.CostEstimate(flops=flops, bytes_accessed=4_000_000, transcendentals=0),
-        compiler_params=pltpu.CompilerParams(vmem_limit_bytes=48 * 1024 * 1024),
-        name=name,
+        compiler_params=pltpu.CompilerParams(vmem_limit_bytes=int(limit * 1024**2)),
     )(*scalars, *arrays)
 
 
@@ -331,90 +402,103 @@
     states = in_coeff.shape[1]
     model = out_proj.shape[1]
     shards = lax.axis_size(SEQ)
-    y = lax.axis_index("head")
+    y = lax.axis_index("head").astype(jnp.int32)[None]
     offset = (lax.axis_index(SEQ) * rows).astype(jnp.int32)[None]
     starts = doc_starts[None, :]
     shape = jax.ShapeDtypeStruct
-    summary, scaled, first, factor = call(
+    arrays = [stream, in_coeff, step_raw, step_bias[None], decay_rate[None], starts]
+    summary, into, factor = call(
         functools.partial(state_kernel, head_size),
         [
-            shape((states, width + LANES), BF16),
-            shape((rows, width), BF16),
-            shape((states, width), F32),
+            shape((shards, states // shards, width + LANES), BF16),
+            shape((2 * PAD, rows + LANES), BF16),
             shape((2 * PAD, rows + LANES), BF16),
         ],
+        [offset, y],
+        arrays,
+        2_000_000_000,
+        FULL,
+        [pltpu.VMEM(a.shape, a.dtype) for a in arrays] + [pltpu.SemaphoreType.DMA((len(arrays),))],
+    )
+    pieces = lax.all_to_all(summary, SEQ, 0, 0, tiled=True)
+    base, slope, first = call(
+        functools.partial(within_kernel, head_size),
+        [
+            shape((rows, width), F32),
+            shape((rows, width), F32),
+            shape((states, width), F32),
+        ],
         [offset],
-        [stream, in_coeff, step_raw, step_bias[None], decay_rate[None], starts],
-        2_000_000_000,
-        "state",
-    )
-    pieces = lax.all_to_all(
-        summary.reshape(shards, states // shards, width + LANES), SEQ, 0, 0, tiled=True
-    )
-    base, slope = call(
-        functools.partial(within_kernel, head_size),
-        [shape((rows, width), F32), shape((rows, width), F32)],
-        [offset],
-        [stream, gate_input, in_coeff, out_coeff, scaled, factor, skip_scale[None], starts],
+        [stream, gate_input, in_coeff, out_coeff, into, factor, skip_scale[None], starts],
         4_000_000_000,
-        "within",
+        FULL,
     )
     prior = call(
         functools.partial(scan_kernel, head_size),
         shape((shards, states // shards, width), BF16),
         [],
         [pieces],
-        1_000_000_000,
-        "scan",
-    )
-    incoming = lax.all_to_all(prior, SEQ, 0, 0, tiled=True).reshape(states, width)
-    one, two, three = y ^ 1, y ^ 2, y ^ 3
-    blocks = jnp.stack([one, two, three, two, y, three, y, one]).astype(jnp.int32)
+        10_000_000_000,
+        8,
+    )
+    incoming = lax.all_to_all(prior, SEQ, 0, 0, tiled=True)
     step = rows // 4
     half = model // 2
-    hidden, squares, send_a, send_b = call(
+    hidden, squares = call(
         functools.partial(finish_kernel, head_size),
-        [
-            shape((rows, width), BF16),
-            shape((1, rows), F32),
-            shape((2 * step, half), BF16),
-            shape((2 * step, half), BF16),
-        ],
-        [offset, blocks],
-        [out_coeff, incoming, first, factor, base, slope, norm_gain[None], starts, out_proj],
+        [shape((rows, width), BF16), shape((4, step), F32)],
+        [offset],
+        [out_coeff, incoming, first, factor, base, slope, norm_gain, starts],
         4_000_000_000,
-        "finish",
+        22,
+    )
+    send_a, send_b = call(
+        far_kernel,
+        [shape((step + 8, half), BF16), shape((step, half), BF16)],
+        [y],
+        [hidden, out_proj, squares],
+        1_000_000_000,
+        16,
     )
     pair_1 = [(i, i ^ 1) for i in range(4)]
     pair_3 = [(i, i ^ 3) for i in range(4)]
-    all_squares = lax.all_to_all(squares.reshape(4, 1, step), "head", 0, 0, tiled=True)
     got_a = lax.ppermute(send_a, "head", pair_1)
     got_b = lax.ppermute(send_b, "head", pair_3)
-    keep_a, keep_b = call(
+    send_a, send_b = call(
+        near_kernel,
+        [shape((step + 8, half), BF16), shape((step, half), BF16)],
+        [y],
+        [hidden, out_proj, squares],
+        1_000_000_000,
+        16,
+    )
+    near_a = lax.ppermute(send_a, "head", pair_1)
+    near_b = lax.ppermute(send_b, "head", pair_3)
+    own, via_a, via_b = call(
         keep_kernel,
-        [shape((2 * step, half), BF16), shape((2 * step, half), BF16)],
-        [blocks],
+        [shape((step, model), F32), shape((step, half), F32), shape((step, half), F32)],
+        [y],
         [hidden, out_proj],
         2_000_000_000,
-        "keep",
-    )
-    more_a, more_b = call(
+        16,
+    )
+    send_a, send_b = call(
         middle_kernel,
-        [shape((step, half), BF16), shape((step, half), BF16)],
-        [],
-        [keep_a, keep_b, got_a, got_b],
+        [shape((step + 8, half), BF16), shape((step, half), BF16)],
+        [y],
+        [squares, via_a, via_b, got_a, got_b],
         1_000_000_000,
-        "middle",
-    )
-    far_a = lax.ppermute(more_a, "head", pair_3)
-    far_b = lax.ppermute(more_b, "head", pair_1)
+        8,
+    )
+    far_a = lax.ppermute(send_a, "head", pair_3)
+    far_b = lax.ppermute(send_b, "head", pair_1)
     return call(
         functools.partial(last_kernel, total_channels),
         shape((step, model), BF16),
-        [],
-        [all_squares, keep_a, keep_b, got_a, got_b, far_a, far_b],
+        [y],
+        [squares, own, near_a, near_b, far_a, far_b],
         1_000_000_000,
-        "last",
+        8,
     )
 
 

time: 95.9 us -> 93.2 us (0.972)
  the two profiles are of different devices: /device:TPU:8 before, /device:TPU:6 now
where the time goes in v2:
time: 93.2 us; the launch traced here: 92.7 us
  blocking collectives  25.7 us (28%)
  waiting for transfers between devices  25 us (27%)
  Pallas kernels  19 us (20%)
  starting transfers between devices  14.9 us (16%)
  local copies, waits for them, and re-layouts  8.12 us (9%)
    all_to_all x1, blocking collectives, local(): pieces = lax.all_to_all(summary, SEQ, 0, 0, tiled=True)  25.7 us
    pallas_call x9, Pallas kernels, call(): pl.pallas_call(kernel, out_shape=out_shape, in_specs=[SMEM_SPEC] * len(sc...  19 us
    ppermute x1, waiting for transfers between devices, local(): near_b = lax.ppermute(send_b, 'head', pair_3)  14.1 us
    unnamed x18, local copies, waits for them, and re-layouts  8.12 us
    all_to_all x1, starting transfers between devices, local(): incoming = lax.all_to_all(prior, SEQ, 0, 0, tiled=True)  6.76 us
    all_to_all x1, waiting for transfers between devices, local(): incoming = lax.all_to_all(prior, SEQ, 0, 0, tiled=True)  6.12 us
    ppermute x1, waiting for transfers between devices, local(): got_b = lax.ppermute(send_b, 'head', pair_3)  4.74 us
    ppermute x1, starting transfers between devices, local(): far_a = lax.ppermute(send_a, 'head', pair_3)  2.27 us
  transfers between devices with their start and end apart: 7, of which 3 were waited for; matrix products, arithmetic and copies ran while one was open for 0% of the time, Pallas kernels for 10%

profile of v2, /device:TPU:6, one launch (start us, length us, event | category | flops | bytes accessed | tf_op | source)
XLA Modules:
  0.0 92.7 jit_solution(6591867845150267850)
XLA Ops:
  0.0 3.3 %shard_map.109 = (bf16[64,2,1408]{2,1,0:T(2,128)(2,1)}, bf16[64,640]{1,0:T(8,128)(2,1)}, bf16[64,640]{1,0:T(8,128)(2,1)}) custom-call(s32[1]{0:T(128)} %bitcast.1.offset_ref, s32[1]{0:T(128)} %bitcast.y_ref, bf16[512,1280]{1,0:T(8,128)(2,1)} %stream_ref.1, bf16[512,128]{1,0:T(8,128)(2,1)} %in_ref.1, f32[20,512]{1,0:T(8,128)} %step_hbm.1, f32[1,20]{1,0:T(1,128)} %bitcast.11, ...), custom_call_target="tpu_custom_call" | custom-call | flops 2000000000 | bytes 4000000 | tf_op jit(solution)/shard_map/pallas_call | solution.py:374
  3.3 25.7 %all_to_all.10.pieces_ref = bf16[64,2,1408]{2,1,0:T(2,128)(2,1)S(1)} all-to-all(bf16[64,2,1408]{2,1,0:T(2,128)(2,1)} %get-tuple-element.22), channel_id=1, replica_groups=mesh['seq_0'=4,'seq_1'=8,'seq_2'=2,'head'=4] {'seq_0','seq_1','seq_2'}, dimensions={0} | all-to-all | bytes 720896 | tf_op jit(solution)/shard_map/all_to_all | solution.py:423
  29.0 1.4 %shard_map.110 = bf16[64,2,1280]{2,1,0:T(2,128)(2,1)} custom-call(bf16[64,2,1408]{2,1,0:T(2,128)(2,1)S(1)} %all_to_all.10.pieces_ref), custom_call_target="tpu_custom_call" | custom-call | flops 10000000000 | bytes 4000000 | tf_op jit(solution)/shard_map/pallas_call | solution.py:374
  30.4 6.8 %all-to-all-start.1 = ((bf16[64,2,1280]{2,1,0:T(2,128)(2,1)}), bf16[64,2,1280]{2,1,0:T(2,128)(2,1)}, u32[]{:S(2)}, u32[]{:S(2)}) async-start(bf16[64,2,1280]{2,1,0:T(2,128)(2,1)} %shard_map.110), calls=%async_computation.1 | async-start | bytes 655360 | tf_op jit(solution)/shard_map/all_to_all | solution.py:444
  37.2 6.7 %shard_map.111 = (f32[512,1280]{1,0:T(8,128)}, f32[512,1280]{1,0:T(8,128)}, f32[128,1280]{1,0:T(8,128)}) custom-call(s32[1]{0:T(128)} %bitcast.1.offset_ref, bf16[512,1280]{1,0:T(8,128)(2,1)} %stream_ref.1, bf16[512,1280]{1,0:T(8,128)(2,1)} %gate_ref.1, bf16[512,128]{1,0:T(8,128)(2,1)} %in_ref.1, bf16[512,128]{1,0:T(8,128)(2,1)} %out_ref.3, ...), custom_call_target="tpu_custom_call" | custom-call | flops 4000000000 | bytes 4000000 | tf_op jit(solution)/shard_map/pallas_call | solution.py:374
  43.9 6.1 %all-to-all-done.1.before_ref = bf16[64,2,1280]{2,1,0:T(2,128)(2,1)} async-done(((bf16[64,2,1280]{2,1,0:T(2,128)(2,1)}), bf16[64,2,1280]{2,1,0:T(2,128)(2,1)}, u32[]{:S(2)}, u32[]{:S(2)}) %all-to-all-start.1) | async-done | bytes 327712 | tf_op jit(solution)/shard_map/all_to_all | solution.py:444
  50.0 1.1 %copy-done = bf16[512,128]{1,0:T(8,128)(2,1)S(1)} copy-done((bf16[512,128]{1,0:T(8,128)(2,1)S(1)}, bf16[512,128]{1,0:T(8,128)(2,1)}, u32[]{:S(2)}) %copy-start) | copy-done | bytes 131096
  51.0 1.0 %copy-done.1 = f32[1280]{0:T(1024)S(1)} copy-done((f32[1280]{0:T(1024)S(1)}, f32[1280]{0:T(1024)}, u32[]{:S(2)}) %copy-start.1) | copy-done | bytes 5144
  52.0 0.7 copy-done.2
  52.6 1.7 %copy-done.3 = f32[512,1280]{1,0:T(8,128)S(1)} copy-done((f32[512,1280]{1,0:T(8,128)S(1)}, f32[512,1280]{1,0:T(8,128)}, u32[]{:S(2)}) %copy-start.3) | copy-done | bytes 2621464
  54.4 1.7 %copy-done.4 = f32[512,1280]{1,0:T(8,128)S(1)} copy-done((f32[512,1280]{1,0:T(8,128)S(1)}, f32[512,1280]{1,0:T(8,128)}, u32[]{:S(2)}) %copy-start.4) | copy-done | bytes 2621464
  56.1 1.1 %copy-done.5 = f32[128,1280]{1,0:T(8,128)S(1)} copy-done((f32[128,1280]{1,0:T(8,128)S(1)}, f32[128,1280]{1,0:T(8,128)}, u32[]{:S(2)}) %copy-start.5) | copy-done | bytes 655384
  57.2 0.9 copy-done.6
  58.1 2.2 %shard_map.112 = (bf16[512,1280]{1,0:T(8,128)(2,1)S(1)}, f32[4,128]{1,0:T(4,128)S(1)}) custom-call(s32[1]{0:T(128)} %bitcast.1.offset_ref, bf16[512,128]{1,0:T(8,128)(2,1)S(1)} %copy-done, bf16[64,2,1280]{2,1,0:T(2,128)(2,1)} %all-to-all-done.1.before_ref, f32[128,1280]{1,0:T(8,128)S(1)} %copy-done.5, bf16[64,640]{1,0:T(8,128)(2,1)S(1)} %copy-done.6, ...), custom_call_target="tpu_custom_call" | custom-call | flops 4000000000 | bytes 4000000 | tf_op jit(solution)/shard_map/pallas_call | solution.py:374
  60.3 0.0 slice-done
  60.4 1.0 %shard_map.115 = (bf16[136,1280]{1,0:T(8,128)(2,1)S(1)}, bf16[128,1280]{1,0:T(8,128)(2,1)S(1)}) custom-call(s32[1]{0:T(128)} %bitcast.y_ref, bf16[512,1280]{1,0:T(8,128)(2,1)S(1)} %get-tuple-element.29.hidden_ref, bf16[1280,2560]{1,0:T(8,128)(2,1)S(1)} %bitcast.7, f32[4,128]{1,0:T(4,128)S(1)} %get-tuple-element.28.squares_ref), custom_call_target="tpu_custom_call" | custom-call | flops 1000000000 | bytes 4000000 | tf_op jit(solution)/shard_map/pallas_call | solution.py:374
  61.4 1.7 %collective-permute-start.2 = (bf16[136,1280]{1,0:T(8,128)(2,1)S(1)}, bf16[136,1280]{1,0:T(8,128)(2,1)S(1)}, u32[]{:S(2)}, u32[]{:S(2)}) collective-permute-start(bf16[136,1280]{1,0:T(8,128)(2,1)S(1)} %get-tuple-element.35), channel_id=1, source_target_pairs={{0,1},{1,0},{2,3},{3,2},{4,5},{5,4},{6,7},{7,6},{8,9},{9,8},{10,11... | collective-permute-start | bytes 1044488 | tf_op jit(solution)/shard_map/ppermute | solution.py:465
  63.1 2.2 %collective-permute-start.3 = (bf16[128,1280]{1,0:T(8,128)(2,1)S(1)}, bf16[128,1280]{1,0:T(8,128)(2,1)S(1)}, u32[]{:S(2)}, u32[]{:S(2)}) collective-permute-start(bf16[128,1280]{1,0:T(8,128)(2,1)S(1)} %get-tuple-element.36), channel_id=1, source_target_pairs={{0,3},{1,2},{2,1},{3,0},{4,7},{5,6},{6,5},{7,4},{8,11},{9,10},{10,... | collective-permute-start | bytes 983048 | tf_op jit(solution)/shard_map/ppermute | solution.py:466
  65.3 1.0 %shard_map.114 = (bf16[136,1280]{1,0:T(8,128)(2,1)S(1)}, bf16[128,1280]{1,0:T(8,128)(2,1)S(1)}) custom-call(s32[1]{0:T(128)} %bitcast.y_ref, bf16[512,1280]{1,0:T(8,128)(2,1)S(1)} %get-tuple-element.29.hidden_ref, bf16[1280,2560]{1,0:T(8,128)(2,1)S(1)} %bitcast.7, f32[4,128]{1,0:T(4,128)S(1)} %get-tuple-element.28.squares_ref), custom_call_target="tpu_custom_call" | custom-call | flops 1000000000 | bytes 4000000 | tf_op jit(solution)/shard_map/pallas_call | solution.py:374
  66.3 0.9 %collective-permute-start = (bf16[136,1280]{1,0:T(8,128)(2,1)S(1)}, bf16[136,1280]{1,0:T(8,128)(2,1)S(1)}, u32[]{:S(2)}, u32[]{:S(2)}) collective-permute-start(bf16[136,1280]{1,0:T(8,128)(2,1)S(1)} %get-tuple-element.31), channel_id=1, source_target_pairs={{0,1},{1,0},{2,3},{3,2},{4,5},{5,4},{6,7},{7,6},{8,9},{9,8},{10,11... | collective-permute-start | bytes 1044488 | tf_op jit(solution)/shard_map/ppermute | solution.py:475
  67.2 1.9 %shard_map.113 = (f32[128,2560]{1,0:T(8,128)S(1)}, f32[128,1280]{1,0:T(8,128)S(1)}, f32[128,1280]{1,0:T(8,128)S(1)}) custom-call(s32[1]{0:T(128)} %bitcast.y_ref, bf16[512,1280]{1,0:T(8,128)(2,1)S(1)} %get-tuple-element.29.hidden_ref, bf16[1280,2560]{1,0:T(8,128)(2,1)S(1)} %bitcast.7), custom_call_target="tpu_custom_call" | custom-call | flops 2000000000 | bytes 4000000 | tf_op jit(solution)/shard_map/pallas_call | solution.py:374
  69.1 4.7 %collective-permute-done.3.got_b_ref = bf16[128,1280]{1,0:T(8,128)(2,1)S(1)} collective-permute-done((bf16[128,1280]{1,0:T(8,128)(2,1)S(1)}, bf16[128,1280]{1,0:T(8,128)(2,1)S(1)}, u32[]{:S(2)}, u32[]{:S(2)}) %collective-permute-start.3) | collective-permute-done | bytes 327712 | tf_op jit(solution)/shard_map/ppermute | solution.py:466
  73.8 0.0 collective-permute-done.2.got_a_ref
  73.8 0.1 shard_map.116
  74.0 2.3 %collective-permute-start.4 = (bf16[136,1280]{1,0:T(8,128)(2,1)S(1)}, bf16[136,1280]{1,0:T(8,128)(2,1)S(1)}, u32[]{:S(2)}, u32[]{:S(2)}) collective-permute-start(bf16[136,1280]{1,0:T(8,128)(2,1)S(1)} %get-tuple-element.37), channel_id=1, source_target_pairs={{0,3},{1,2},{2,1},{3,0},{4,7},{5,6},{6,5},{7,4},{8,11},{9,10},{10,... | collective-permute-start | bytes 1044488 | tf_op jit(solution)/shard_map/ppermute | solution.py:493
  76.2 1.1 %collective-permute-start.1 = (bf16[128,1280]{1,0:T(8,128)(2,1)S(1)}, bf16[128,1280]{1,0:T(8,128)(2,1)S(1)}, u32[]{:S(2)}, u32[]{:S(2)}) collective-permute-start(bf16[128,1280]{1,0:T(8,128)(2,1)S(1)} %get-tuple-element.32), channel_id=1, source_target_pairs={{0,3},{1,2},{2,1},{3,0},{4,7},{5,6},{6,5},{7,4},{8,11},{9,10},{10,... | collective-permute-start | bytes 983048 | tf_op jit(solution)/shard_map/ppermute | solution.py:476
  77.3 0.0 collective-permute-start.5
  77.3 14.1 %collective-permute-done.1.near_b_ref = bf16[128,1280]{1,0:T(8,128)(2,1)S(1)} collective-permute-done((bf16[128,1280]{1,0:T(8,128)(2,1)S(1)}, bf16[128,1280]{1,0:T(8,128)(2,1)S(1)}, u32[]{:S(2)}, u32[]{:S(2)}) %collective-permute-start.1) | collective-permute-done | bytes 327712 | tf_op jit(solution)/shard_map/ppermute | solution.py:476
  91.4 0.0 collective-permute-done.near_a_ref
  91.4 0.0 collective-permute-done.5.far_b_ref
  91.4 0.0 collective-permute-done.4.far_a_ref
  91.4 1.3 %shard_map.117 = bf16[128,2560]{1,0:T(8,128)(2,1)} custom-call(s32[1]{0:T(128)} %bitcast.y_ref, f32[4,128]{1,0:T(4,128)S(1)} %get-tuple-element.28.squares_ref, f32[128,2560]{1,0:T(8,128)S(1)} %get-tuple-element.30.own_ref, bf16[136,1280]{1,0:T(8,128)(2,1)S(1)} %collective-permute-done.near_a_ref, bf16[128,1280]{1,0:T(8,128)(2,1)S(1)} %collective-permute-done.1.near_b_ref, ...), custom_call_target="tpu_custom_call" | custom-call | flops 1000000000 | bytes 4000000 | tf_op jit(solution)/shard_map/pallas_call | solution.py:374
  (11 shorter events, 0.0 us)
Async XLA Ops:
  30.4 19.6 %all-to-all-start.1 = ((bf16[64,2,1280]{2,1,0:T(2,128)(2,1)}), bf16[64,2,1280]{2,1,0:T(2,128)(2,1)}, u32[]{:S(2)}, u32[]{:S(2)}) async-start(bf16[64,2,1280]{2,1,0:T(2,128)(2,1)} %shard_map.110), calls=%async_computation.1 | async-start | bytes 655360 | tf_op jit(solution)/shard_map/all_to_all | solution.py:444
  50.0 10.4 %slice-start = ((s8[6553600]{0:T(1024)(128)(4,1)}), s8[4194304]{0:T(1024)(128)(4,1)S(1)}, s32[]{:S(2)}) async-start(s8[6553600]{0:T(1024)(128)(4,1)} %bitcast.6), calls=%async_computation.2 | async-start | bytes 8388608
  50.0 1.1 %copy-start = (bf16[512,128]{1,0:T(8,128)(2,1)S(1)}, bf16[512,128]{1,0:T(8,128)(2,1)}, u32[]{:S(2)}) copy-start(bf16[512,128]{1,0:T(8,128)(2,1)} %out_ref.3) | copy-start | bytes 393220
  51.0 1.0 %copy-start.1 = (f32[1280]{0:T(1024)S(1)}, f32[1280]{0:T(1024)}, u32[]{:S(2)}) copy-start(f32[1280]{0:T(1024)} %gain_ref.1) | copy-start | bytes 15364
  52.0 0.7 copy-start.2
  52.6 1.7 %copy-start.3 = (f32[512,1280]{1,0:T(8,128)S(1)}, f32[512,1280]{1,0:T(8,128)}, u32[]{:S(2)}) copy-start(f32[512,1280]{1,0:T(8,128)} %get-tuple-element.26.base_ref) | copy-start | bytes 7864324
  54.4 1.7 %copy-start.4 = (f32[512,1280]{1,0:T(8,128)S(1)}, f32[512,1280]{1,0:T(8,128)}, u32[]{:S(2)}) copy-start(f32[512,1280]{1,0:T(8,128)} %get-tuple-element.27.slope_ref) | copy-start | bytes 7864324
  56.1 1.1 %copy-start.5 = (f32[128,1280]{1,0:T(8,128)S(1)}, f32[128,1280]{1,0:T(8,128)}, u32[]{:S(2)}) copy-start(f32[128,1280]{1,0:T(8,128)} %get-tuple-element.25.first_ref) | copy-start | bytes 1966084
  57.2 0.9 copy-start.6
  58.1 2.3 %slice-start.1 = ((s8[6553600]{0:T(1024)(128)(4,1)}), s8[2359296]{0:T(1024)(128)(4,1)S(1)}, s32[]{:S(2)}) async-start(s8[6553600]{0:T(1024)(128)(4,1)} %bitcast.6), calls=%async_computation.3 | async-start | bytes 4718592
  61.4 12.4 %collective-permute-start.2 = (bf16[136,1280]{1,0:T(8,128)(2,1)S(1)}, bf16[136,1280]{1,0:T(8,128)(2,1)S(1)}, u32[]{:S(2)}, u32[]{:S(2)}) collective-permute-start(bf16[136,1280]{1,0:T(8,128)(2,1)S(1)} %get-tuple-element.35), channel_id=1, source_target_pairs={{0,1},{1,0},{2,3},{3,2},{4,5},{5,4},{6,7},{7,6},{8,9},{9,8},{10,11... | collective-permute-start | bytes 1044488 | tf_op jit(solution)/shard_map/ppermute | solution.py:465
  63.1 10.8 %collective-permute-start.3 = (bf16[128,1280]{1,0:T(8,128)(2,1)S(1)}, bf16[128,1280]{1,0:T(8,128)(2,1)S(1)}, u32[]{:S(2)}, u32[]{:S(2)}) collective-permute-start(bf16[128,1280]{1,0:T(8,128)(2,1)S(1)} %get-tuple-element.36), channel_id=1, source_target_pairs={{0,3},{1,2},{2,1},{3,0},{4,7},{5,6},{6,5},{7,4},{8,11},{9,10},{10,... | collective-permute-start | bytes 983048 | tf_op jit(solution)/shard_map/ppermute | solution.py:466
  66.3 25.2 %collective-permute-start = (bf16[136,1280]{1,0:T(8,128)(2,1)S(1)}, bf16[136,1280]{1,0:T(8,128)(2,1)S(1)}, u32[]{:S(2)}, u32[]{:S(2)}) collective-permute-start(bf16[136,1280]{1,0:T(8,128)(2,1)S(1)} %get-tuple-element.31), channel_id=1, source_target_pairs={{0,1},{1,0},{2,3},{3,2},{4,5},{5,4},{6,7},{7,6},{8,9},{9,8},{10,11... | collective-permute-start | bytes 1044488 | tf_op jit(solution)/shard_map/ppermute | solution.py:475
  74.0 17.5 %collective-permute-start.4 = (bf16[136,1280]{1,0:T(8,128)(2,1)S(1)}, bf16[136,1280]{1,0:T(8,128)(2,1)S(1)}, u32[]{:S(2)}, u32[]{:S(2)}) collective-permute-start(bf16[136,1280]{1,0:T(8,128)(2,1)S(1)} %get-tuple-element.37), channel_id=1, source_target_pairs={{0,3},{1,2},{2,1},{3,0},{4,7},{5,6},{6,5},{7,4},{8,11},{9,10},{10,... | collective-permute-start | bytes 1044488 | tf_op jit(solution)/shard_map/ppermute | solution.py:493
  76.2 15.2 %collective-permute-start.1 = (bf16[128,1280]{1,0:T(8,128)(2,1)S(1)}, bf16[128,1280]{1,0:T(8,128)(2,1)S(1)}, u32[]{:S(2)}, u32[]{:S(2)}) collective-permute-start(bf16[128,1280]{1,0:T(8,128)(2,1)S(1)} %get-tuple-element.32), channel_id=1, source_target_pairs={{0,3},{1,2},{2,1},{3,0},{4,7},{5,6},{6,5},{7,4},{8,11},{9,10},{10,... | collective-permute-start | bytes 983048 | tf_op jit(solution)/shard_map/ppermute | solution.py:476
  77.3 14.1 %collective-permute-start.5 = (bf16[128,1280]{1,0:T(8,128)(2,1)S(1)}, bf16[128,1280]{1,0:T(8,128)(2,1)S(1)}, u32[]{:S(2)}, u32[]{:S(2)}) collective-permute-start(bf16[128,1280]{1,0:T(8,128)(2,1)S(1)} %get-tuple-element.38), channel_id=1, source_target_pairs={{0,1},{1,0},{2,3},{3,2},{4,5},{5,4},{6,7},{7,6},{8,9},{9,8},{10,11... | collective-permute-start | bytes 983048 | tf_op jit(solution)/shard_map/ppermute | solution.py:494

commit v3 on v2

--- a/solution.py
+++ b/solution.py
@@ -10,6 +10,7 @@
 
 BLOCK = 256
 SEQ = ("seq_0", "seq_1", "seq_2")
+CHIPS = ("seq_0", "seq_1")
 SEQ_HEAD = ("seq_0", "seq_1", "seq_2", "head")
 EPSILON = 1e-05
 F32 = jnp.float32
@@ -80,6 +81,7 @@
     head_size,
     offset_ref,
     y_ref,
+    core_ref,
     stream_hbm,
     in_hbm,
     step_hbm,
@@ -171,7 +173,7 @@
     whole = jnp.concatenate(
         [summary, jnp.broadcast_to(link_row, (summary.shape[0], LANES))], axis=1
     ).astype(BF16)
-    summary_ref[...] = whole.reshape(summary_ref.shape)
+    summary_ref[...] = whole
 
 
 def within_kernel(
@@ -223,10 +225,7 @@
         slope_ref[cut, :] = per_lane * gate
 
 
-def scan_kernel(head_size, pieces_ref, before_ref):
-    shards, rows, wide = pieces_ref.shape
-    width = wide - LANES
-    links = pieces_ref[:, 0, width:]
+def link_lanes(links, width, head_size):
     lane = lax.broadcasted_iota(jnp.int32, (LANES, width), 0)
     spot = lax.broadcasted_iota(jnp.int32, (LANES, width), 1)
     head = jnp.where(lane >= PAD, lane - PAD, lane)
@@ -234,11 +233,43 @@
     spread = jnp.where(
         (lane < 2 * PAD) & (spot >= first) & (spot < first + head_size), 1.0, 0.0
     ).astype(BF16)
-    per_lane = dot(links, spread)
+    return dot(links, spread)
+
+
+def combine_kernel(head_size, core_ref, own_ref, other_ref, pieces_ref):
+    states, wide = own_ref.shape
+    width = wide - LANES
+    half = width // 2
+    first_core = core_ref[0] == 0
+    own = own_ref[...].astype(F32)
+    other = other_ref[...].astype(F32)
+    earlier = jnp.where(first_core, own, other)
+    later = jnp.where(first_core, other, own)
+    rate = link_lanes(later[:8, width:].astype(BF16), width, head_size)[:1, :]
+    total = rate * earlier[:, :width] + later[:, :width]
+    total = jnp.where(first_core, total[:, :half], total[:, half:])
+    parts_a, parts_b = own[:8, width:], other[:8, width:]
+    link = (parts_a + pltpu.roll(parts_a, LANES - PAD, 1)) * (
+        parts_b + pltpu.roll(parts_b, LANES - PAD, 1)
+    )
+    lane = lax.broadcasted_iota(jnp.int32, link.shape, 1)
+    heads = half // head_size
+    link = jnp.where(first_core, link, pltpu.roll(link, LANES - heads, 1))
+    link = jnp.where(lane < heads, link, 0.0)
+    high = link.astype(BF16).astype(F32)
+    link = high + pltpu.roll(link - high, PAD, 1)
+    link = jnp.broadcast_to(link[:1, :], (states, LANES))
+    pieces_ref[...] = jnp.concatenate([total, link], axis=1).astype(BF16).reshape(pieces_ref.shape)
+
+
+def scan_kernel(head_size, pieces_ref, before_ref):
+    chips, rows, wide = pieces_ref.shape
+    width = wide - LANES
+    per_lane = link_lanes(pieces_ref[:, 0, width:], width, head_size)
     state = jnp.zeros((rows, width), F32)
-    for shard in range(shards):
-        before_ref[shard] = state.astype(BF16)
-        state = per_lane[shard : shard + 1, :] * state + pieces_ref[shard, :, :width].astype(F32)
+    for chip in range(chips):
+        before_ref[chip] = state.astype(BF16)
+        state = per_lane[chip : chip + 1, :] * state + pieces_ref[chip, :, :width].astype(F32)
 
 
 def with_squares(piece, squares):
@@ -260,8 +291,11 @@
 def finish_kernel(
     head_size,
     offset_ref,
+    core_ref,
     out_ref,
     before_ref,
+    before_other_ref,
+    other_ref,
     first_ref,
     factor_ref,
     base_ref,
@@ -278,7 +312,15 @@
     before = jnp.max(docs_column(starts, offset - 1, 8)[:1, :], axis=0, keepdims=True)
     spread = head_lanes(width, head_size)
     constant_rows = dot_first(factor_ref[:, rows:], spread)[:8, :]
-    state = before_ref[...].reshape(-1, width).astype(F32)
+    first_core = core_ref[0] == 0
+    states = other_ref.shape[0]
+    half_a = before_ref[...].reshape(states, width // 2).astype(F32)
+    half_b = before_other_ref[...].reshape(states, width // 2).astype(F32)
+    state = jnp.concatenate(
+        [jnp.where(first_core, half_a, half_b), jnp.where(first_core, half_b, half_a)], axis=1
+    )
+    rate = link_lanes(other_ref[:8, width:], width, head_size)[:1, :]
+    state = jnp.where(first_core, state, rate * state + other_ref[:, :width].astype(F32))
     gain = gain_ref[...].reshape(1, width)
     step = rows // 4
     for block in range(rows // BLOCK):
@@ -401,7 +443,8 @@
     head_size = width // heads
     states = in_coeff.shape[1]
     model = out_proj.shape[1]
-    shards = lax.axis_size(SEQ)
+    chips = lax.axis_size(CHIPS)
+    core = lax.axis_index("seq_2").astype(jnp.int32)[None]
     y = lax.axis_index("head").astype(jnp.int32)[None]
     offset = (lax.axis_index(SEQ) * rows).astype(jnp.int32)[None]
     starts = doc_starts[None, :]
@@ -410,17 +453,36 @@
     summary, into, factor = call(
         functools.partial(state_kernel, head_size),
         [
-            shape((shards, states // shards, width + LANES), BF16),
+            shape((states, width + LANES), BF16),
             shape((2 * PAD, rows + LANES), BF16),
             shape((2 * PAD, rows + LANES), BF16),
         ],
-        [offset, y],
+        [offset, y, core],
         arrays,
         2_000_000_000,
         FULL,
         [pltpu.VMEM(a.shape, a.dtype) for a in arrays] + [pltpu.SemaphoreType.DMA((len(arrays),))],
     )
-    pieces = lax.all_to_all(summary, SEQ, 0, 0, tiled=True)
+    other = lax.ppermute(summary, "seq_2", [(0, 1), (1, 0)])
+    pieces = call(
+        functools.partial(combine_kernel, head_size),
+        shape((chips, states // chips, width // 2 + LANES), BF16),
+        [core],
+        [summary, other],
+        200_000_000,
+        8,
+    )
+    pieces = lax.all_to_all(pieces, CHIPS, 0, 0, tiled=True)
+    prior = call(
+        functools.partial(scan_kernel, head_size),
+        shape((chips, states // chips, width // 2), BF16),
+        [],
+        [pieces],
+        10_000_000_000,
+        8,
+    )
+    incoming = lax.all_to_all(prior, CHIPS, 0, 0, tiled=True)
+    incoming_other = lax.ppermute(incoming, "seq_2", [(0, 1), (1, 0)])
     base, slope, first = call(
         functools.partial(within_kernel, head_size),
         [
@@ -431,25 +493,16 @@
         [offset],
         [stream, gate_input, in_coeff, out_coeff, into, factor, skip_scale[None], starts],
         4_000_000_000,
-        FULL,
-    )
-    prior = call(
-        functools.partial(scan_kernel, head_size),
-        shape((shards, states // shards, width), BF16),
-        [],
-        [pieces],
-        10_000_000_000,
-        8,
-    )
-    incoming = lax.all_to_all(prior, SEQ, 0, 0, tiled=True)
+        22,
+    )
     step = rows // 4
     half = model // 2
     hidden, squares = call(
         functools.partial(finish_kernel, head_size),
         [shape((rows, width), BF16), shape((4, step), F32)],
-        [offset],
-        [out_coeff, incoming, first, factor, base, slope, norm_gain, starts],
-        4_000_000_000,
+        [offset, core],
+        [out_coeff, incoming, incoming_other, other, first, factor, base, slope, norm_gain, starts],
+        1_000_000_000,
         22,
     )
     send_a, send_b = call(

time: 93.2 us -> 81.1 us (0.87)
  the two profiles are of different devices: /device:TPU:6 before, /device:TPU:1 now
where the time goes in v3:
time: 81.1 us; the launch traced here: 80.9 us
  blocking collectives  33.6 us (41%)
  waiting for transfers between devices  20.3 us (25%)
  Pallas kernels  12.9 us (16%)
  starting transfers between devices  12.9 us (16%)
  local copies, waits for them, and re-layouts  1.04 us (1%)
    all_to_all x1, blocking collectives, local(): pieces = lax.all_to_all(pieces, CHIPS, 0, 0, tiled=True)  18.8 us
    all_to_all x1, blocking collectives, local(): incoming = lax.all_to_all(prior, CHIPS, 0, 0, tiled=True)  14.8 us
    ppermute x1, waiting for transfers between devices, local(): near_b = lax.ppermute(send_b, 'head', pair_3)  14.1 us
    pallas_call x10, Pallas kernels, call(): pl.pallas_call(kernel, out_shape=out_shape, in_specs=[SMEM_SPEC] * len(sc...  12.9 us
    ppermute x1, waiting for transfers between devices, local(): got_b = lax.ppermute(send_b, 'head', pair_3)  4.71 us
    ppermute x1, starting transfers between devices, local(): other = lax.ppermute(summary, 'seq_2', [(0, 1), (1, 0)])  3.29 us
    ppermute x1, starting transfers between devices, local(): incoming_other = lax.ppermute(incoming, 'seq_2', [(0, 1), (1, 0)])  2.92 us
    ppermute x1, starting transfers between devices, local(): far_a = lax.ppermute(send_a, 'head', pair_3)  2.01 us
  transfers between devices with their start and end apart: 8, of which 3 were waited for; matrix products, arithmetic and copies ran while one was open for 0% of the time, Pallas kernels for 7%

profile of v3, /device:TPU:1, one launch (start us, length us, event | category | flops | bytes accessed | tf_op | source)
XLA Modules:
  0.0 80.9 jit_solution(8450491184059630896)
XLA Ops:
  0.0 3.3 %shard_map.109 = (bf16[128,1408]{1,0:T(8,128)(2,1)}, bf16[64,640]{1,0:T(8,128)(2,1)}, bf16[64,640]{1,0:T(8,128)(2,1)}) custom-call(s32[1]{0:T(128)} %bitcast.1.offset_ref, s32[1]{0:T(128)} %bitcast.y_ref, s32[1]{0:T(128)} %bitcast.2.core_ref, bf16[512,1280]{1,0:T(8,128)(2,1)} %stream_ref.1, bf16[512,128]{1,0:T(8,128)(2,1)} %in_ref.1, f32[20,512]{1,0:T(8,128)} %step_hbm.1, ...), custom_call_target="tpu_custom_call" | custom-call | flops 2000000000 | bytes 4000000 | tf_op jit(solution)/shard_map/pallas_call | solution.py:416
  3.3 3.3 %collective-permute-start = (bf16[128,1408]{1,0:T(8,128)(2,1)}, bf16[128,1408]{1,0:T(8,128)(2,1)S(1)}, u32[]{:S(2)}, u32[]{:S(2)}) collective-permute-start(bf16[128,1408]{1,0:T(8,128)(2,1)} %get-tuple-element.22.own_ref), channel_id=1, source_target_pairs={{0,4},{4,0},{1,5},{5,1},{2,6},{6,2},{3,7},{7,3},{8,12},{12,8},{9,1... | collective-permute-start | bytes 1081352 | tf_op jit(solution)/shard_map/ppermute | solution.py:466
  6.6 1.5 %collective-permute-done.other_ref = bf16[128,1408]{1,0:T(8,128)(2,1)S(1)} collective-permute-done((bf16[128,1408]{1,0:T(8,128)(2,1)}, bf16[128,1408]{1,0:T(8,128)(2,1)S(1)}, u32[]{:S(2)}, u32[]{:S(2)}) %collective-permute-start) | collective-permute-done | bytes 360480 | tf_op jit(solution)/shard_map/ppermute | solution.py:466
  8.1 1.0 %copy-done = bf16[128,1408]{1,0:T(8,128)(2,1)S(1)} copy-done((bf16[128,1408]{1,0:T(8,128)(2,1)S(1)}, bf16[128,1408]{1,0:T(8,128)(2,1)}, u32[]{:S(2)}) %copy-start) | copy-done | bytes 360472
  9.1 0.3 shard_map.110
  9.4 18.8 %all_to_all.10.pieces_ref = bf16[32,4,768]{2,1,0:T(4,128)(2,1)S(1)} all-to-all(bf16[32,4,768]{2,1,0:T(4,128)(2,1)S(1)} %shard_map.110), channel_id=1, replica_groups=mesh['seq_0'=4,'seq_1'=8,'seq_2'=2,'head'=4] {'seq_0','seq_1'}, dimensions={0} | all-to-all | bytes 393216 | tf_op jit(solution)/shard_map/all_to_all | solution.py:475
  28.2 0.0 copy-start.6
  28.2 0.0 copy-start.7
  28.2 0.0 copy-start.8
  28.2 0.0 slice-start.1
  28.2 0.3 shard_map.111
  28.5 14.8 %all_to_all.11.before_ref = bf16[32,4,640]{2,1,0:T(4,128)(2,1)S(1)} all-to-all(bf16[32,4,640]{2,1,0:T(4,128)(2,1)S(1)} %shard_map.111), channel_id=1, replica_groups=mesh['seq_0'=4,'seq_1'=8,'seq_2'=2,'head'=4] {'seq_0','seq_1'}, dimensions={0} | all-to-all | bytes 327680 | tf_op jit(solution)/shard_map/all_to_all | solution.py:484
  43.3 2.9 %collective-permute-start.1 = (bf16[32,4,640]{2,1,0:T(4,128)(2,1)S(1)}, bf16[32,4,640]{2,1,0:T(4,128)(2,1)S(1)}, u32[]{:S(2)}, u32[]{:S(2)}) collective-permute-start(bf16[32,4,640]{2,1,0:T(4,128)(2,1)S(1)} %all_to_all.11.before_ref), channel_id=1, source_target_pairs={{0,4},{4,0},{1,5},{5,1},{2,6},{6,2},{3,7},{7,3},{8,12},{12,8},{9,1... | collective-permute-start | bytes 491528 | tf_op jit(solution)/shard_map/ppermute | solution.py:485
  46.2 0.0 copy-start.3
  46.2 2.5 %shard_map.112 = (f32[512,1280]{1,0:T(8,128)S(1)}, f32[512,1280]{1,0:T(8,128)S(1)}, f32[128,1280]{1,0:T(8,128)S(1)}) custom-call(s32[1]{0:T(128)} %bitcast.1.offset_ref, bf16[512,1280]{1,0:T(8,128)(2,1)S(1)} %copy-done.5, bf16[512,1280]{1,0:T(8,128)(2,1)S(1)} %copy-done.6, bf16[512,128]{1,0:T(8,128)(2,1)S(1)} %copy-done.7, bf16[512,128]{1,0:T(8,128)(2,1)S(1)} %copy-done.1, ...), custom_call_target="tpu_custom_call" | custom-call | flops 4000000000 | bytes 4000000 | tf_op jit(solution)/shard_map/pallas_call | solution.py:416
  48.8 0.0 collective-permute-done.1.before_other_ref
  48.8 1.2 %shard_map.113 = (bf16[512,1280]{1,0:T(8,128)(2,1)S(1)}, f32[4,128]{1,0:T(4,128)S(1)}) custom-call(s32[1]{0:T(128)} %bitcast.1.offset_ref, s32[1]{0:T(128)} %bitcast.2.core_ref, bf16[512,128]{1,0:T(8,128)(2,1)S(1)} %copy-done.1, bf16[32,4,640]{2,1,0:T(4,128)(2,1)S(1)} %all_to_all.11.before_ref, ...), custom_call_target="tpu_custom_call" | custom-call | flops 1000000000 | bytes 4000000 | tf_op jit(solution)/shard_map/pallas_call | solution.py:416
  50.0 1.0 %shard_map.116 = (bf16[136,1280]{1,0:T(8,128)(2,1)S(1)}, bf16[128,1280]{1,0:T(8,128)(2,1)S(1)}) custom-call(s32[1]{0:T(128)} %bitcast.y_ref, bf16[512,1280]{1,0:T(8,128)(2,1)S(1)} %get-tuple-element.29.hidden_ref, bf16[1280,2560]{1,0:T(8,128)(2,1)S(1)} %bitcast.8, f32[4,128]{1,0:T(4,128)S(1)} %get-tuple-element.28.squares_ref), custom_call_target="tpu_custom_call" | custom-call | flops 1000000000 | bytes 4000000 | tf_op jit(solution)/shard_map/pallas_call | solution.py:416
  51.0 1.4 %collective-permute-start.4 = (bf16[136,1280]{1,0:T(8,128)(2,1)S(1)}, bf16[136,1280]{1,0:T(8,128)(2,1)S(1)}, u32[]{:S(2)}, u32[]{:S(2)}) collective-permute-start(bf16[136,1280]{1,0:T(8,128)(2,1)S(1)} %get-tuple-element.35), channel_id=1, source_target_pairs={{0,1},{1,0},{2,3},{3,2},{4,5},{5,4},{6,7},{7,6},{8,9},{9,8},{10,11... | collective-permute-start | bytes 1044488 | tf_op jit(solution)/shard_map/ppermute | solution.py:518
  52.4 1.9 %collective-permute-start.5 = (bf16[128,1280]{1,0:T(8,128)(2,1)S(1)}, bf16[128,1280]{1,0:T(8,128)(2,1)S(1)}, u32[]{:S(2)}, u32[]{:S(2)}) collective-permute-start(bf16[128,1280]{1,0:T(8,128)(2,1)S(1)} %get-tuple-element.36), channel_id=1, source_target_pairs={{0,3},{1,2},{2,1},{3,0},{4,7},{5,6},{6,5},{7,4},{8,11},{9,10},{10,... | collective-permute-start | bytes 983048 | tf_op jit(solution)/shard_map/ppermute | solution.py:519
  54.3 1.0 %shard_map.115 = (bf16[136,1280]{1,0:T(8,128)(2,1)S(1)}, bf16[128,1280]{1,0:T(8,128)(2,1)S(1)}) custom-call(s32[1]{0:T(128)} %bitcast.y_ref, bf16[512,1280]{1,0:T(8,128)(2,1)S(1)} %get-tuple-element.29.hidden_ref, bf16[1280,2560]{1,0:T(8,128)(2,1)S(1)} %bitcast.8, f32[4,128]{1,0:T(4,128)S(1)} %get-tuple-element.28.squares_ref), custom_call_target="tpu_custom_call" | custom-call | flops 1000000000 | bytes 4000000 | tf_op jit(solution)/shard_map/pallas_call | solution.py:416
  55.3 0.7 collective-permute-start.2
  56.0 1.9 %shard_map.114 = (f32[128,2560]{1,0:T(8,128)S(1)}, f32[128,1280]{1,0:T(8,128)S(1)}, f32[128,1280]{1,0:T(8,128)S(1)}) custom-call(s32[1]{0:T(128)} %bitcast.y_ref, bf16[512,1280]{1,0:T(8,128)(2,1)S(1)} %get-tuple-element.29.hidden_ref, bf16[1280,2560]{1,0:T(8,128)(2,1)S(1)} %bitcast.8), custom_call_target="tpu_custom_call" | custom-call | flops 2000000000 | bytes 4000000 | tf_op jit(solution)/shard_map/pallas_call | solution.py:416
  57.9 4.7 %collective-permute-done.5.got_b_ref = bf16[128,1280]{1,0:T(8,128)(2,1)S(1)} collective-permute-done((bf16[128,1280]{1,0:T(8,128)(2,1)S(1)}, bf16[128,1280]{1,0:T(8,128)(2,1)S(1)}, u32[]{:S(2)}, u32[]{:S(2)}) %collective-permute-start.5) | collective-permute-done | bytes 327712 | tf_op jit(solution)/shard_map/ppermute | solution.py:519
  62.6 0.0 collective-permute-done.4.got_a_ref
  62.6 0.2 shard_map.117
  62.7 2.0 %collective-permute-start.6 = (bf16[136,1280]{1,0:T(8,128)(2,1)S(1)}, bf16[136,1280]{1,0:T(8,128)(2,1)S(1)}, u32[]{:S(2)}, u32[]{:S(2)}) collective-permute-start(bf16[136,1280]{1,0:T(8,128)(2,1)S(1)} %get-tuple-element.37), channel_id=1, source_target_pairs={{0,3},{1,2},{2,1},{3,0},{4,7},{5,6},{6,5},{7,4},{8,11},{9,10},{10,... | collective-permute-start | bytes 1044488 | tf_op jit(solution)/shard_map/ppermute | solution.py:546
  64.8 0.8 collective-permute-start.3
  65.5 0.0 collective-permute-start.7
  65.5 14.1 %collective-permute-done.3.near_b_ref = bf16[128,1280]{1,0:T(8,128)(2,1)S(1)} collective-permute-done((bf16[128,1280]{1,0:T(8,128)(2,1)S(1)}, bf16[128,1280]{1,0:T(8,128)(2,1)S(1)}, u32[]{:S(2)}, u32[]{:S(2)}) %collective-permute-start.3) | collective-permute-done | bytes 327712 | tf_op jit(solution)/shard_map/ppermute | solution.py:529
  79.6 0.0 collective-permute-done.2.near_a_ref
  79.6 1.3 %shard_map.118 = bf16[128,2560]{1,0:T(8,128)(2,1)} custom-call(s32[1]{0:T(128)} %bitcast.y_ref, f32[4,128]{1,0:T(4,128)S(1)} %get-tuple-element.28.squares_ref, f32[128,2560]{1,0:T(8,128)S(1)} %get-tuple-element.30.own_ref, bf16[136,1280]{1,0:T(8,128)(2,1)S(1)} %collective-permute-done.2.near_a_ref, bf16[128,1280]{1,0:T(8,128)(2,1)S(1)} %collective-permute-done.3.near_b_ref, ...), custom_call_target="tpu_custom_call" | custom-call | flops 1000000000 | bytes 4000000 | tf_op jit(solution)/shard_map/pallas_call | solution.py:416
  (21 shorter events, 0.0 us)
Async XLA Ops:
  3.3 4.8 %collective-permute-start = (bf16[128,1408]{1,0:T(8,128)(2,1)}, bf16[128,1408]{1,0:T(8,128)(2,1)S(1)}, u32[]{:S(2)}, u32[]{:S(2)}) collective-permute-start(bf16[128,1408]{1,0:T(8,128)(2,1)} %get-tuple-element.22.own_ref), channel_id=1, source_target_pairs={{0,4},{4,0},{1,5},{5,1},{2,6},{6,2},{3,7},{7,3},{8,12},{12,8},{9,1... | collective-permute-start | bytes 1081352 | tf_op jit(solution)/shard_map/ppermute | solution.py:466
  8.1 1.0 %copy-start = (bf16[128,1408]{1,0:T(8,128)(2,1)S(1)}, bf16[128,1408]{1,0:T(8,128)(2,1)}, u32[]{:S(2)}) copy-start(bf16[128,1408]{1,0:T(8,128)(2,1)} %get-tuple-element.22.own_ref) | copy-start | bytes 1081348
  9.1 40.9 %slice-start = ((s8[6553600]{0:T(1024)(128)(4,1)}), s8[4194304]{0:T(1024)(128)(4,1)S(1)}, s32[]{:S(2)}) async-start(s8[6553600]{0:T(1024)(128)(4,1)} %bitcast.7), calls=%async_computation.2 | async-start | bytes 8388608
  28.1 18.0 %copy-start.1 = (bf16[512,128]{1,0:T(8,128)(2,1)S(1)}, bf16[512,128]{1,0:T(8,128)(2,1)}, u32[]{:S(2)}) copy-start(bf16[512,128]{1,0:T(8,128)(2,1)} %out_ref.3) | copy-start | bytes 393220
  28.1 18.0 %copy-start.2 = (bf16[64,640]{1,0:T(8,128)(2,1)S(1)}, bf16[64,640]{1,0:T(8,128)(2,1)}, u32[]{:S(2)}) copy-start(bf16[64,640]{1,0:T(8,128)(2,1)} %get-tuple-element.24.factor_ref) | copy-start | bytes 245764
  28.1 18.0 %copy-start.4 = (s32[128]{0:T(128)S(1)}, s32[128]{0:T(128)}, u32[]{:S(2)}) copy-start(s32[128]{0:T(128)} %param.21) | copy-start | bytes 1540
  28.2 18.0 %copy-start.5 = (bf16[512,1280]{1,0:T(8,128)(2,1)S(1)}, bf16[512,1280]{1,0:T(8,128)(2,1)}, u32[]{:S(2)}) copy-start(bf16[512,1280]{1,0:T(8,128)(2,1)} %stream_ref.1) | copy-start | bytes 3932164
  28.2 18.0 %copy-start.6 = (bf16[512,1280]{1,0:T(8,128)(2,1)S(1)}, bf16[512,1280]{1,0:T(8,128)(2,1)}, u32[]{:S(2)}) copy-start(bf16[512,1280]{1,0:T(8,128)(2,1)} %gate_ref.1) | copy-start | bytes 3932164
  28.2 18.0 %copy-start.7 = (bf16[512,128]{1,0:T(8,128)(2,1)S(1)}, bf16[512,128]{1,0:T(8,128)(2,1)}, u32[]{:S(2)}) copy-start(bf16[512,128]{1,0:T(8,128)(2,1)} %in_ref.1) | copy-start | bytes 393220
  28.2 18.0 %copy-start.8 = (f32[20]{0:T(128)S(1)}, f32[20]{0:T(128)}, u32[]{:S(2)}) copy-start(f32[20]{0:T(128)} %param.18) | copy-start | bytes 244
  28.2 18.0 %copy-start.9 = (bf16[64,640]{1,0:T(8,128)(2,1)S(1)}, bf16[64,640]{1,0:T(8,128)(2,1)}, u32[]{:S(2)}) copy-start(bf16[64,640]{1,0:T(8,128)(2,1)} %get-tuple-element.23.into_ref) | copy-start | bytes 245764
  28.2 21.8 %slice-start.1 = ((s8[6553600]{0:T(1024)(128)(4,1)}), s8[2359296]{0:T(1024)(128)(4,1)S(1)}, s32[]{:S(2)}) async-start(s8[6553600]{0:T(1024)(128)(4,1)} %bitcast.7), calls=%async_computation.3 | async-start | bytes 4718592
  43.3 5.5 %collective-permute-start.1 = (bf16[32,4,640]{2,1,0:T(4,128)(2,1)S(1)}, bf16[32,4,640]{2,1,0:T(4,128)(2,1)S(1)}, u32[]{:S(2)}, u32[]{:S(2)}) collective-permute-start(bf16[32,4,640]{2,1,0:T(4,128)(2,1)S(1)} %all_to_all.11.before_ref), channel_id=1, source_target_pairs={{0,4},{4,0},{1,5},{5,1},{2,6},{6,2},{3,7},{7,3},{8,12},{12,8},{9,1... | collective-permute-start | bytes 491528 | tf_op jit(solution)/shard_map/ppermute | solution.py:485
  46.2 2.6 %copy-start.3 = (f32[1280]{0:T(1024)S(1)}, f32[1280]{0:T(1024)}, u32[]{:S(2)}) copy-start(f32[1280]{0:T(1024)} %gain_ref.1) | copy-start | bytes 15364
  51.0 11.6 %collective-permute-start.4 = (bf16[136,1280]{1,0:T(8,128)(2,1)S(1)}, bf16[136,1280]{1,0:T(8,128)(2,1)S(1)}, u32[]{:S(2)}, u32[]{:S(2)}) collective-permute-start(bf16[136,1280]{1,0:T(8,128)(2,1)S(1)} %get-tuple-element.35), channel_id=1, source_target_pairs={{0,1},{1,0},{2,3},{3,2},{4,5},{5,4},{6,7},{7,6},{8,9},{9,8},{10,11... | collective-permute-start | bytes 1044488 | tf_op jit(solution)/shard_map/ppermute | solution.py:518
  52.4 10.2 %collective-permute-start.5 = (bf16[128,1280]{1,0:T(8,128)(2,1)S(1)}, bf16[128,1280]{1,0:T(8,128)(2,1)S(1)}, u32[]{:S(2)}, u32[]{:S(2)}) collective-permute-start(bf16[128,1280]{1,0:T(8,128)(2,1)S(1)} %get-tuple-element.36), channel_id=1, source_target_pairs={{0,3},{1,2},{2,1},{3,0},{4,7},{5,6},{6,5},{7,4},{8,11},{9,10},{10,... | collective-permute-start | bytes 983048 | tf_op jit(solution)/shard_map/ppermute | solution.py:519
  55.3 24.3 %collective-permute-start.2 = (bf16[136,1280]{1,0:T(8,128)(2,1)S(1)}, bf16[136,1280]{1,0:T(8,128)(2,1)S(1)}, u32[]{:S(2)}, u32[]{:S(2)}) collective-permute-start(bf16[136,1280]{1,0:T(8,128)(2,1)S(1)} %get-tuple-element.31), channel_id=1, source_target_pairs={{0,1},{1,0},{2,3},{3,2},{4,5},{5,4},{6,7},{7,6},{8,9},{9,8},{10,11... | collective-permute-start | bytes 1044488 | tf_op jit(solution)/shard_map/ppermute | solution.py:528
  62.7 16.9 %collective-permute-start.6 = (bf16[136,1280]{1,0:T(8,128)(2,1)S(1)}, bf16[136,1280]{1,0:T(8,128)(2,1)S(1)}, u32[]{:S(2)}, u32[]{:S(2)}) collective-permute-start(bf16[136,1280]{1,0:T(8,128)(2,1)S(1)} %get-tuple-element.37), channel_id=1, source_target_pairs={{0,3},{1,2},{2,1},{3,0},{4,7},{5,6},{6,5},{7,4},{8,11},{9,10},{10,... | collective-permute-start | bytes 1044488 | tf_op jit(solution)/shard_map/ppermute | solution.py:546
  64.8 14.9 %collective-permute-start.3 = (bf16[128,1280]{1,0:T(8,128)(2,1)S(1)}, bf16[128,1280]{1,0:T(8,128)(2,1)S(1)}, u32[]{:S(2)}, u32[]{:S(2)}) collective-permute-start(bf16[128,1280]{1,0:T(8,128)(2,1)S(1)} %get-tuple-element.32), channel_id=1, source_target_pairs={{0,3},{1,2},{2,1},{3,0},{4,7},{5,6},{6,5},{7,4},{8,11},{9,10},{10,... | collective-permute-start | bytes 983048 | tf_op jit(solution)/shard_map/ppermute | solution.py:529
  65.5 14.1 %collective-permute-start.7 = (bf16[128,1280]{1,0:T(8,128)(2,1)S(1)}, bf16[128,1280]{1,0:T(8,128)(2,1)S(1)}, u32[]{:S(2)}, u32[]{:S(2)}) collective-permute-start(bf16[128,1280]{1,0:T(8,128)(2,1)S(1)} %get-tuple-element.38), channel_id=1, source_target_pairs={{0,1},{1,0},{2,3},{3,2},{4,5},{5,4},{6,7},{7,6},{8,9},{9,8},{10,11... | collective-permute-start | bytes 983048 | tf_op jit(solution)/shard_map/ppermute | solution.py:547

commit v4 on v3

--- a/solution.py
+++ b/solution.py
@@ -89,6 +89,7 @@
     rate_hbm,
     starts_hbm,
     summary_ref,
+    first_ref,
     into_ref,
     factor_ref,
     stream_ref,
@@ -167,6 +168,7 @@
         scaled = (stream_ref[cut, :].astype(F32) * per_lane[cut, :]).astype(BF16)
         to_end = jnp.where(docs[cut, :] == ends[block], in_ref[cut, :].astype(F32), 0.0)
         states.append(constant_rows[block : block + 1, :] * dot_first(to_end.astype(BF16), scaled))
+    first_ref[...] = states[0].astype(BF16)
     summary = constant_rows[3:4, :] * states[0] + states[1]
     high = link.astype(BF16).astype(F32)
     link_row = as_row(high, LANES) + pltpu.roll(as_row(link - high, LANES), PAD, 1)
@@ -176,9 +178,10 @@
     summary_ref[...] = whole
 
 
-def within_kernel(
+def block_terms(
     head_size,
-    offset_ref,
+    offset,
+    block,
     stream_ref,
     gate_ref,
     in_ref,
@@ -187,42 +190,57 @@
     factor_ref,
     skip_ref,
     starts_ref,
-    base_ref,
-    slope_ref,
-    first_ref,
 ):
     rows, width = stream_ref.shape
     heads = skip_ref.shape[1]
-    offset = offset_ref[0]
+    step = rows // 4
+    inner = block % (BLOCK // step)
+    start = pl.multiple_of(block * step, step)
+    origin = pl.multiple_of((block - inner) * step, BLOCK)
+    here = pl.ds(start, step)
+    whole = pl.ds(origin, BLOCK)
     starts = starts_ref[...]
-    docs = docs_column(starts, offset, rows)
-    docs_across = docs_row(starts, offset, rows)
+    docs = docs_column(starts, offset + start, step)
+    docs_across = docs_row(starts, offset + origin, BLOCK)
+    before = jnp.max(docs_column(starts, offset + origin - 1, 8)[:1, :], axis=0, keepdims=True)
     spread = head_lanes(width, head_size)
     skip = jnp.concatenate(
         [as_column(skip_ref[...], heads), jnp.zeros((PAD - heads, 1), F32)], axis=0
     )
     skip_row = dot_first(two_parts(jnp.broadcast_to(skip, (PAD, LANES))), spread)[:1, :]
-    i = lax.broadcasted_iota(jnp.int32, (BLOCK, BLOCK), 0)
-    j = lax.broadcasted_iota(jnp.int32, (BLOCK, BLOCK), 1)
-    constant_rows = dot_first(into_ref[:, rows:], spread)[:8, :]
-    for block in range(rows // BLOCK):
-        cut = slice(block * BLOCK, (block + 1) * BLOCK)
-        scaled = stream_ref[cut, :].astype(F32) * dot_first(into_ref[:, cut], spread)
-        scaled = scaled.astype(BF16)
-        if block == 0:
-            end = docs[BLOCK - 1 : BLOCK, :]
-            to_end = jnp.where(docs[cut, :] == end, in_ref[cut, :].astype(F32), 0.0)
-            first_ref[...] = constant_rows[:1, :] * dot_first(to_end.astype(BF16), scaled)
-        scores = dot_last(out_ref[cut, :], in_ref[cut, :])
-        live = (i >= j) & (docs[cut, :] == docs_across[:, cut])
-        weights = jnp.where(live, scores, 0.0).astype(BF16)
-        per_lane = dot_first(factor_ref[:, cut], spread)
-        within = dot(weights, scaled)
-        value = per_lane * within + skip_row * stream_ref[cut, :].astype(F32)
-        gate = gate_ref[cut, :].astype(F32)
-        gate = gate / (1.0 + jnp.exp(-gate))
-        base_ref[cut, :] = value * gate
-        slope_ref[cut, :] = per_lane * gate
+    scaled = stream_ref[whole, :].astype(F32) * dot_first(into_ref[:, whole], spread)
+    own = out_ref[here, :]
+    scores = dot_last(own, in_ref[whole, :])
+    i = inner * step + lax.broadcasted_iota(jnp.int32, (step, BLOCK), 0)
+    j = lax.broadcasted_iota(jnp.int32, (step, BLOCK), 1)
+    live = (i >= j) & (docs == docs_across)
+    weights = jnp.where(live, scores, 0.0).astype(BF16)
+    per_lane = dot_first(factor_ref[:, here], spread)
+    value = per_lane * dot(weights, scaled.astype(BF16)) + skip_row * stream_ref[here, :].astype(F32)
+    gate = gate_ref[here, :].astype(F32)
+    gate = gate / (1.0 + jnp.exp(-gate))
+    joined = jnp.where(docs == before, own.astype(F32), 0.0).astype(BF16)
+    return value * gate, per_lane * gate, joined
+
+
+def block_hidden(base, slope, joined, state, gain):
+    gated = base + slope * dot(joined, state)
+    square = gated * gated
+    total = square[:, :LANES]
+    for lane in range(LANES, square.shape[1], LANES):
+        total = total + square[:, lane : lane + LANES]
+    return (gated * gain).astype(BF16), jnp.sum(jnp.transpose(total), axis=0, keepdims=True)
+
+
+def ahead_kernel(head_size, offset_ref, y_ref, *refs):
+    base_ref, slope_ref, joined_ref = refs[-3:]
+    base_ref[...], slope_ref[...], joined_ref[...] = block_terms(
+        head_size, offset_ref[0], y_ref[0] ^ 2, *refs[:-3]
+    )
+
+
+def pass_kernel(from_ref, to_ref):
+    to_ref[...] = from_ref[...]
 
 
 def link_lanes(links, width, head_size):
@@ -288,11 +306,15 @@
     return row[:, :step] + row[:, step : 2 * step]
 
 
-def finish_kernel(
+def state_of(states_ref, block):
+    states = states_ref.shape[0] // 2
+    return states_ref[pl.ds(pl.multiple_of((block // 2) * states, states), states), :]
+
+
+def far_kernel(
     head_size,
-    offset_ref,
+    y_ref,
     core_ref,
-    out_ref,
     before_ref,
     before_other_ref,
     other_ref,
@@ -300,20 +322,19 @@
     factor_ref,
     base_ref,
     slope_ref,
+    joined_ref,
     gain_ref,
-    starts_ref,
-    hidden_ref,
-    squares_ref,
+    proj_ref,
+    send_a_ref,
+    send_b_ref,
+    states_ref,
 ):
-    rows, width = base_ref.shape
-    offset = offset_ref[0]
-    starts = starts_ref[...]
-    docs = docs_column(starts, offset, rows)
-    before = jnp.max(docs_column(starts, offset - 1, 8)[:1, :], axis=0, keepdims=True)
+    width = base_ref.shape[1]
+    states = other_ref.shape[0]
+    rows = factor_ref.shape[1] - LANES
     spread = head_lanes(width, head_size)
     constant_rows = dot_first(factor_ref[:, rows:], spread)[:8, :]
     first_core = core_ref[0] == 0
-    states = other_ref.shape[0]
     half_a = before_ref[...].reshape(states, width // 2).astype(F32)
     half_b = before_other_ref[...].reshape(states, width // 2).astype(F32)
     state = jnp.concatenate(
@@ -321,103 +342,104 @@
     )
     rate = link_lanes(other_ref[:8, width:], width, head_size)[:1, :]
     state = jnp.where(first_core, state, rate * state + other_ref[:, :width].astype(F32))
-    gain = gain_ref[...].reshape(1, width)
-    step = rows // 4
-    for block in range(rows // BLOCK):
-        cut = slice(block * BLOCK, (block + 1) * BLOCK)
-        joined = jnp.where(docs[cut, :] == before, out_ref[cut, :].astype(F32), 0.0).astype(BF16)
-        carried = dot(joined, (constant_rows[block : block + 1, :] * state).astype(BF16))
-        gated = base_ref[cut, :] + slope_ref[cut, :] * carried
-        square = gated * gated
-        total = square[:, :LANES]
-        for lane in range(LANES, width, LANES):
-            total = total + square[:, lane : lane + LANES]
-        for part in range(BLOCK // step):
-            piece = total[part * step : (part + 1) * step, :]
-            number = block * (BLOCK // step) + part
-            squares_ref[number : number + 1, :] = jnp.sum(
-                jnp.transpose(piece), axis=0, keepdims=True
-            )
-        hidden_ref[cut, :] = (gated * gain).astype(BF16)
-        state = constant_rows[2:3, :] * state + first_ref[...]
-        before = docs[(block + 1) * BLOCK - 1 : (block + 1) * BLOCK, :]
-
-
-def far_kernel(y_ref, hidden_ref, proj_ref, squares_ref, send_a_ref, send_b_ref):
-    step = hidden_ref.shape[0] // 4
-    half = proj_ref.shape[1] // 2
-    far = y_ref[0] ^ 2
-    piece = hidden_ref[pl.ds(far * step, step), :]
-    send_a_ref[...] = with_squares(
-        dot(piece, proj_ref[:, :half]), squares_ref[pl.ds(far, 1), :]
-    )
-    send_b_ref[...] = dot(piece, proj_ref[:, half:]).astype(BF16)
-
-
-def near_kernel(y_ref, hidden_ref, proj_ref, squares_ref, send_a_ref, send_b_ref):
-    step = hidden_ref.shape[0] // 4
-    half = proj_ref.shape[1] // 2
-    one, three = y_ref[0] ^ 1, y_ref[0] ^ 3
-    send_a_ref[...] = with_squares(
-        dot(hidden_ref[pl.ds(one * step, step), :], proj_ref[:, :half]),
-        squares_ref[pl.ds(one, 1), :],
-    )
-    send_b_ref[...] = dot(
-        hidden_ref[pl.ds(three * step, step), :], proj_ref[:, half:]
-    ).astype(BF16)
-
-
-def keep_kernel(y_ref, hidden_ref, proj_ref, own_ref, via_a_ref, via_b_ref):
-    step = hidden_ref.shape[0] // 4
-    half = proj_ref.shape[1] // 2
-    one, three = y_ref[0] ^ 1, y_ref[0] ^ 3
-    via_a_ref[...] = dot(hidden_ref[pl.ds(three * step, step), :], proj_ref[:, :half])
-    via_b_ref[...] = dot(hidden_ref[pl.ds(one * step, step), :], proj_ref[:, half:])
-    own_ref[...] = dot(hidden_ref[pl.ds(y_ref[0] * step, step), :], proj_ref[...])
-
-
-def middle_kernel(
-    y_ref, squares_ref, via_a_ref, via_b_ref, got_a_ref, got_b_ref, send_a_ref, send_b_ref
-):
+    states_ref[:states, :] = (constant_rows[:1, :] * state).astype(BF16)
+    state = constant_rows[2:3, :] * state + first_ref[...].astype(F32)
+    states_ref[states:, :] = (constant_rows[1:2, :] * state).astype(BF16)
+    piece, squares = block_hidden(
+        base_ref[...],
+        slope_ref[...],
+        joined_ref[...],
+        state_of(states_ref, y_ref[0] ^ 2),
+        gain_ref[...].reshape(1, width),
+    )
+    low = send_b_ref.shape[1]
+    send_b_ref[...] = dot(piece, proj_ref[:, -low:]).astype(BF16)
+    send_a_ref[...] = with_squares(dot(piece, proj_ref[:, :-low]), squares)
+
+
+def near_kernel(head_size, offset_ref, y_ref, states_ref, gain_ref, proj_ref, *refs):
+    send_a_ref, send_b_ref, hidden_ref, squares_ref = refs[-4:]
+    step = refs[0].shape[0] // 4
+    low = send_b_ref.shape[1]
+    gain = gain_ref[...].reshape(1, -1)
+    for number, block in enumerate((y_ref[0] ^ 3, y_ref[0] ^ 1)):
+        terms = block_terms(head_size, offset_ref[0], block, *refs[:-4])
+        piece, squares = block_hidden(*terms, state_of(states_ref, block), gain)
+        hidden_ref[number * step : (number + 1) * step, :] = piece
+        if number == 0:
+            send_b_ref[...] = dot(piece, proj_ref[:, -low:]).astype(BF16)
+            squares_ref[...] = squares
+        else:
+            send_a_ref[...] = with_squares(dot(piece, proj_ref[:, :-low]), squares)
+
+
+def keep_kernel(head_size, offset_ref, y_ref, states_ref, gain_ref, proj_ref, hidden_ref, *refs):
+    own_ref, via_a_ref, via_b_ref, squares_ref = refs[-4:]
+    step = refs[0].shape[0] // 4
+    low = via_b_ref.shape[1]
+    via_a_ref[...] = dot(hidden_ref[:step, :], proj_ref[:, :-low])
+    via_b_ref[...] = dot(hidden_ref[step:, :], proj_ref[:, -low:])
+    terms = block_terms(head_size, offset_ref[0], y_ref[0], *refs[:-4])
+    piece, squares = block_hidden(
+        *terms, state_of(states_ref, y_ref[0]), gain_ref[...].reshape(1, -1)
+    )
+    squares_ref[...] = squares
+    own_ref[...] = dot(piece, proj_ref[...])
+
+
+def middle_kernel(squares_ref, via_a_ref, via_b_ref, got_a_ref, got_b_ref, send_a_ref, send_b_ref):
     step = via_a_ref.shape[0]
-    squares = squares_ref[pl.ds(y_ref[0] ^ 3, 1), :] + squares_of(got_a_ref, step)
+    squares = squares_ref[...] + squares_of(got_a_ref, step)
     send_a_ref[...] = with_squares(via_a_ref[...] + got_a_ref[:step, :].astype(F32), squares)
     send_b_ref[...] = (via_b_ref[...] + got_b_ref[...].astype(F32)).astype(BF16)
 
 
 def last_kernel(
     channels,
-    y_ref,
     squares_ref,
     own_ref,
     near_a_ref,
     near_b_ref,
     far_a_ref,
     far_b_ref,
+    out_hbm,
     out_ref,
+    left,
 ):
     step, model = own_ref.shape
-    half = model // 2
-    squares = squares_ref[pl.ds(y_ref[0], 1), :]
+    edge = near_a_ref.shape[1]
+    squares = squares_ref[...]
     squares = squares + squares_of(near_a_ref, step) + squares_of(far_a_ref, step)
     scale = as_column(lax.rsqrt(squares / channels + EPSILON), step)
-    for near_ref, far_ref, low in ((near_a_ref, far_a_ref, 0), (near_b_ref, far_b_ref, half)):
-        total = (
-            own_ref[:, low : low + half]
-            + near_ref[:step, :].astype(F32)
-            + far_ref[:step, :].astype(F32)
-        )
-        out_ref[:, low : low + half] = (total * scale).astype(BF16)
-
-
-def call(kernel, out_shape, scalars, arrays, flops, limit, scratch=()):
+    chunk = step // 4
+    copies = []
+    for number in range(4):
+        cut = slice(number * chunk, (number + 1) * chunk)
+        for near_ref, far_ref, low, high in (
+            (near_a_ref, far_a_ref, 0, edge),
+            (near_b_ref, far_b_ref, edge, model),
+        ):
+            total = (
+                own_ref[cut, low:high]
+                + near_ref[cut, :].astype(F32)
+                + far_ref[cut, :].astype(F32)
+            )
+            out_ref[cut, low:high] = (total * scale[cut, :]).astype(BF16)
+        here = pl.ds(number * chunk, chunk)
+        copy = pltpu.make_async_copy(out_ref.at[here, :], out_hbm.at[here, :], left.at[number])
+        copy.start()
+        copies.append(copy)
+    for copy in copies:
+        copy.wait()
+
+
+def call(kernel, out_shape, scalars, arrays, flops, limit, scratch=(), space=VMEM_SPEC, result=VMEM_SPEC):
     single = not isinstance(out_shape, (tuple, list))
-    space = HBM_SPEC if scratch else VMEM_SPEC
     return pl.pallas_call(
         kernel,
         out_shape=out_shape,
         in_specs=[SMEM_SPEC] * len(scalars) + [space] * len(arrays),
-        out_specs=VMEM_SPEC if single else [VMEM_SPEC] * len(out_shape),
+        out_specs=result if single else [result] * len(out_shape),
         scratch_shapes=scratch,
         cost_estimate=pl.CostEstimate(flops=flops, bytes_accessed=4_000_000, transcendentals=0),
         compiler_params=pltpu.CompilerParams(vmem_limit_bytes=int(limit * 1024**2)),
@@ -450,10 +472,11 @@
     starts = doc_starts[None, :]
     shape = jax.ShapeDtypeStruct
     arrays = [stream, in_coeff, step_raw, step_bias[None], decay_rate[None], starts]
-    summary, into, factor = call(
+    summary, first, into, factor = call(
         functools.partial(state_kernel, head_size),
         [
             shape((states, width + LANES), BF16),
+            shape((states, width), BF16),
             shape((2 * PAD, rows + LANES), BF16),
             shape((2 * PAD, rows + LANES), BF16),
         ],
@@ -462,13 +485,15 @@
         2_000_000_000,
         FULL,
         [pltpu.VMEM(a.shape, a.dtype) for a in arrays] + [pltpu.SemaphoreType.DMA((len(arrays),))],
+        HBM_SPEC,
     )
     other = lax.ppermute(summary, "seq_2", [(0, 1), (1, 0)])
+    own = call(pass_kernel, shape(summary.shape, BF16), [], [summary], 100_000_000, 4)
     pieces = call(
         functools.partial(combine_kernel, head_size),
         shape((chips, states // chips, width // 2 + LANES), BF16),
         [core],
-        [summary, other],
+        [own, other],
         200_000_000,
         8,
     )
@@ -483,33 +508,47 @@
     )
     incoming = lax.all_to_all(prior, CHIPS, 0, 0, tiled=True)
     incoming_other = lax.ppermute(incoming, "seq_2", [(0, 1), (1, 0)])
-    base, slope, first = call(
-        functools.partial(within_kernel, head_size),
+    step = rows // 4
+    edge = model * 11 // 20
+    rest = model - edge
+    tokens = [
+        stream,
+        gate_input,
+        in_coeff,
+        out_coeff,
+        into,
+        factor,
+        skip_scale[None],
+        starts,
+    ]
+    base, slope, joined = call(
+        functools.partial(ahead_kernel, head_size),
+        [shape((step, width), F32), shape((step, width), F32), shape((step, states), BF16)],
+        [offset, y],
+        tokens,
+        2_000_000_000,
+        16,
+    )
+    send_a, send_b, ready = call(
+        functools.partial(far_kernel, head_size),
         [
-            shape((rows, width), F32),
-            shape((rows, width), F32),
-            shape((states, width), F32),
+            shape((step + 8, edge), BF16),
+            shape((step, rest), BF16),
+            shape((2 * states, width), BF16),
         ],
-        [offset],
-        [stream, gate_input, in_coeff, out_coeff, into, factor, skip_scale[None], starts],
-        4_000_000_000,
-        22,
-    )
-    step = rows // 4
-    half = model // 2
-    hidden, squares = call(
-        functools.partial(finish_kernel, head_size),
-        [shape((rows, width), BF16), shape((4, step), F32)],
-        [offset, core],
-        [out_coeff, incoming, incoming_other, other, first, factor, base, slope, norm_gain, starts],
-        1_000_000_000,
-        22,
-    )
-    send_a, send_b = call(
-        far_kernel,
-        [shape((step + 8, half), BF16), shape((step, half), BF16)],
-        [y],
-        [hidden, out_proj, squares],
+        [y, core],
+        [
+            incoming,
+            incoming_other,
+            other,
+            first,
+            factor,
+            base,
+            slope,
+            joined,
+            norm_gain,
+            out_proj,
+        ],
         1_000_000_000,
         16,
     )
@@ -517,29 +556,39 @@
     pair_3 = [(i, i ^ 3) for i in range(4)]
     got_a = lax.ppermute(send_a, "head", pair_1)
     got_b = lax.ppermute(send_b, "head", pair_3)
-    send_a, send_b = call(
-        near_kernel,
-        [shape((step + 8, half), BF16), shape((step, half), BF16)],
-        [y],
-        [hidden, out_proj, squares],
-        1_000_000_000,
-        16,
+    send_a, send_b, hidden, via_squares = call(
+        functools.partial(near_kernel, head_size),
+        [
+            shape((step + 8, edge), BF16),
+            shape((step, rest), BF16),
+            shape((2 * step, width), BF16),
+            shape((1, step), F32),
+        ],
+        [offset, y],
+        [ready, norm_gain, out_proj] + tokens,
+        2_000_000_000,
+        20,
     )
     near_a = lax.ppermute(send_a, "head", pair_1)
     near_b = lax.ppermute(send_b, "head", pair_3)
-    own, via_a, via_b = call(
-        keep_kernel,
-        [shape((step, model), F32), shape((step, half), F32), shape((step, half), F32)],
-        [y],
-        [hidden, out_proj],
+    own, via_a, via_b, squares = call(
+        functools.partial(keep_kernel, head_size),
+        [
+            shape((step, model), F32),
+            shape((step, edge), F32),
+            shape((step, rest), F32),
+            shape((1, step), F32),
+        ],
+        [offset, y],
+        [ready, norm_gain, out_proj, hidden] + tokens,
         2_000_000_000,
-        16,
+        20,
     )
     send_a, send_b = call(
         middle_kernel,
-        [shape((step + 8, half), BF16), shape((step, half), BF16)],
-        [y],
-        [squares, via_a, via_b, got_a, got_b],
+        [shape((step + 8, edge), BF16), shape((step, rest), BF16)],
+        [],
+        [via_squares, via_a, via_b, got_a, got_b],
         1_000_000_000,
         8,
     )
@@ -548,10 +597,13 @@
     return call(
         functools.partial(last_kernel, total_channels),
         shape((step, model), BF16),
-        [y],
+        [],
         [squares, own, near_a, near_b, far_a, far_b],
         1_000_000_000,
         8,
+        [pltpu.VMEM((step, model), BF16), pltpu.SemaphoreType.DMA((4,))],
+        VMEM_SPEC,
+        HBM_SPEC,
     )
 
 

time: 81.1 us -> 77.6 us (0.957)
  the two profiles are of different devices: /device:TPU:1 before, /device:TPU:8 now
where the time goes in v4:
time: 77.6 us; the launch traced here: 76.3 us
  blocking collectives  37.8 us (49%)
  waiting for transfers between devices  14.8 us (19%)
  Pallas kernels  13.8 us (18%)
  starting transfers between devices  8.44 us (11%)
  local copies, waits for them, and re-layouts  1.04 us (1%)
    all_to_all x1, blocking collectives, local(): pieces = lax.all_to_all(pieces, CHIPS, 0, 0, tiled=True)  23 us
    all_to_all x1, blocking collectives, local(): incoming = lax.all_to_all(prior, CHIPS, 0, 0, tiled=True)  14.8 us
    pallas_call x10, Pallas kernels, call(): pl.pallas_call(kernel, out_shape=out_shape, in_specs=[SMEM_SPEC] * len(sc...  13.8 us
    ppermute x1, waiting for transfers between devices, local(): near_b = lax.ppermute(send_b, 'head', pair_3)  12 us
    ppermute x1, starting transfers between devices, local(): got_b = lax.ppermute(send_b, 'head', pair_3)  2.41 us
    ppermute x1, starting transfers between devices, local(): far_a = lax.ppermute(send_a, 'head', pair_3)  1.66 us
    ppermute x1, starting transfers between devices, local(): far_b = lax.ppermute(send_b, 'head', pair_1)  1.66 us
    ppermute x1, starting transfers between devices, local(): near_a = lax.ppermute(send_a, 'head', pair_1)  1.63 us
  transfers between devices with their start and end apart: 8, of which 4 were waited for; matrix products, arithmetic and copies ran while one was open for 0% of the time, Pallas kernels for 9%

profile of v4, /device:TPU:8, one launch (start us, length us, event | category | flops | bytes accessed | tf_op | source)
XLA Modules:
  0.0 76.3 jit_solution(8666908872554702703)
XLA Ops:
  0.0 3.4 %shard_map.109 = (bf16[128,1408]{1,0:T(8,128)(2,1)}, bf16[128,1280]{1,0:T(8,128)(2,1)}, bf16[64,640]{1,0:T(8,128)(2,1)}, bf16[64,640]{1,0:T(8,128)(2,1)}) custom-call(s32[1]{0:T(128)} %bitcast.offset_ref, s32[1]{0:T(128)} %bitcast.1.y_ref, s32[1]{0:T(128)} %bitcast.2.core_ref, bf16[512,1280]{1,0:T(8,128)(2,1)} %refs_0_.5, bf16[512,128]{1,0:T(8,128)(2,1)} %refs_2_.5, ...), custom_call_target="tpu_custom_call" | custom-call | flops 2000000000 | bytes 4000000 | tf_op jit(solution)/shard_map/pallas_call | solution.py:438
  3.4 0.1 collective-permute-start
  3.5 1.0 %copy-done.5 = bf16[128,1408]{1,0:T(8,128)(2,1)S(1)} copy-done((bf16[128,1408]{1,0:T(8,128)(2,1)S(1)}, bf16[128,1408]{1,0:T(8,128)(2,1)}, u32[]{:S(2)}) %copy-start.5) | copy-done | bytes 360472
  4.5 0.9 %collective-permute-done.other_ref = bf16[128,1408]{1,0:T(8,128)(2,1)S(1)} collective-permute-done((bf16[128,1408]{1,0:T(8,128)(2,1)}, bf16[128,1408]{1,0:T(8,128)(2,1)S(1)}, u32[]{:S(2)}, u32[]{:S(2)}) %collective-permute-start) | collective-permute-done | bytes 360480 | tf_op jit(solution)/shard_map/ppermute | solution.py:490
  5.4 0.3 shard_map.111
  5.6 23.0 %all_to_all.10.pieces_ref = bf16[32,4,768]{2,1,0:T(4,128)(2,1)S(1)} all-to-all(bf16[32,4,768]{2,1,0:T(4,128)(2,1)S(1)} %shard_map.111), channel_id=1, replica_groups=mesh['seq_0'=4,'seq_1'=8,'seq_2'=2,'head'=4] {'seq_0','seq_1'}, dimensions={0} | all-to-all | bytes 393216 | tf_op jit(solution)/shard_map/all_to_all | solution.py:500
  28.7 0.0 copy-start.4
  28.7 0.0 copy-start.9
  28.7 0.0 copy-start.10
  28.7 0.0 slice-start.1
  28.8 0.3 shard_map.112
  29.0 14.8 %all_to_all.11.before_ref = bf16[32,4,640]{2,1,0:T(4,128)(2,1)S(1)} all-to-all(bf16[32,4,640]{2,1,0:T(4,128)(2,1)S(1)} %shard_map.112), channel_id=1, replica_groups=mesh['seq_0'=4,'seq_1'=8,'seq_2'=2,'head'=4] {'seq_0','seq_1'}, dimensions={0} | all-to-all | bytes 327680 | tf_op jit(solution)/shard_map/all_to_all | solution.py:509
  43.8 0.0 collective-permute-start.1
  43.9 0.0 copy-start.8
  43.9 1.0 %shard_map.113 = (f32[128,1280]{1,0:T(8,128)S(1)}, f32[128,1280]{1,0:T(8,128)S(1)}, bf16[128,128]{1,0:T(8,128)(2,1)S(1)}) custom-call(s32[1]{0:T(128)} %bitcast.offset_ref, s32[1]{0:T(128)} %bitcast.1.y_ref, bf16[512,1280]{1,0:T(8,128)(2,1)S(1)} %copy-done, bf16[512,1280]{1,0:T(8,128)(2,1)S(1)} %copy-done.1, bf16[512,128]{1,0:T(8,128)(2,1)S(1)} %copy-done.3, ...), custom_call_target="tpu_custom_call" | custom-call | flops 2000000000 | bytes 4000000 | tf_op jit(solution)/shard_map/pallas_call | solution.py:438
  44.9 0.3 collective-permute-done.1.before_other_ref
  45.2 2.1 %shard_map.114 = (bf16[136,1408]{1,0:T(8,128)(2,1)S(1)}, bf16[128,1152]{1,0:T(8,128)(2,1)S(1)}, bf16[256,1280]{1,0:T(8,128)(2,1)S(1)}) custom-call(s32[1]{0:T(128)} %bitcast.1.y_ref, s32[1]{0:T(128)} %bitcast.2.core_ref, bf16[32,4,640]{2,1,0:T(4,128)(2,1)S(1)} %all_to_all.11.before_ref, bf16[32,4,640]{2,1,0:T(4,128)(2,1)S(1)} %collective-permute-done.1.before_other_ref, ...), custom_call_target="tpu_custom_call" | custom-call | flops 1000000000 | bytes 4000000 | tf_op jit(solution)/shard_map/pallas_call | solution.py:438
  47.3 0.5 collective-permute-start.4
  47.8 2.4 %collective-permute-start.5 = (bf16[128,1152]{1,0:T(8,128)(2,1)S(1)}, bf16[128,1152]{1,0:T(8,128)(2,1)S(1)}, u32[]{:S(2)}, u32[]{:S(2)}) collective-permute-start(bf16[128,1152]{1,0:T(8,128)(2,1)S(1)} %get-tuple-element.42), channel_id=1, source_target_pairs={{0,3},{1,2},{2,1},{3,0},{4,7},{5,6},{6,5},{7,4},{8,11},{9,10},{10,... | collective-permute-start | bytes 884744 | tf_op jit(solution)/shard_map/ppermute | solution.py:558
  50.2 3.0 %shard_map.115 = (bf16[136,1408]{1,0:T(8,128)(2,1)S(1)}, bf16[128,1152]{1,0:T(8,128)(2,1)S(1)}, bf16[256,1280]{1,0:T(8,128)(2,1)S(1)}, f32[1,128]{1,0:T(1,128)S(1)}) custom-call(s32[1]{0:T(128)} %bitcast.offset_ref, s32[1]{0:T(128)} %bitcast.1.y_ref, bf16[256,1280]{1,0:T(8,128)(2,1)S(1)} %get-tuple-element.32.states_ref, f32[1280]{0:T(1024)S(1)} %copy-done.8, ...), custom_call_target="tpu_custom_call" | custom-call | flops 2000000000 | bytes 4000000 | tf_op jit(solution)/shard_map/pallas_call | solution.py:438
  53.2 1.6 %collective-permute-start.2 = (bf16[136,1408]{1,0:T(8,128)(2,1)S(1)}, bf16[136,1408]{1,0:T(8,128)(2,1)S(1)}, u32[]{:S(2)}, u32[]{:S(2)}) collective-permute-start(bf16[136,1408]{1,0:T(8,128)(2,1)S(1)} %get-tuple-element.36), channel_id=1, source_target_pairs={{0,1},{1,0},{2,3},{3,2},{4,5},{5,4},{6,7},{7,6},{8,9},{9,8},{10,11... | collective-permute-start | bytes 1148936 | tf_op jit(solution)/shard_map/ppermute | solution.py:572
  54.8 2.8 %shard_map.116 = (f32[128,2560]{1,0:T(8,128)S(1)}, f32[128,1408]{1,0:T(8,128)S(1)}, f32[128,1152]{1,0:T(8,128)S(1)}, f32[1,128]{1,0:T(1,128)S(1)}) custom-call(s32[1]{0:T(128)} %bitcast.offset_ref, s32[1]{0:T(128)} %bitcast.1.y_ref, bf16[256,1280]{1,0:T(8,128)(2,1)S(1)} %get-tuple-element.32.states_ref, f32[1280]{0:T(1024)S(1)} %copy-done.8, ...), custom_call_target="tpu_custom_call" | custom-call | flops 2000000000 | bytes 4000000 | tf_op jit(solution)/shard_map/pallas_call | solution.py:438
  57.6 0.0 collective-permute-done.5.got_b_ref
  57.6 1.6 %collective-permute-done.4.got_a_ref = bf16[136,1408]{1,0:T(8,128)(2,1)S(1)} collective-permute-done((bf16[136,1408]{1,0:T(8,128)(2,1)S(1)}, bf16[136,1408]{1,0:T(8,128)(2,1)S(1)}, u32[]{:S(2)}, u32[]{:S(2)}) %collective-permute-start.4) | collective-permute-done | bytes 383008 | tf_op jit(solution)/shard_map/ppermute | solution.py:557
  59.1 0.1 shard_map.117
  59.3 1.7 %collective-permute-start.6 = (bf16[136,1408]{1,0:T(8,128)(2,1)S(1)}, bf16[136,1408]{1,0:T(8,128)(2,1)S(1)}, u32[]{:S(2)}, u32[]{:S(2)}) collective-permute-start(bf16[136,1408]{1,0:T(8,128)(2,1)S(1)} %get-tuple-element.43), channel_id=1, source_target_pairs={{0,3},{1,2},{2,1},{3,0},{4,7},{5,6},{6,5},{7,4},{8,11},{9,10},{10,... | collective-permute-start | bytes 1148936 | tf_op jit(solution)/shard_map/ppermute | solution.py:595
  60.9 0.5 collective-permute-start.3
  61.4 1.7 %collective-permute-start.7 = (bf16[128,1152]{1,0:T(8,128)(2,1)S(1)}, bf16[128,1152]{1,0:T(8,128)(2,1)S(1)}, u32[]{:S(2)}, u32[]{:S(2)}) collective-permute-start(bf16[128,1152]{1,0:T(8,128)(2,1)S(1)} %get-tuple-element.44), channel_id=1, source_target_pairs={{0,1},{1,0},{2,3},{3,2},{4,5},{5,4},{6,7},{7,6},{8,9},{9,8},{10,11... | collective-permute-start | bytes 884744 | tf_op jit(solution)/shard_map/ppermute | solution.py:596
  63.1 12.0 %collective-permute-done.3.near_b_ref = bf16[128,1152]{1,0:T(8,128)(2,1)S(1)} collective-permute-done((bf16[128,1152]{1,0:T(8,128)(2,1)S(1)}, bf16[128,1152]{1,0:T(8,128)(2,1)S(1)}, u32[]{:S(2)}, u32[]{:S(2)}) %collective-permute-start.3) | collective-permute-done | bytes 294944 | tf_op jit(solution)/shard_map/ppermute | solution.py:573
  75.1 0.0 collective-permute-done.2.near_a_ref
  75.1 0.0 collective-permute-done.7.far_b_ref
  75.1 1.0 %shard_map.118 = bf16[128,2560]{1,0:T(8,128)(2,1)} custom-call(f32[1,128]{1,0:T(1,128)S(1)} %get-tuple-element.34.squares_ref, f32[128,2560]{1,0:T(8,128)S(1)} %get-tuple-element.35.own_ref, bf16[136,1408]{1,0:T(8,128)(2,1)S(1)} %collective-permute-done.2.near_a_ref, bf16[128,1152]{1,0:T(8,128)(2,1)S(1)} %collective-permute-done.3.near_b_ref, ...), custom_call_target="tpu_custom_call" | custom-call | flops 1000000000 | bytes 4000000 | tf_op jit(solution)/shard_map/pallas_call | solution.py:438
  (23 shorter events, 0.1 us)
Async XLA Ops:
  3.4 2.0 %collective-permute-start = (bf16[128,1408]{1,0:T(8,128)(2,1)}, bf16[128,1408]{1,0:T(8,128)(2,1)S(1)}, u32[]{:S(2)}, u32[]{:S(2)}) collective-permute-start(bf16[128,1408]{1,0:T(8,128)(2,1)} %get-tuple-element.25.from_ref), channel_id=1, source_target_pairs={{0,4},{4,0},{1,5},{5,1},{2,6},{6,2},{3,7},{7,3},{8,12},{12,8},{9,1... | collective-permute-start | bytes 1081352 | tf_op jit(solution)/shard_map/ppermute | solution.py:490
  3.5 1.0 %copy-start.5 = (bf16[128,1408]{1,0:T(8,128)(2,1)S(1)}, bf16[128,1408]{1,0:T(8,128)(2,1)}, u32[]{:S(2)}) copy-start(bf16[128,1408]{1,0:T(8,128)(2,1)} %get-tuple-element.25.from_ref) | copy-start | bytes 1081348
  5.4 39.8 %slice-start = ((s8[6553600]{0:T(1024)(128)(4,1)}), s8[4194304]{0:T(1024)(128)(4,1)S(1)}, s32[]{:S(2)}) async-start(s8[6553600]{0:T(1024)(128)(4,1)} %bitcast.7), calls=%async_computation.2 | async-start | bytes 8388608
  28.7 15.1 %copy-start = (bf16[512,1280]{1,0:T(8,128)(2,1)S(1)}, bf16[512,1280]{1,0:T(8,128)(2,1)}, u32[]{:S(2)}) copy-start(bf16[512,1280]{1,0:T(8,128)(2,1)} %refs_0_.5) | copy-start | bytes 3932164
  28.7 15.1 %copy-start.1 = (bf16[512,1280]{1,0:T(8,128)(2,1)S(1)}, bf16[512,1280]{1,0:T(8,128)(2,1)}, u32[]{:S(2)}) copy-start(bf16[512,1280]{1,0:T(8,128)(2,1)} %refs_1_.5) | copy-start | bytes 3932164
  28.7 15.1 %copy-start.2 = (bf16[64,640]{1,0:T(8,128)(2,1)S(1)}, bf16[64,640]{1,0:T(8,128)(2,1)}, u32[]{:S(2)}) copy-start(bf16[64,640]{1,0:T(8,128)(2,1)} %get-tuple-element.27.refs_5_.factor_ref) | copy-start | bytes 245764
  28.7 15.1 %copy-start.3 = (bf16[512,128]{1,0:T(8,128)(2,1)S(1)}, bf16[512,128]{1,0:T(8,128)(2,1)}, u32[]{:S(2)}) copy-start(bf16[512,128]{1,0:T(8,128)(2,1)} %refs_2_.5) | copy-start | bytes 393220
  28.7 15.1 %copy-start.4 = (bf16[512,128]{1,0:T(8,128)(2,1)S(1)}, bf16[512,128]{1,0:T(8,128)(2,1)}, u32[]{:S(2)}) copy-start(bf16[512,128]{1,0:T(8,128)(2,1)} %refs_3_.5) | copy-start | bytes 393220
  28.7 15.1 %copy-start.6 = (bf16[64,640]{1,0:T(8,128)(2,1)S(1)}, bf16[64,640]{1,0:T(8,128)(2,1)}, u32[]{:S(2)}) copy-start(bf16[64,640]{1,0:T(8,128)(2,1)} %get-tuple-element.28.refs_4_) | copy-start | bytes 245764
  28.7 15.1 %copy-start.9 = (s32[128]{0:T(128)S(1)}, s32[128]{0:T(128)}, u32[]{:S(2)}) copy-start(s32[128]{0:T(128)} %param.21) | copy-start | bytes 1540
  28.7 15.1 %copy-start.10 = (f32[20]{0:T(128)S(1)}, f32[20]{0:T(128)}, u32[]{:S(2)}) copy-start(f32[20]{0:T(128)} %param.18) | copy-start | bytes 244
  28.7 16.5 %slice-start.1 = ((s8[6553600]{0:T(1024)(128)(4,1)}), s8[2359296]{0:T(1024)(128)(4,1)S(1)}, s32[]{:S(2)}) async-start(s8[6553600]{0:T(1024)(128)(4,1)} %bitcast.7), calls=%async_computation.3 | async-start | bytes 4718592
  43.8 1.4 %collective-permute-start.1 = (bf16[32,4,640]{2,1,0:T(4,128)(2,1)S(1)}, bf16[32,4,640]{2,1,0:T(4,128)(2,1)S(1)}, u32[]{:S(2)}, u32[]{:S(2)}) collective-permute-start(bf16[32,4,640]{2,1,0:T(4,128)(2,1)S(1)} %all_to_all.11.before_ref), channel_id=1, source_target_pairs={{0,4},{4,0},{1,5},{5,1},{2,6},{6,2},{3,7},{7,3},{8,12},{12,8},{9,1... | collective-permute-start | bytes 491528 | tf_op jit(solution)/shard_map/ppermute | solution.py:510
  43.9 1.3 %copy-start.7 = (bf16[128,1280]{1,0:T(8,128)(2,1)S(1)}, bf16[128,1280]{1,0:T(8,128)(2,1)}, u32[]{:S(2)}) copy-start(bf16[128,1280]{1,0:T(8,128)(2,1)} %get-tuple-element.26.first_ref) | copy-start | bytes 983044
  43.9 1.3 %copy-start.8 = (f32[1280]{0:T(1024)S(1)}, f32[1280]{0:T(1024)}, u32[]{:S(2)}) copy-start(f32[1280]{0:T(1024)} %gain_ref.5) | copy-start | bytes 15364
  47.3 11.9 %collective-permute-start.4 = (bf16[136,1408]{1,0:T(8,128)(2,1)S(1)}, bf16[136,1408]{1,0:T(8,128)(2,1)S(1)}, u32[]{:S(2)}, u32[]{:S(2)}) collective-permute-start(bf16[136,1408]{1,0:T(8,128)(2,1)S(1)} %get-tuple-element.41), channel_id=1, source_target_pairs={{0,1},{1,0},{2,3},{3,2},{4,5},{5,4},{6,7},{7,6},{8,9},{9,8},{10,11... | collective-permute-start | bytes 1148936 | tf_op jit(solution)/shard_map/ppermute | solution.py:557
  47.8 9.8 %collective-permute-start.5 = (bf16[128,1152]{1,0:T(8,128)(2,1)S(1)}, bf16[128,1152]{1,0:T(8,128)(2,1)S(1)}, u32[]{:S(2)}, u32[]{:S(2)}) collective-permute-start(bf16[128,1152]{1,0:T(8,128)(2,1)S(1)} %get-tuple-element.42), channel_id=1, source_target_pairs={{0,3},{1,2},{2,1},{3,0},{4,7},{5,6},{6,5},{7,4},{8,11},{9,10},{10,... | collective-permute-start | bytes 884744 | tf_op jit(solution)/shard_map/ppermute | solution.py:558
  53.2 21.9 %collective-permute-start.2 = (bf16[136,1408]{1,0:T(8,128)(2,1)S(1)}, bf16[136,1408]{1,0:T(8,128)(2,1)S(1)}, u32[]{:S(2)}, u32[]{:S(2)}) collective-permute-start(bf16[136,1408]{1,0:T(8,128)(2,1)S(1)} %get-tuple-element.36), channel_id=1, source_target_pairs={{0,1},{1,0},{2,3},{3,2},{4,5},{5,4},{6,7},{7,6},{8,9},{9,8},{10,11... | collective-permute-start | bytes 1148936 | tf_op jit(solution)/shard_map/ppermute | solution.py:572
  59.3 15.8 %collective-permute-start.6 = (bf16[136,1408]{1,0:T(8,128)(2,1)S(1)}, bf16[136,1408]{1,0:T(8,128)(2,1)S(1)}, u32[]{:S(2)}, u32[]{:S(2)}) collective-permute-start(bf16[136,1408]{1,0:T(8,128)(2,1)S(1)} %get-tuple-element.43), channel_id=1, source_target_pairs={{0,3},{1,2},{2,1},{3,0},{4,7},{5,6},{6,5},{7,4},{8,11},{9,10},{10,... | collective-permute-start | bytes 1148936 | tf_op jit(solution)/shard_map/ppermute | solution.py:595
  60.9 14.1 %collective-permute-start.3 = (bf16[128,1152]{1,0:T(8,128)(2,1)S(1)}, bf16[128,1152]{1,0:T(8,128)(2,1)S(1)}, u32[]{:S(2)}, u32[]{:S(2)}) collective-permute-start(bf16[128,1152]{1,0:T(8,128)(2,1)S(1)} %get-tuple-element.37), channel_id=1, source_target_pairs={{0,3},{1,2},{2,1},{3,0},{4,7},{5,6},{6,5},{7,4},{8,11},{9,10},{10,... | collective-permute-start | bytes 884744 | tf_op jit(solution)/shard_map/ppermute | solution.py:573
  61.4 13.7 %collective-permute-start.7 = (bf16[128,1152]{1,0:T(8,128)(2,1)S(1)}, bf16[128,1152]{1,0:T(8,128)(2,1)S(1)}, u32[]{:S(2)}, u32[]{:S(2)}) collective-permute-start(bf16[128,1152]{1,0:T(8,128)(2,1)S(1)} %get-tuple-element.44), channel_id=1, source_target_pairs={{0,1},{1,0},{2,3},{3,2},{4,5},{5,4},{6,7},{7,6},{8,9},{9,8},{10,11... | collective-permute-start | bytes 884744 | tf_op jit(solution)/shard_map/ppermute | solution.py:596

commit v5 on v4

--- a/solution.py
+++ b/solution.py
@@ -17,7 +17,6 @@
 BF16 = jnp.bfloat16
 PAD = 32
 LANES = 128
-FULL = 67_043_328 / 1024**2
 
 VMEM_SPEC = pl.BlockSpec(memory_space=pltpu.VMEM)
 SMEM_SPEC = pl.BlockSpec(memory_space=pltpu.SMEM)
@@ -114,10 +113,14 @@
     ]
     for copy in copies:
         copy.start()
+    heads, rows = step_ref.shape
+    width = stream_ref.shape[1]
+    spread = head_lanes(width, head_size)
+    i = lax.broadcasted_iota(jnp.int32, (BLOCK, BLOCK), 0)
+    j = lax.broadcasted_iota(jnp.int32, (BLOCK, BLOCK), 1)
+    upper = jnp.where(i <= j, 1.0, 0.0)
     for copy in copies[:4]:
         copy.wait()
-    heads, rows = step_ref.shape
-    width = stream_ref.shape[1]
     offset = offset_ref[0]
     starts = starts_ref[...]
     docs = docs_column(starts, offset, rows)
@@ -125,9 +128,6 @@
     raw = step_ref[...] + as_column(bias_ref[...], heads)
     step = jnp.maximum(raw, 0.0) + jnp.log1p(jnp.exp(-jnp.abs(raw)))
     log_decay = -step * as_column(rate_ref[...], heads)
-    i = lax.broadcasted_iota(jnp.int32, (BLOCK, BLOCK), 0)
-    j = lax.broadcasted_iota(jnp.int32, (BLOCK, BLOCK), 1)
-    upper = jnp.where(i <= j, 1.0, 0.0)
     into, out_of, half, last = [], [], [], []
     for block in range(rows // BLOCK):
         cut = slice(block * BLOCK, (block + 1) * BLOCK)
@@ -152,7 +152,6 @@
     constants = jnp.where(lane == 2, gate_0, constants)
     constants = jnp.where(lane == 3, gate_1, constants)
     nothing = jnp.zeros((PAD - heads, rows + LANES), F32)
-    spread = head_lanes(width, head_size)
     wide_in = jnp.concatenate([jnp.concatenate(into + [constants], axis=1), nothing], axis=0)
     wide_out = jnp.concatenate([jnp.concatenate(out_of + [constants], axis=1), nothing], axis=0)
     factor_ref[...] = two_parts(wide_out)
@@ -232,15 +231,15 @@
     return (gated * gain).astype(BF16), jnp.sum(jnp.transpose(total), axis=0, keepdims=True)
 
 
-def ahead_kernel(head_size, offset_ref, y_ref, *refs):
-    base_ref, slope_ref, joined_ref = refs[-3:]
+def ahead_kernel(head_size, offset_ref, y_ref, other_ref, *refs):
+    base_ref, slope_ref, joined_ref, lanes_ref = refs[-4:]
     base_ref[...], slope_ref[...], joined_ref[...] = block_terms(
-        head_size, offset_ref[0], y_ref[0] ^ 2, *refs[:-3]
-    )
-
-
-def pass_kernel(from_ref, to_ref):
-    to_ref[...] = from_ref[...]
+        head_size, offset_ref[0], y_ref[0] ^ 2, *refs[:-4]
+    )
+    rows, width = refs[0].shape
+    factor_ref = refs[5]
+    lanes_ref[:8, :] = dot_first(factor_ref[:, rows:], head_lanes(width, head_size))[:8, :]
+    lanes_ref[8:, :] = link_lanes(other_ref[:8, width:], width, head_size)
 
 
 def link_lanes(links, width, head_size):
@@ -312,35 +311,33 @@
 
 
 def far_kernel(
-    head_size,
     y_ref,
     core_ref,
     before_ref,
     before_other_ref,
     other_ref,
     first_ref,
-    factor_ref,
+    lanes_ref,
     base_ref,
     slope_ref,
     joined_ref,
     gain_ref,
     proj_ref,
     send_a_ref,
-    send_b_ref,
+    hidden_ref,
     states_ref,
+    squares_ref,
 ):
     width = base_ref.shape[1]
     states = other_ref.shape[0]
-    rows = factor_ref.shape[1] - LANES
-    spread = head_lanes(width, head_size)
-    constant_rows = dot_first(factor_ref[:, rows:], spread)[:8, :]
+    constant_rows = lanes_ref[:8, :]
     first_core = core_ref[0] == 0
     half_a = before_ref[...].reshape(states, width // 2).astype(F32)
     half_b = before_other_ref[...].reshape(states, width // 2).astype(F32)
     state = jnp.concatenate(
         [jnp.where(first_core, half_a, half_b), jnp.where(first_core, half_b, half_a)], axis=1
     )
-    rate = link_lanes(other_ref[:8, width:], width, head_size)[:1, :]
+    rate = lanes_ref[8:9, :]
     state = jnp.where(first_core, state, rate * state + other_ref[:, :width].astype(F32))
     states_ref[:states, :] = (constant_rows[:1, :] * state).astype(BF16)
     state = constant_rows[2:3, :] * state + first_ref[...].astype(F32)
@@ -352,9 +349,15 @@
         state_of(states_ref, y_ref[0] ^ 2),
         gain_ref[...].reshape(1, width),
     )
-    low = send_b_ref.shape[1]
-    send_b_ref[...] = dot(piece, proj_ref[:, -low:]).astype(BF16)
-    send_a_ref[...] = with_squares(dot(piece, proj_ref[:, :-low]), squares)
+    hidden_ref[...] = piece
+    squares_ref[...] = squares
+    send_a_ref[...] = dot(piece, proj_ref[:, : send_a_ref.shape[1]]).astype(BF16)
+
+
+def far_b_kernel(hidden_ref, proj_ref, squares_ref, send_b_ref):
+    send_b_ref[...] = with_squares(
+        dot(hidden_ref[...], proj_ref[:, -send_b_ref.shape[1] :]), squares_ref[...]
+    )
 
 
 def near_kernel(head_size, offset_ref, y_ref, states_ref, gain_ref, proj_ref, *refs):
@@ -367,10 +370,10 @@
         piece, squares = block_hidden(*terms, state_of(states_ref, block), gain)
         hidden_ref[number * step : (number + 1) * step, :] = piece
         if number == 0:
-            send_b_ref[...] = dot(piece, proj_ref[:, -low:]).astype(BF16)
+            send_b_ref[...] = with_squares(dot(piece, proj_ref[:, -low:]), squares)
+        else:
+            send_a_ref[...] = dot(piece, proj_ref[:, :-low]).astype(BF16)
             squares_ref[...] = squares
-        else:
-            send_a_ref[...] = with_squares(dot(piece, proj_ref[:, :-low]), squares)
 
 
 def keep_kernel(head_size, offset_ref, y_ref, states_ref, gain_ref, proj_ref, hidden_ref, *refs):
@@ -389,9 +392,9 @@
 
 def middle_kernel(squares_ref, via_a_ref, via_b_ref, got_a_ref, got_b_ref, send_a_ref, send_b_ref):
     step = via_a_ref.shape[0]
-    squares = squares_ref[...] + squares_of(got_a_ref, step)
-    send_a_ref[...] = with_squares(via_a_ref[...] + got_a_ref[:step, :].astype(F32), squares)
-    send_b_ref[...] = (via_b_ref[...] + got_b_ref[...].astype(F32)).astype(BF16)
+    squares = squares_ref[...] + squares_of(got_b_ref, step)
+    send_a_ref[...] = (via_a_ref[...] + got_a_ref[...].astype(F32)).astype(BF16)
+    send_b_ref[...] = with_squares(via_b_ref[...] + got_b_ref[:step, :].astype(F32), squares)
 
 
 def last_kernel(
@@ -409,7 +412,7 @@
     step, model = own_ref.shape
     edge = near_a_ref.shape[1]
     squares = squares_ref[...]
-    squares = squares + squares_of(near_a_ref, step) + squares_of(far_a_ref, step)
+    squares = squares + squares_of(near_b_ref, step) + squares_of(far_b_ref, step)
     scale = as_column(lax.rsqrt(squares / channels + EPSILON), step)
     chunk = step // 4
     copies = []
@@ -471,7 +474,10 @@
     offset = (lax.axis_index(SEQ) * rows).astype(jnp.int32)[None]
     starts = doc_starts[None, :]
     shape = jax.ShapeDtypeStruct
-    arrays = [stream, in_coeff, step_raw, step_bias[None], decay_rate[None], starts]
+    arrays = [
+        pltpu.with_memory_space_constraint(a, pltpu.HBM)
+        for a in (stream, in_coeff, step_raw, step_bias[None], decay_rate[None], starts)
+    ]
     summary, first, into, factor = call(
         functools.partial(state_kernel, head_size),
         [
@@ -483,17 +489,16 @@
         [offset, y, core],
         arrays,
         2_000_000_000,
-        FULL,
+        24,
         [pltpu.VMEM(a.shape, a.dtype) for a in arrays] + [pltpu.SemaphoreType.DMA((len(arrays),))],
         HBM_SPEC,
     )
     other = lax.ppermute(summary, "seq_2", [(0, 1), (1, 0)])
-    own = call(pass_kernel, shape(summary.shape, BF16), [], [summary], 100_000_000, 4)
     pieces = call(
         functools.partial(combine_kernel, head_size),
         shape((chips, states // chips, width // 2 + LANES), BF16),
         [core],
-        [own, other],
+        [summary, other],
         200_000_000,
         8,
     )
@@ -509,7 +514,7 @@
     incoming = lax.all_to_all(prior, CHIPS, 0, 0, tiled=True)
     incoming_other = lax.ppermute(incoming, "seq_2", [(0, 1), (1, 0)])
     step = rows // 4
-    edge = model * 11 // 20
+    edge = model * 12 // 20
     rest = model - edge
     tokens = [
         stream,
@@ -521,20 +526,26 @@
         skip_scale[None],
         starts,
     ]
-    base, slope, joined = call(
+    base, slope, joined, lanes = call(
         functools.partial(ahead_kernel, head_size),
-        [shape((step, width), F32), shape((step, width), F32), shape((step, states), BF16)],
+        [
+            shape((step, width), F32),
+            shape((step, width), F32),
+            shape((step, states), BF16),
+            shape((16, width), F32),
+        ],
         [offset, y],
-        tokens,
+        [other] + tokens,
         2_000_000_000,
         16,
     )
-    send_a, send_b, ready = call(
-        functools.partial(far_kernel, head_size),
+    send_a, hidden, ready, squares = call(
+        far_kernel,
         [
-            shape((step + 8, edge), BF16),
-            shape((step, rest), BF16),
+            shape((step, edge), BF16),
+            shape((step, width), BF16),
             shape((2 * states, width), BF16),
+            shape((1, step), F32),
         ],
         [y, core],
         [
@@ -542,7 +553,7 @@
             incoming_other,
             other,
             first,
-            factor,
+            lanes,
             base,
             slope,
             joined,
@@ -555,12 +566,20 @@
     pair_1 = [(i, i ^ 1) for i in range(4)]
     pair_3 = [(i, i ^ 3) for i in range(4)]
     got_a = lax.ppermute(send_a, "head", pair_1)
+    send_b = call(
+        far_b_kernel,
+        shape((step + 8, rest), BF16),
+        [],
+        [hidden, out_proj, squares],
+        400_000_000,
+        12,
+    )
     got_b = lax.ppermute(send_b, "head", pair_3)
     send_a, send_b, hidden, via_squares = call(
         functools.partial(near_kernel, head_size),
         [
-            shape((step + 8, edge), BF16),
-            shape((step, rest), BF16),
+            shape((step, edge), BF16),
+            shape((step + 8, rest), BF16),
             shape((2 * step, width), BF16),
             shape((1, step), F32),
         ],
@@ -586,7 +605,7 @@
     )
     send_a, send_b = call(
         middle_kernel,
-        [shape((step + 8, edge), BF16), shape((step, rest), BF16)],
+        [shape((step, edge), BF16), shape((step + 8, rest), BF16)],
         [],
         [via_squares, via_a, via_b, got_a, got_b],
         1_000_000_000,

time: 77.6 us -> 76.2 us (0.982)
  local copies, waits for them, and re-layouts: 1.04 us -> 0.05 us
    unnamed x26 -> x18, local copies, waits for them, and re-layouts: 1.04 us -> 0.05 us
    ppermute x1, waiting for transfers between devices: 0.86 us -> 1.66 us  [local(): other = lax.ppermute(summary, 'seq_2', [(0, 1), (1, 0)])]
  transfers between devices with their start and end apart: 8 -> 8, of which waited for: 4 -> 4; matrix products, arithmetic and copies ran while one was open for 0% -> 0% of each run, Pallas kernels for 9% -> 10%
where the time goes in v5:
time: 76.2 us; the launch traced here: 74.8 us
  blocking collectives  37.8 us (50%)
  waiting for transfers between devices  15 us (20%)
  Pallas kernels  13.1 us (17%)
  starting transfers between devices  8.52 us (11%)
    all_to_all x1, blocking collectives, local(): pieces = lax.all_to_all(pieces, CHIPS, 0, 0, tiled=True)  23 us
    all_to_all x1, blocking collectives, local(): incoming = lax.all_to_all(prior, CHIPS, 0, 0, tiled=True)  14.8 us
    pallas_call x10, Pallas kernels, call(): pl.pallas_call(kernel, out_shape=out_shape, in_specs=[SMEM_SPEC] * len(sc...  13.1 us
    ppermute x1, waiting for transfers between devices, local(): near_b = lax.ppermute(send_b, 'head', pair_3)  12 us
    ppermute x1, starting transfers between devices, local(): got_b = lax.ppermute(send_b, 'head', pair_3)  2.49 us
    ppermute x1, waiting for transfers between devices, local(): other = lax.ppermute(summary, 'seq_2', [(0, 1), (1, 0)])  1.66 us
    ppermute x1, starting transfers between devices, local(): far_a = lax.ppermute(send_a, 'head', pair_3)  1.66 us
    ppermute x1, starting transfers between devices, local(): far_b = lax.ppermute(send_b, 'head', pair_1)  1.66 us
  transfers between devices with their start and end apart: 8, of which 4 were waited for; matrix products, arithmetic and copies ran while one was open for 0% of the time, Pallas kernels for 10%

profile of v5, /device:TPU:8, one launch (start us, length us, event | category | flops | bytes accessed | tf_op | source)
XLA Modules:
  0.0 74.8 jit_solution(17953805285919277646)
XLA Ops:
  0.0 2.6 %shard_map.109 = (bf16[128,1408]{1,0:T(8,128)(2,1)S(1)}, bf16[128,1280]{1,0:T(8,128)(2,1)S(1)}, bf16[64,640]{1,0:T(8,128)(2,1)S(1)}, bf16[64,640]{1,0:T(8,128)(2,1)S(1)}) custom-call(s32[1]{0:T(128)} %bitcast.offset_ref, s32[1]{0:T(128)} %bitcast.1.y_ref, s32[1]{0:T(128)} %bitcast.2.core_ref, bf16[512,1280]{1,0:T(8,128)(2,1)} %refs_0_.5, ...), custom_call_target="tpu_custom_call" | custom-call | flops 2000000000 | bytes 4000000 | tf_op jit(solution)/shard_map/pallas_call | solution.py:441
  2.6 0.1 collective-permute-start
  2.7 1.7 %collective-permute-done.other_ref = bf16[128,1408]{1,0:T(8,128)(2,1)S(1)} collective-permute-done((bf16[128,1408]{1,0:T(8,128)(2,1)S(1)}, bf16[128,1408]{1,0:T(8,128)(2,1)S(1)}, u32[]{:S(2)}, u32[]{:S(2)}) %collective-permute-start) | collective-permute-done | bytes 360480 | tf_op jit(solution)/shard_map/ppermute | solution.py:496
  4.4 0.3 shard_map.110
  4.6 23.0 %all_to_all.10.pieces_ref = bf16[32,4,768]{2,1,0:T(4,128)(2,1)S(1)} all-to-all(bf16[32,4,768]{2,1,0:T(4,128)(2,1)S(1)} %shard_map.110), channel_id=1, replica_groups=mesh['seq_0'=4,'seq_1'=8,'seq_2'=2,'head'=4] {'seq_0','seq_1'}, dimensions={0} | all-to-all | bytes 393216 | tf_op jit(solution)/shard_map/all_to_all | solution.py:505
  27.7 0.0 copy-start.5
  27.7 0.0 copy-start.6
  27.7 0.0 slice-start.1
  27.7 0.3 shard_map.111
  28.0 14.8 %all_to_all.11.before_ref = bf16[32,4,640]{2,1,0:T(4,128)(2,1)S(1)} all-to-all(bf16[32,4,640]{2,1,0:T(4,128)(2,1)S(1)} %shard_map.111), channel_id=1, replica_groups=mesh['seq_0'=4,'seq_1'=8,'seq_2'=2,'head'=4] {'seq_0','seq_1'}, dimensions={0} | all-to-all | bytes 327680 | tf_op jit(solution)/shard_map/all_to_all | solution.py:514
  42.8 0.0 collective-permute-start.1
  42.8 0.0 copy-start.4
  42.8 1.1 %shard_map.112 = (f32[128,1280]{1,0:T(8,128)S(1)}, f32[128,1280]{1,0:T(8,128)S(1)}, bf16[128,128]{1,0:T(8,128)(2,1)S(1)}, f32[16,1280]{1,0:T(8,128)S(1)}) custom-call(s32[1]{0:T(128)} %bitcast.offset_ref, s32[1]{0:T(128)} %bitcast.1.y_ref, bf16[128,1408]{1,0:T(8,128)(2,1)S(1)} %collective-permute-done.other_ref, bf16[512,1280]{1,0:T(8,128)(2,1)S(1)} %copy-done, ...), custom_call_target="tpu_custom_call" | custom-call | flops 2000000000 | bytes 4000000 | tf_op jit(solution)/shard_map/pallas_call | solution.py:441
  43.9 0.3 collective-permute-done.1.before_other_ref
  44.2 1.5 %shard_map.113 = (bf16[128,1536]{1,0:T(8,128)(2,1)S(1)}, bf16[128,1280]{1,0:T(8,128)(2,1)S(1)}, bf16[256,1280]{1,0:T(8,128)(2,1)S(1)}, f32[1,128]{1,0:T(1,128)S(1)}) custom-call(s32[1]{0:T(128)} %bitcast.1.y_ref, s32[1]{0:T(128)} %bitcast.2.core_ref, bf16[32,4,640]{2,1,0:T(4,128)(2,1)S(1)} %all_to_all.11.before_ref, ...), custom_call_target="tpu_custom_call" | custom-call | flops 1000000000 | bytes 4000000 | tf_op jit(solution)/shard_map/pallas_call | solution.py:441
  45.7 0.5 collective-permute-start.4
  46.2 0.5 shard_map.116
  46.7 2.5 %collective-permute-start.5 = (bf16[136,1024]{1,0:T(8,128)(2,1)S(1)}, bf16[136,1024]{1,0:T(8,128)(2,1)S(1)}, u32[]{:S(2)}, u32[]{:S(2)}) collective-permute-start(bf16[136,1024]{1,0:T(8,128)(2,1)S(1)} %shard_map.116), channel_id=1, source_target_pairs={{0,3},{1,2},{2,1},{3,0},{4,7},{5,6},{6,5},{7,4},{8,11},{9,10},{10,... | collective-permute-start | bytes 835592 | tf_op jit(solution)/shard_map/ppermute | solution.py:577
  49.2 3.0 %shard_map.114 = (bf16[128,1536]{1,0:T(8,128)(2,1)S(1)}, bf16[136,1024]{1,0:T(8,128)(2,1)S(1)}, bf16[256,1280]{1,0:T(8,128)(2,1)S(1)}, f32[1,128]{1,0:T(1,128)S(1)}) custom-call(s32[1]{0:T(128)} %bitcast.offset_ref, s32[1]{0:T(128)} %bitcast.1.y_ref, bf16[256,1280]{1,0:T(8,128)(2,1)S(1)} %get-tuple-element.35.states_ref, f32[1280]{0:T(1024)S(1)} %copy-done.4, ...), custom_call_target="tpu_custom_call" | custom-call | flops 2000000000 | bytes 4000000 | tf_op jit(solution)/shard_map/pallas_call | solution.py:441
  52.3 1.6 %collective-permute-start.2 = (bf16[128,1536]{1,0:T(8,128)(2,1)S(1)}, bf16[128,1536]{1,0:T(8,128)(2,1)S(1)}, u32[]{:S(2)}, u32[]{:S(2)}) collective-permute-start(bf16[128,1536]{1,0:T(8,128)(2,1)S(1)} %get-tuple-element.39), channel_id=1, source_target_pairs={{0,1},{1,0},{2,3},{3,2},{4,5},{5,4},{6,7},{7,6},{8,9},{9,8},{10,11... | collective-permute-start | bytes 1179656 | tf_op jit(solution)/shard_map/ppermute | solution.py:591
  53.9 2.8 %shard_map.115 = (f32[128,2560]{1,0:T(8,128)S(1)}, f32[128,1536]{1,0:T(8,128)S(1)}, f32[128,1024]{1,0:T(8,128)S(1)}, f32[1,128]{1,0:T(1,128)S(1)}) custom-call(s32[1]{0:T(128)} %bitcast.offset_ref, s32[1]{0:T(128)} %bitcast.1.y_ref, bf16[256,1280]{1,0:T(8,128)(2,1)S(1)} %get-tuple-element.35.states_ref, f32[1280]{0:T(1024)S(1)} %copy-done.4, ...), custom_call_target="tpu_custom_call" | custom-call | flops 2000000000 | bytes 4000000 | tf_op jit(solution)/shard_map/pallas_call | solution.py:441
  56.7 0.0 collective-permute-done.5.got_b_ref
  56.7 1.1 %collective-permute-done.4.got_a_ref = bf16[128,1536]{1,0:T(8,128)(2,1)S(1)} collective-permute-done((bf16[128,1536]{1,0:T(8,128)(2,1)S(1)}, bf16[128,1536]{1,0:T(8,128)(2,1)S(1)}, u32[]{:S(2)}, u32[]{:S(2)}) %collective-permute-start.4) | collective-permute-done | bytes 393248 | tf_op jit(solution)/shard_map/ppermute | solution.py:568
  57.7 0.2 shard_map.117
  57.9 1.7 %collective-permute-start.6 = (bf16[128,1536]{1,0:T(8,128)(2,1)S(1)}, bf16[128,1536]{1,0:T(8,128)(2,1)S(1)}, u32[]{:S(2)}, u32[]{:S(2)}) collective-permute-start(bf16[128,1536]{1,0:T(8,128)(2,1)S(1)} %get-tuple-element.47), channel_id=1, source_target_pairs={{0,3},{1,2},{2,1},{3,0},{4,7},{5,6},{6,5},{7,4},{8,11},{9,10},{10,... | collective-permute-start | bytes 1179656 | tf_op jit(solution)/shard_map/ppermute | solution.py:614
  59.6 0.5 collective-permute-start.3
  60.0 1.7 %collective-permute-start.7 = (bf16[136,1024]{1,0:T(8,128)(2,1)S(1)}, bf16[136,1024]{1,0:T(8,128)(2,1)S(1)}, u32[]{:S(2)}, u32[]{:S(2)}) collective-permute-start(bf16[136,1024]{1,0:T(8,128)(2,1)S(1)} %get-tuple-element.48), channel_id=1, source_target_pairs={{0,1},{1,0},{2,3},{3,2},{4,5},{5,4},{6,7},{7,6},{8,9},{9,8},{10,11... | collective-permute-start | bytes 835592 | tf_op jit(solution)/shard_map/ppermute | solution.py:615
  61.7 12.0 %collective-permute-done.3.near_b_ref = bf16[136,1024]{1,0:T(8,128)(2,1)S(1)} collective-permute-done((bf16[136,1024]{1,0:T(8,128)(2,1)S(1)}, bf16[136,1024]{1,0:T(8,128)(2,1)S(1)}, u32[]{:S(2)}, u32[]{:S(2)}) %collective-permute-start.3) | collective-permute-done | bytes 278560 | tf_op jit(solution)/shard_map/ppermute | solution.py:592
  73.7 0.0 collective-permute-done.2.near_a_ref
  73.7 0.0 collective-permute-done.7.far_b_ref
  73.7 0.0 collective-permute-done.6.far_a_ref
  73.7 1.0 %shard_map.118 = bf16[128,2560]{1,0:T(8,128)(2,1)} custom-call(f32[1,128]{1,0:T(1,128)S(1)} %get-tuple-element.37.squares_ref, f32[128,2560]{1,0:T(8,128)S(1)} %get-tuple-element.38.own_ref, bf16[128,1536]{1,0:T(8,128)(2,1)S(1)} %collective-permute-done.2.near_a_ref, bf16[136,1024]{1,0:T(8,128)(2,1)S(1)} %collective-permute-done.3.near_b_ref, ...), custom_call_target="tpu_custom_call" | custom-call | flops 1000000000 | bytes 4000000 | tf_op jit(solution)/shard_map/pallas_call | solution.py:441
  (15 shorter events, 0.0 us)
Async XLA Ops:
  2.6 1.8 %collective-permute-start = (bf16[128,1408]{1,0:T(8,128)(2,1)S(1)}, bf16[128,1408]{1,0:T(8,128)(2,1)S(1)}, u32[]{:S(2)}, u32[]{:S(2)}) collective-permute-start(bf16[128,1408]{1,0:T(8,128)(2,1)S(1)} %get-tuple-element.27.own_ref), channel_id=1, source_target_pairs={{0,4},{4,0},{1,5},{5,1},{2,6},{6,2},{3,7},{7,3},{8,12},{12,8},{9,1... | collective-permute-start | bytes 1081352 | tf_op jit(solution)/shard_map/ppermute | solution.py:496
  4.4 39.8 %slice-start = ((s8[6553600]{0:T(1024)(128)(4,1)}), s8[4194304]{0:T(1024)(128)(4,1)S(1)}, s32[]{:S(2)}) async-start(s8[6553600]{0:T(1024)(128)(4,1)} %bitcast.7), calls=%async_computation.2 | async-start | bytes 8388608
  27.7 15.1 %copy-start = (bf16[512,1280]{1,0:T(8,128)(2,1)S(1)}, bf16[512,1280]{1,0:T(8,128)(2,1)}, u32[]{:S(2)}) copy-start(bf16[512,1280]{1,0:T(8,128)(2,1)} %refs_0_.5) | copy-start | bytes 3932164
  27.7 15.1 %copy-start.1 = (bf16[512,1280]{1,0:T(8,128)(2,1)S(1)}, bf16[512,1280]{1,0:T(8,128)(2,1)}, u32[]{:S(2)}) copy-start(bf16[512,1280]{1,0:T(8,128)(2,1)} %refs_1_.5) | copy-start | bytes 3932164
  27.7 15.1 %copy-start.2 = (bf16[512,128]{1,0:T(8,128)(2,1)S(1)}, bf16[512,128]{1,0:T(8,128)(2,1)}, u32[]{:S(2)}) copy-start(bf16[512,128]{1,0:T(8,128)(2,1)} %refs_2_.5) | copy-start | bytes 393220
  27.7 15.1 %copy-start.3 = (bf16[512,128]{1,0:T(8,128)(2,1)S(1)}, bf16[512,128]{1,0:T(8,128)(2,1)}, u32[]{:S(2)}) copy-start(bf16[512,128]{1,0:T(8,128)(2,1)} %refs_3_.5) | copy-start | bytes 393220
  27.7 15.1 %copy-start.5 = (s32[128]{0:T(128)S(1)}, s32[128]{0:T(128)}, u32[]{:S(2)}) copy-start(s32[128]{0:T(128)} %param.21) | copy-start | bytes 1540
  27.7 15.1 %copy-start.6 = (f32[20]{0:T(128)S(1)}, f32[20]{0:T(128)}, u32[]{:S(2)}) copy-start(f32[20]{0:T(128)} %param.18) | copy-start | bytes 244
  27.7 16.5 %slice-start.1 = ((s8[6553600]{0:T(1024)(128)(4,1)}), s8[2359296]{0:T(1024)(128)(4,1)S(1)}, s32[]{:S(2)}) async-start(s8[6553600]{0:T(1024)(128)(4,1)} %bitcast.7), calls=%async_computation.3 | async-start | bytes 4718592
  42.8 1.4 %collective-permute-start.1 = (bf16[32,4,640]{2,1,0:T(4,128)(2,1)S(1)}, bf16[32,4,640]{2,1,0:T(4,128)(2,1)S(1)}, u32[]{:S(2)}, u32[]{:S(2)}) collective-permute-start(bf16[32,4,640]{2,1,0:T(4,128)(2,1)S(1)} %all_to_all.11.before_ref), channel_id=1, source_target_pairs={{0,4},{4,0},{1,5},{5,1},{2,6},{6,2},{3,7},{7,3},{8,12},{12,8},{9,1... | collective-permute-start | bytes 491528 | tf_op jit(solution)/shard_map/ppermute | solution.py:515
  42.8 1.4 %copy-start.4 = (f32[1280]{0:T(1024)S(1)}, f32[1280]{0:T(1024)}, u32[]{:S(2)}) copy-start(f32[1280]{0:T(1024)} %gain_ref.5) | copy-start | bytes 15364
  45.7 12.1 %collective-permute-start.4 = (bf16[128,1536]{1,0:T(8,128)(2,1)S(1)}, bf16[128,1536]{1,0:T(8,128)(2,1)S(1)}, u32[]{:S(2)}, u32[]{:S(2)}) collective-permute-start(bf16[128,1536]{1,0:T(8,128)(2,1)S(1)} %get-tuple-element.44), channel_id=1, source_target_pairs={{0,1},{1,0},{2,3},{3,2},{4,5},{5,4},{6,7},{7,6},{8,9},{9,8},{10,11... | collective-permute-start | bytes 1179656 | tf_op jit(solution)/shard_map/ppermute | solution.py:568
  46.7 9.9 %collective-permute-start.5 = (bf16[136,1024]{1,0:T(8,128)(2,1)S(1)}, bf16[136,1024]{1,0:T(8,128)(2,1)S(1)}, u32[]{:S(2)}, u32[]{:S(2)}) collective-permute-start(bf16[136,1024]{1,0:T(8,128)(2,1)S(1)} %shard_map.116), channel_id=1, source_target_pairs={{0,3},{1,2},{2,1},{3,0},{4,7},{5,6},{6,5},{7,4},{8,11},{9,10},{10,... | collective-permute-start | bytes 835592 | tf_op jit(solution)/shard_map/ppermute | solution.py:577
  52.3 21.4 %collective-permute-start.2 = (bf16[128,1536]{1,0:T(8,128)(2,1)S(1)}, bf16[128,1536]{1,0:T(8,128)(2,1)S(1)}, u32[]{:S(2)}, u32[]{:S(2)}) collective-permute-start(bf16[128,1536]{1,0:T(8,128)(2,1)S(1)} %get-tuple-element.39), channel_id=1, source_target_pairs={{0,1},{1,0},{2,3},{3,2},{4,5},{5,4},{6,7},{7,6},{8,9},{9,8},{10,11... | collective-permute-start | bytes 1179656 | tf_op jit(solution)/shard_map/ppermute | solution.py:591
  57.9 15.8 %collective-permute-start.6 = (bf16[128,1536]{1,0:T(8,128)(2,1)S(1)}, bf16[128,1536]{1,0:T(8,128)(2,1)S(1)}, u32[]{:S(2)}, u32[]{:S(2)}) collective-permute-start(bf16[128,1536]{1,0:T(8,128)(2,1)S(1)} %get-tuple-element.47), channel_id=1, source_target_pairs={{0,3},{1,2},{2,1},{3,0},{4,7},{5,6},{6,5},{7,4},{8,11},{9,10},{10,... | collective-permute-start | bytes 1179656 | tf_op jit(solution)/shard_map/ppermute | solution.py:614
  59.6 14.1 %collective-permute-start.3 = (bf16[136,1024]{1,0:T(8,128)(2,1)S(1)}, bf16[136,1024]{1,0:T(8,128)(2,1)S(1)}, u32[]{:S(2)}, u32[]{:S(2)}) collective-permute-start(bf16[136,1024]{1,0:T(8,128)(2,1)S(1)} %get-tuple-element.40), channel_id=1, source_target_pairs={{0,3},{1,2},{2,1},{3,0},{4,7},{5,6},{6,5},{7,4},{8,11},{9,10},{10,... | collective-permute-start | bytes 835592 | tf_op jit(solution)/shard_map/ppermute | solution.py:592
  60.0 13.6 %collective-permute-start.7 = (bf16[136,1024]{1,0:T(8,128)(2,1)S(1)}, bf16[136,1024]{1,0:T(8,128)(2,1)S(1)}, u32[]{:S(2)}, u32[]{:S(2)}) collective-permute-start(bf16[136,1024]{1,0:T(8,128)(2,1)S(1)} %get-tuple-element.48), channel_id=1, source_target_pairs={{0,1},{1,0},{2,3},{3,2},{4,5},{5,4},{6,7},{7,6},{8,9},{9,8},{10,11... | collective-permute-start | bytes 835592 | tf_op jit(solution)/shard_map/ppermute | solution.py:615

commit v6 on v4

--- a/solution.py
+++ b/solution.py
@@ -17,7 +17,6 @@
 BF16 = jnp.bfloat16
 PAD = 32
 LANES = 128
-FULL = 67_043_328 / 1024**2
 
 VMEM_SPEC = pl.BlockSpec(memory_space=pltpu.VMEM)
 SMEM_SPEC = pl.BlockSpec(memory_space=pltpu.SMEM)
@@ -114,10 +113,14 @@
     ]
     for copy in copies:
         copy.start()
+    heads, rows = step_ref.shape
+    width = stream_ref.shape[1]
+    spread = head_lanes(width, head_size)
+    i = lax.broadcasted_iota(jnp.int32, (BLOCK, BLOCK), 0)
+    j = lax.broadcasted_iota(jnp.int32, (BLOCK, BLOCK), 1)
+    upper = jnp.where(i <= j, 1.0, 0.0)
     for copy in copies[:4]:
         copy.wait()
-    heads, rows = step_ref.shape
-    width = stream_ref.shape[1]
     offset = offset_ref[0]
     starts = starts_ref[...]
     docs = docs_column(starts, offset, rows)
@@ -125,9 +128,6 @@
     raw = step_ref[...] + as_column(bias_ref[...], heads)
     step = jnp.maximum(raw, 0.0) + jnp.log1p(jnp.exp(-jnp.abs(raw)))
     log_decay = -step * as_column(rate_ref[...], heads)
-    i = lax.broadcasted_iota(jnp.int32, (BLOCK, BLOCK), 0)
-    j = lax.broadcasted_iota(jnp.int32, (BLOCK, BLOCK), 1)
-    upper = jnp.where(i <= j, 1.0, 0.0)
     into, out_of, half, last = [], [], [], []
     for block in range(rows // BLOCK):
         cut = slice(block * BLOCK, (block + 1) * BLOCK)
@@ -152,14 +152,13 @@
     constants = jnp.where(lane == 2, gate_0, constants)
     constants = jnp.where(lane == 3, gate_1, constants)
     nothing = jnp.zeros((PAD - heads, rows + LANES), F32)
-    spread = head_lanes(width, head_size)
     wide_in = jnp.concatenate([jnp.concatenate(into + [constants], axis=1), nothing], axis=0)
     wide_out = jnp.concatenate([jnp.concatenate(out_of + [constants], axis=1), nothing], axis=0)
     factor_ref[...] = two_parts(wide_out)
     into_parts = two_parts(wide_in)
     into_ref[...] = into_parts
-    per_lane = dot_first(into_parts, spread)
-    constant_rows = per_lane[rows : rows + 8, :]
+    per_lane = dot_first(into_parts[:, :rows], spread)
+    constant_rows = dot_first(into_parts[:, rows : rows + 8], spread)
     for copy in copies[4:]:
         copy.wait()
     states = []
@@ -237,10 +236,6 @@
     base_ref[...], slope_ref[...], joined_ref[...] = block_terms(
         head_size, offset_ref[0], y_ref[0] ^ 2, *refs[:-3]
     )
-
-
-def pass_kernel(from_ref, to_ref):
-    to_ref[...] = from_ref[...]
 
 
 def link_lanes(links, width, head_size):
@@ -471,7 +466,10 @@
     offset = (lax.axis_index(SEQ) * rows).astype(jnp.int32)[None]
     starts = doc_starts[None, :]
     shape = jax.ShapeDtypeStruct
-    arrays = [stream, in_coeff, step_raw, step_bias[None], decay_rate[None], starts]
+    arrays = [
+        pltpu.with_memory_space_constraint(a, pltpu.HBM)
+        for a in (stream, in_coeff, step_raw, step_bias[None], decay_rate[None], starts)
+    ]
     summary, first, into, factor = call(
         functools.partial(state_kernel, head_size),
         [
@@ -483,17 +481,16 @@
         [offset, y, core],
         arrays,
         2_000_000_000,
-        FULL,
+        24,
         [pltpu.VMEM(a.shape, a.dtype) for a in arrays] + [pltpu.SemaphoreType.DMA((len(arrays),))],
         HBM_SPEC,
     )
     other = lax.ppermute(summary, "seq_2", [(0, 1), (1, 0)])
-    own = call(pass_kernel, shape(summary.shape, BF16), [], [summary], 100_000_000, 4)
     pieces = call(
         functools.partial(combine_kernel, head_size),
         shape((chips, states // chips, width // 2 + LANES), BF16),
         [core],
-        [own, other],
+        [summary, other],
         200_000_000,
         8,
     )

time: 77.6 us -> 76.4 us (0.985)
  local copies, waits for them, and re-layouts: 1.04 us -> 0.05 us
    unnamed x26 -> x18, local copies, waits for them, and re-layouts: 1.04 us -> 0.05 us
    ppermute x1, waiting for transfers between devices: 0.86 us -> 1.66 us  [local(): other = lax.ppermute(summary, 'seq_2', [(0, 1), (1, 0)])]
    pallas_call x10 -> x9, Pallas kernels: 13.8 us -> 13.3 us  [call(): pl.pallas_call(kernel, out_shape=out_shape, in_specs=[SMEM_SPEC] * len(sc...]
  transfers between devices with their start and end apart: 8 -> 8, of which waited for: 4 -> 4; matrix products, arithmetic and copies ran while one was open for 0% -> 0% of each run, Pallas kernels for 9% -> 10%
where the time goes in v6:
time: 76.4 us; the launch traced here: 75.1 us
  blocking collectives  37.8 us (49%)
  waiting for transfers between devices  15.2 us (20%)
  Pallas kernels  13.3 us (17%)
  starting transfers between devices  8.43 us (11%)
    all_to_all x1, blocking collectives, local(): pieces = lax.all_to_all(pieces, CHIPS, 0, 0, tiled=True)  23 us
    all_to_all x1, blocking collectives, local(): incoming = lax.all_to_all(prior, CHIPS, 0, 0, tiled=True)  14.8 us
    pallas_call x9, Pallas kernels, call(): pl.pallas_call(kernel, out_shape=out_shape, in_specs=[SMEM_SPEC] * len(sc...  13.3 us
    ppermute x1, waiting for transfers between devices, local(): near_b = lax.ppermute(send_b, 'head', pair_3)  12 us
    ppermute x1, starting transfers between devices, local(): got_b = lax.ppermute(send_b, 'head', pair_3)  2.41 us
    ppermute x1, starting transfers between devices, local(): far_a = lax.ppermute(send_a, 'head', pair_3)  1.66 us
    ppermute x1, waiting for transfers between devices, local(): other = lax.ppermute(summary, 'seq_2', [(0, 1), (1, 0)])  1.66 us
    ppermute x1, starting transfers between devices, local(): far_b = lax.ppermute(send_b, 'head', pair_1)  1.66 us
  transfers between devices with their start and end apart: 8, of which 4 were waited for; matrix products, arithmetic and copies ran while one was open for 0% of the time, Pallas kernels for 10%

profile of v6, /device:TPU:8, one launch (start us, length us, event | category | flops | bytes accessed | tf_op | source)
XLA Modules:
  0.0 75.1 jit_solution(11613736693767465221)
XLA Ops:
  0.0 2.4 %shard_map.109 = (bf16[128,1408]{1,0:T(8,128)(2,1)S(1)}, bf16[128,1280]{1,0:T(8,128)(2,1)S(1)}, bf16[64,640]{1,0:T(8,128)(2,1)S(1)}, bf16[64,640]{1,0:T(8,128)(2,1)S(1)}) custom-call(s32[1]{0:T(128)} %bitcast.offset_ref, s32[1]{0:T(128)} %bitcast.1.y_ref, s32[1]{0:T(128)} %bitcast.2.core_ref, bf16[512,1280]{1,0:T(8,128)(2,1)} %refs_0_.5, ...), custom_call_target="tpu_custom_call" | custom-call | flops 2000000000 | bytes 4000000 | tf_op jit(solution)/shard_map/pallas_call | solution.py:433
  2.5 0.1 collective-permute-start
  2.6 1.7 %collective-permute-done.other_ref = bf16[128,1408]{1,0:T(8,128)(2,1)S(1)} collective-permute-done((bf16[128,1408]{1,0:T(8,128)(2,1)S(1)}, bf16[128,1408]{1,0:T(8,128)(2,1)S(1)}, u32[]{:S(2)}, u32[]{:S(2)}) %collective-permute-start) | collective-permute-done | bytes 360480 | tf_op jit(solution)/shard_map/ppermute | solution.py:488
  4.2 0.3 shard_map.110
  4.5 23.0 %all_to_all.10.pieces_ref = bf16[32,4,768]{2,1,0:T(4,128)(2,1)S(1)} all-to-all(bf16[32,4,768]{2,1,0:T(4,128)(2,1)S(1)} %shard_map.110), channel_id=1, replica_groups=mesh['seq_0'=4,'seq_1'=8,'seq_2'=2,'head'=4] {'seq_0','seq_1'}, dimensions={0} | all-to-all | bytes 393216 | tf_op jit(solution)/shard_map/all_to_all | solution.py:497
  27.5 0.0 copy-start.5
  27.6 0.0 copy-start.6
  27.6 0.0 slice-start.1
  27.6 0.3 shard_map.111
  27.8 14.8 %all_to_all.11.before_ref = bf16[32,4,640]{2,1,0:T(4,128)(2,1)S(1)} all-to-all(bf16[32,4,640]{2,1,0:T(4,128)(2,1)S(1)} %shard_map.111), channel_id=1, replica_groups=mesh['seq_0'=4,'seq_1'=8,'seq_2'=2,'head'=4] {'seq_0','seq_1'}, dimensions={0} | all-to-all | bytes 327680 | tf_op jit(solution)/shard_map/all_to_all | solution.py:506
  42.6 0.0 collective-permute-start.1
  42.6 0.0 copy-done.1
  42.7 0.0 copy-start.4
  42.7 1.0 %shard_map.112 = (f32[128,1280]{1,0:T(8,128)S(1)}, f32[128,1280]{1,0:T(8,128)S(1)}, bf16[128,128]{1,0:T(8,128)(2,1)S(1)}) custom-call(s32[1]{0:T(128)} %bitcast.offset_ref, s32[1]{0:T(128)} %bitcast.1.y_ref, bf16[512,1280]{1,0:T(8,128)(2,1)S(1)} %copy-done, bf16[512,1280]{1,0:T(8,128)(2,1)S(1)} %copy-done.1, bf16[512,128]{1,0:T(8,128)(2,1)S(1)} %copy-done.2, ...), custom_call_target="tpu_custom_call" | custom-call | flops 2000000000 | bytes 4000000 | tf_op jit(solution)/shard_map/pallas_call | solution.py:433
  43.7 0.3 collective-permute-done.1.before_other_ref
  44.0 2.1 %shard_map.113 = (bf16[136,1408]{1,0:T(8,128)(2,1)S(1)}, bf16[128,1152]{1,0:T(8,128)(2,1)S(1)}, bf16[256,1280]{1,0:T(8,128)(2,1)S(1)}) custom-call(s32[1]{0:T(128)} %bitcast.1.y_ref, s32[1]{0:T(128)} %bitcast.2.core_ref, bf16[32,4,640]{2,1,0:T(4,128)(2,1)S(1)} %all_to_all.11.before_ref, bf16[32,4,640]{2,1,0:T(4,128)(2,1)S(1)} %collective-permute-done.1.before_other_ref, ...), custom_call_target="tpu_custom_call" | custom-call | flops 1000000000 | bytes 4000000 | tf_op jit(solution)/shard_map/pallas_call | solution.py:433
  46.2 0.5 collective-permute-start.4
  46.7 2.4 %collective-permute-start.5 = (bf16[128,1152]{1,0:T(8,128)(2,1)S(1)}, bf16[128,1152]{1,0:T(8,128)(2,1)S(1)}, u32[]{:S(2)}, u32[]{:S(2)}) collective-permute-start(bf16[128,1152]{1,0:T(8,128)(2,1)S(1)} %get-tuple-element.42), channel_id=1, source_target_pairs={{0,3},{1,2},{2,1},{3,0},{4,7},{5,6},{6,5},{7,4},{8,11},{9,10},{10,... | collective-permute-start | bytes 884744 | tf_op jit(solution)/shard_map/ppermute | solution.py:555
  49.1 3.1 %shard_map.114 = (bf16[136,1408]{1,0:T(8,128)(2,1)S(1)}, bf16[128,1152]{1,0:T(8,128)(2,1)S(1)}, bf16[256,1280]{1,0:T(8,128)(2,1)S(1)}, f32[1,128]{1,0:T(1,128)S(1)}) custom-call(s32[1]{0:T(128)} %bitcast.offset_ref, s32[1]{0:T(128)} %bitcast.1.y_ref, bf16[256,1280]{1,0:T(8,128)(2,1)S(1)} %get-tuple-element.32.states_ref, f32[1280]{0:T(1024)S(1)} %copy-done.4, ...), custom_call_target="tpu_custom_call" | custom-call | flops 2000000000 | bytes 4000000 | tf_op jit(solution)/shard_map/pallas_call | solution.py:433
  52.3 1.6 %collective-permute-start.2 = (bf16[136,1408]{1,0:T(8,128)(2,1)S(1)}, bf16[136,1408]{1,0:T(8,128)(2,1)S(1)}, u32[]{:S(2)}, u32[]{:S(2)}) collective-permute-start(bf16[136,1408]{1,0:T(8,128)(2,1)S(1)} %get-tuple-element.36), channel_id=1, source_target_pairs={{0,1},{1,0},{2,3},{3,2},{4,5},{5,4},{6,7},{7,6},{8,9},{9,8},{10,11... | collective-permute-start | bytes 1148936 | tf_op jit(solution)/shard_map/ppermute | solution.py:569
  53.9 2.9 %shard_map.115 = (f32[128,2560]{1,0:T(8,128)S(1)}, f32[128,1408]{1,0:T(8,128)S(1)}, f32[128,1152]{1,0:T(8,128)S(1)}, f32[1,128]{1,0:T(1,128)S(1)}) custom-call(s32[1]{0:T(128)} %bitcast.offset_ref, s32[1]{0:T(128)} %bitcast.1.y_ref, bf16[256,1280]{1,0:T(8,128)(2,1)S(1)} %get-tuple-element.32.states_ref, f32[1280]{0:T(1024)S(1)} %copy-done.4, ...), custom_call_target="tpu_custom_call" | custom-call | flops 2000000000 | bytes 4000000 | tf_op jit(solution)/shard_map/pallas_call | solution.py:433
  56.8 0.0 collective-permute-done.5.got_b_ref
  56.8 1.2 %collective-permute-done.4.got_a_ref = bf16[136,1408]{1,0:T(8,128)(2,1)S(1)} collective-permute-done((bf16[136,1408]{1,0:T(8,128)(2,1)S(1)}, bf16[136,1408]{1,0:T(8,128)(2,1)S(1)}, u32[]{:S(2)}, u32[]{:S(2)}) %collective-permute-start.4) | collective-permute-done | bytes 383008 | tf_op jit(solution)/shard_map/ppermute | solution.py:554
  58.0 0.1 shard_map.116
  58.2 1.7 %collective-permute-start.6 = (bf16[136,1408]{1,0:T(8,128)(2,1)S(1)}, bf16[136,1408]{1,0:T(8,128)(2,1)S(1)}, u32[]{:S(2)}, u32[]{:S(2)}) collective-permute-start(bf16[136,1408]{1,0:T(8,128)(2,1)S(1)} %get-tuple-element.43), channel_id=1, source_target_pairs={{0,3},{1,2},{2,1},{3,0},{4,7},{5,6},{6,5},{7,4},{8,11},{9,10},{10,... | collective-permute-start | bytes 1148936 | tf_op jit(solution)/shard_map/ppermute | solution.py:592
  59.8 0.4 collective-permute-start.3
  60.3 1.7 %collective-permute-start.7 = (bf16[128,1152]{1,0:T(8,128)(2,1)S(1)}, bf16[128,1152]{1,0:T(8,128)(2,1)S(1)}, u32[]{:S(2)}, u32[]{:S(2)}) collective-permute-start(bf16[128,1152]{1,0:T(8,128)(2,1)S(1)} %get-tuple-element.44), channel_id=1, source_target_pairs={{0,1},{1,0},{2,3},{3,2},{4,5},{5,4},{6,7},{7,6},{8,9},{9,8},{10,11... | collective-permute-start | bytes 884744 | tf_op jit(solution)/shard_map/ppermute | solution.py:593
  62.0 12.0 %collective-permute-done.3.near_b_ref = bf16[128,1152]{1,0:T(8,128)(2,1)S(1)} collective-permute-done((bf16[128,1152]{1,0:T(8,128)(2,1)S(1)}, bf16[128,1152]{1,0:T(8,128)(2,1)S(1)}, u32[]{:S(2)}, u32[]{:S(2)}) %collective-permute-start.3) | collective-permute-done | bytes 294944 | tf_op jit(solution)/shard_map/ppermute | solution.py:570
  73.9 0.0 collective-permute-done.2.near_a_ref
  73.9 0.0 collective-permute-done.7.far_b_ref
  73.9 0.0 collective-permute-done.6.far_a_ref
  73.9 1.0 %shard_map.117 = bf16[128,2560]{1,0:T(8,128)(2,1)} custom-call(f32[1,128]{1,0:T(1,128)S(1)} %get-tuple-element.34.squares_ref, f32[128,2560]{1,0:T(8,128)S(1)} %get-tuple-element.35.own_ref, bf16[136,1408]{1,0:T(8,128)(2,1)S(1)} %collective-permute-done.2.near_a_ref, bf16[128,1152]{1,0:T(8,128)(2,1)S(1)} %collective-permute-done.3.near_b_ref, ...), custom_call_target="tpu_custom_call" | custom-call | flops 1000000000 | bytes 4000000 | tf_op jit(solution)/shard_map/pallas_call | solution.py:433
  (14 shorter events, 0.0 us)
Async XLA Ops:
  2.5 1.8 %collective-permute-start = (bf16[128,1408]{1,0:T(8,128)(2,1)S(1)}, bf16[128,1408]{1,0:T(8,128)(2,1)S(1)}, u32[]{:S(2)}, u32[]{:S(2)}) collective-permute-start(bf16[128,1408]{1,0:T(8,128)(2,1)S(1)} %get-tuple-element.25.own_ref), channel_id=1, source_target_pairs={{0,4},{4,0},{1,5},{5,1},{2,6},{6,2},{3,7},{7,3},{8,12},{12,8},{9,1... | collective-permute-start | bytes 1081352 | tf_op jit(solution)/shard_map/ppermute | solution.py:488
  4.2 39.8 %slice-start = ((s8[6553600]{0:T(1024)(128)(4,1)}), s8[4194304]{0:T(1024)(128)(4,1)S(1)}, s32[]{:S(2)}) async-start(s8[6553600]{0:T(1024)(128)(4,1)} %bitcast.7), calls=%async_computation.2 | async-start | bytes 8388608
  27.5 15.1 %copy-start = (bf16[512,1280]{1,0:T(8,128)(2,1)S(1)}, bf16[512,1280]{1,0:T(8,128)(2,1)}, u32[]{:S(2)}) copy-start(bf16[512,1280]{1,0:T(8,128)(2,1)} %refs_0_.5) | copy-start | bytes 3932164
  27.5 15.1 %copy-start.1 = (bf16[512,1280]{1,0:T(8,128)(2,1)S(1)}, bf16[512,1280]{1,0:T(8,128)(2,1)}, u32[]{:S(2)}) copy-start(bf16[512,1280]{1,0:T(8,128)(2,1)} %refs_1_.5) | copy-start | bytes 3932164
  27.5 15.1 %copy-start.2 = (bf16[512,128]{1,0:T(8,128)(2,1)S(1)}, bf16[512,128]{1,0:T(8,128)(2,1)}, u32[]{:S(2)}) copy-start(bf16[512,128]{1,0:T(8,128)(2,1)} %refs_2_.5) | copy-start | bytes 393220
  27.5 15.1 %copy-start.3 = (bf16[512,128]{1,0:T(8,128)(2,1)S(1)}, bf16[512,128]{1,0:T(8,128)(2,1)}, u32[]{:S(2)}) copy-start(bf16[512,128]{1,0:T(8,128)(2,1)} %refs_3_.5) | copy-start | bytes 393220
  27.5 15.1 %copy-start.5 = (s32[128]{0:T(128)S(1)}, s32[128]{0:T(128)}, u32[]{:S(2)}) copy-start(s32[128]{0:T(128)} %param.21) | copy-start | bytes 1540
  27.6 15.1 %copy-start.6 = (f32[20]{0:T(128)S(1)}, f32[20]{0:T(128)}, u32[]{:S(2)}) copy-start(f32[20]{0:T(128)} %param.18) | copy-start | bytes 244
  27.6 16.5 %slice-start.1 = ((s8[6553600]{0:T(1024)(128)(4,1)}), s8[2359296]{0:T(1024)(128)(4,1)S(1)}, s32[]{:S(2)}) async-start(s8[6553600]{0:T(1024)(128)(4,1)} %bitcast.7), calls=%async_computation.3 | async-start | bytes 4718592
  42.6 1.4 %collective-permute-start.1 = (bf16[32,4,640]{2,1,0:T(4,128)(2,1)S(1)}, bf16[32,4,640]{2,1,0:T(4,128)(2,1)S(1)}, u32[]{:S(2)}, u32[]{:S(2)}) collective-permute-start(bf16[32,4,640]{2,1,0:T(4,128)(2,1)S(1)} %all_to_all.11.before_ref), channel_id=1, source_target_pairs={{0,4},{4,0},{1,5},{5,1},{2,6},{6,2},{3,7},{7,3},{8,12},{12,8},{9,1... | collective-permute-start | bytes 491528 | tf_op jit(solution)/shard_map/ppermute | solution.py:507
  42.7 1.4 %copy-start.4 = (f32[1280]{0:T(1024)S(1)}, f32[1280]{0:T(1024)}, u32[]{:S(2)}) copy-start(f32[1280]{0:T(1024)} %gain_ref.5) | copy-start | bytes 15364
  46.2 11.9 %collective-permute-start.4 = (bf16[136,1408]{1,0:T(8,128)(2,1)S(1)}, bf16[136,1408]{1,0:T(8,128)(2,1)S(1)}, u32[]{:S(2)}, u32[]{:S(2)}) collective-permute-start(bf16[136,1408]{1,0:T(8,128)(2,1)S(1)} %get-tuple-element.41), channel_id=1, source_target_pairs={{0,1},{1,0},{2,3},{3,2},{4,5},{5,4},{6,7},{7,6},{8,9},{9,8},{10,11... | collective-permute-start | bytes 1148936 | tf_op jit(solution)/shard_map/ppermute | solution.py:554
  46.7 10.1 %collective-permute-start.5 = (bf16[128,1152]{1,0:T(8,128)(2,1)S(1)}, bf16[128,1152]{1,0:T(8,128)(2,1)S(1)}, u32[]{:S(2)}, u32[]{:S(2)}) collective-permute-start(bf16[128,1152]{1,0:T(8,128)(2,1)S(1)} %get-tuple-element.42), channel_id=1, source_target_pairs={{0,3},{1,2},{2,1},{3,0},{4,7},{5,6},{6,5},{7,4},{8,11},{9,10},{10,... | collective-permute-start | bytes 884744 | tf_op jit(solution)/shard_map/ppermute | solution.py:555
  52.3 21.7 %collective-permute-start.2 = (bf16[136,1408]{1,0:T(8,128)(2,1)S(1)}, bf16[136,1408]{1,0:T(8,128)(2,1)S(1)}, u32[]{:S(2)}, u32[]{:S(2)}) collective-permute-start(bf16[136,1408]{1,0:T(8,128)(2,1)S(1)} %get-tuple-element.36), channel_id=1, source_target_pairs={{0,1},{1,0},{2,3},{3,2},{4,5},{5,4},{6,7},{7,6},{8,9},{9,8},{10,11... | collective-permute-start | bytes 1148936 | tf_op jit(solution)/shard_map/ppermute | solution.py:569
  58.2 15.8 %collective-permute-start.6 = (bf16[136,1408]{1,0:T(8,128)(2,1)S(1)}, bf16[136,1408]{1,0:T(8,128)(2,1)S(1)}, u32[]{:S(2)}, u32[]{:S(2)}) collective-permute-start(bf16[136,1408]{1,0:T(8,128)(2,1)S(1)} %get-tuple-element.43), channel_id=1, source_target_pairs={{0,3},{1,2},{2,1},{3,0},{4,7},{5,6},{6,5},{7,4},{8,11},{9,10},{10,... | collective-permute-start | bytes 1148936 | tf_op jit(solution)/shard_map/ppermute | solution.py:592
  59.8 14.1 %collective-permute-start.3 = (bf16[128,1152]{1,0:T(8,128)(2,1)S(1)}, bf16[128,1152]{1,0:T(8,128)(2,1)S(1)}, u32[]{:S(2)}, u32[]{:S(2)}) collective-permute-start(bf16[128,1152]{1,0:T(8,128)(2,1)S(1)} %get-tuple-element.37), channel_id=1, source_target_pairs={{0,3},{1,2},{2,1},{3,0},{4,7},{5,6},{6,5},{7,4},{8,11},{9,10},{10,... | collective-permute-start | bytes 884744 | tf_op jit(solution)/shard_map/ppermute | solution.py:570
  60.3 13.7 %collective-permute-start.7 = (bf16[128,1152]{1,0:T(8,128)(2,1)S(1)}, bf16[128,1152]{1,0:T(8,128)(2,1)S(1)}, u32[]{:S(2)}, u32[]{:S(2)}) collective-permute-start(bf16[128,1152]{1,0:T(8,128)(2,1)S(1)} %get-tuple-element.44), channel_id=1, source_target_pairs={{0,1},{1,0},{2,3},{3,2},{4,5},{5,4},{6,7},{7,6},{8,9},{9,8},{10,11... | collective-permute-start | bytes 884744 | tf_op jit(solution)/shard_map/ppermute | solution.py:593
